TPU v7x, 32 devices: a whole 2x2x4 slice. The times are simulated.
32 devices in a mesh: gx: 8 (over z, x), gy: 4 (over y, core).
Axes of the slice: x: 2, y: 2, z: 4, core: 2. Of those that a mesh axis runs over, the one named last changes fastest.
Arguments:
- populations: float32 [19, 48, 32, 128], P(None, 'gx', 'gy'), may hold values from 0.03 to 0.06
- cell_mass: float32 [48, 32, 128], P('gx', 'gy'), may hold values from 0.05 to 1
- cell_flags: int32 [48, 32, 128], P('gx', 'gy'), may hold values from 0 to 2
- bubble: int32 [48, 32, 128], P('gx', 'gy'), may hold values from 0 to 95, as said below
- conversion: int32 [48, 32, 128], P('gx', 'gy'), may hold values 0 or 1
- rest_volume: float32 [96], replicated, may hold values from 256 to 2048
Outputs:
- relaxed_populations: float32 [19, 48, 32, 128], P(None, 'gx', 'gy')
- new_mass: float32 [48, 32, 128], P('gx', 'gy')
- gas_density: float32 [96], replicated
Inputs may be any that keep to these rules, and one draw needn't show every extreme that they name: `cell_flags`: 0 gas, 1 interface, 2 liquid. The bubble that a gas or interface cell belongs to; unused for liquid cells. `conversion`: 1 marks an interface cell that becomes liquid in this step; unused for other cells.
All inputs are finite; a program needn't handle non-finite values. No bound on the sum of `conversion` on one device may be relied on, other than what follows from the above.
Results may differ from a plain program's by a relative error of at most 0.0003.
Values sent between devices are 32-bit elements; how exact they have to be, the bound alone decides.
No kernel may reach another device: no remote copies, remote signals or barrier semaphores. Data moves between devices by JAX's collectives and lax.ppermute only.
A program may use at most 64 MiB of HBM per device.

v0:
```python
import jax
import jax.numpy as jnp
import numpy as np
from jax import lax
from jax.sharding import PartitionSpec as P

VELOCITIES = np.array(
    [
        [0, 0, 0],
        [1, 0, 0],
        [-1, 0, 0],
        [0, 1, 0],
        [0, -1, 0],
        [0, 0, 1],
        [0, 0, -1],
        [1, 1, 0],
        [-1, -1, 0],
        [1, -1, 0],
        [-1, 1, 0],
        [1, 0, 1],
        [-1, 0, -1],
        [1, 0, -1],
        [-1, 0, 1],
        [0, 1, 1],
        [0, -1, -1],
        [0, 1, -1],
        [0, -1, 1],
    ]
)
OPPOSITE = np.array([0, 2, 1, 4, 3, 6, 5, 8, 7, 10, 9, 12, 11, 14, 13, 16, 15, 18, 17])
WEIGHTS = np.array([1.0 / 3.0] + [1.0 / 18.0] * 6 + [1.0 / 36.0] * 12)
RELAX = 1.0 / 0.6
AMBIENT = 2.0


def padded_2(cells, sides, width):
    for axis, dim in sides:
        count = lax.axis_size(axis)
        ends = count - 1
        head = lax.slice_in_dim(cells, 0, width, axis=dim)
        tail = lax.slice_in_dim(cells, cells.shape[dim] - width, cells.shape[dim], axis=dim)
        cells = jnp.concatenate(
            [
                lax.ppermute(tail, axis, [(i, (i + 1) % count) for i in range(ends)]),
                cells,
                lax.ppermute(head, axis, [((i + 1) % count, i) for i in range(ends)]),
            ],
            axis=dim,
        )
    return cells


def moments(populations):
    density = jnp.sum(populations, axis=0)
    lattice = jnp.asarray(VELOCITIES.T, jnp.float32)
    flux = jnp.einsum("kq,qxyz->kxyz", lattice, populations, precision=lax.Precision.HIGHEST)
    return (density, flux / density[None])


def unit_equilibrium(velocity):
    lattice = jnp.asarray(VELOCITIES, jnp.float32)
    project = jnp.einsum("qk,kxyz->qxyz", lattice, velocity, precision=lax.Precision.HIGHEST)
    speed = jnp.sum(velocity * velocity, axis=0)
    weights = jnp.asarray(WEIGHTS, jnp.float32)[:, None, None, None]
    return weights * (1.0 + 3.0 * project + 4.5 * project * project - 1.5 * speed[None])


def window(layer, lane, extent_rows, extent_cols):
    offset_rows, offset_cols, offset_depth = (int(value) for value in VELOCITIES[lane])
    begin_rows, begin_cols = (1 - offset_rows, 1 - offset_cols)
    return jnp.roll(
        layer[begin_rows : begin_rows + extent_rows, begin_cols : begin_cols + extent_cols],
        offset_depth,
        axis=2,
    )


def domain(inside_rows, inside_cols, lane, extent_rows, extent_cols):
    begin_rows, begin_cols = (1 - int(VELOCITIES[lane][0]), 1 - int(VELOCITIES[lane][1]))
    return (
        inside_rows[begin_rows : begin_rows + extent_rows][:, None, None]
        & inside_cols[begin_cols : begin_cols + extent_cols][None, :, None]
    )


def pull_cells(padded, inside_rows, inside_cols, populations, fraction):
    extent_rows, extent_cols = (populations.shape[1], populations.shape[2])
    pulled = [populations[0]]
    gas_side = [jnp.zeros(populations.shape[1:], jnp.bool_)]
    mass_flux = jnp.zeros(populations.shape[1:], jnp.float32)
    targets = jnp.zeros(populations.shape[1:], jnp.float32)
    for lane in range(1, 19):
        source = window(padded[lane], lane, extent_rows, extent_cols)
        source_fraction = window(padded[19], lane, extent_rows, extent_cols)
        source_status = window(padded[20], lane, extent_rows, extent_cols)
        in_domain = domain(inside_rows, inside_cols, lane, extent_rows, extent_cols)
        source_flag = jnp.where(source_status > 2.5, source_status - 3.0, source_status)
        bounced = populations[int(OPPOSITE[lane])]
        pulled.append(jnp.where(in_domain, source, bounced))
        gas_side.append(in_domain & (source_flag < 0.5))
        weight = jnp.where(
            in_domain & (source_flag > 1.5),
            1.0,
            jnp.where(in_domain & (source_flag > 0.5), 0.5 * (fraction + source_fraction), 0.0),
        )
        mass_flux = mass_flux + weight * (source - bounced)
        targets = targets + jnp.where(in_domain & (jnp.abs(source_status - 1.0) < 0.5), 1.0, 0.0)
    return (jnp.stack(pulled), jnp.stack(gas_side), mass_flux, targets)


def settle_cells(
    pulled,
    gas_side,
    populations,
    velocity,
    local_gas,
    cell_mass,
    cell_flags,
    conversion,
    mass_flux,
    targets,
):
    unit = unit_equilibrium(velocity)
    paired = unit + unit[OPPOSITE]
    bounced = populations[OPPOSITE]
    wetted = cell_flags > 0
    passed = jnp.where(gas_side, local_gas[None] * paired - bounced, pulled)
    passed = jnp.where(wetted[None], passed, populations)
    moved_density, moved_velocity = moments(passed)
    relaxed = passed - RELAX * (passed - moved_density[None] * unit_equilibrium(moved_velocity))
    relaxed = jnp.where(wetted[None], relaxed, populations)
    filling = (cell_flags == 1) & (conversion == 1)
    updated = jnp.where(
        cell_flags == 1, cell_mass + mass_flux, jnp.where(cell_flags == 2, moved_density, cell_mass)
    )
    portion = jnp.where(filling, (updated - moved_density) / jnp.maximum(targets, 1.0), 0.0)
    updated = jnp.where(filling, moved_density, updated)
    return (relaxed, updated, portion)


def collect_spill(padded_portion, extent_rows, extent_cols):
    gained = jnp.zeros((extent_rows, extent_cols, padded_portion.shape[2]), jnp.float32)
    for lane in range(1, 19):
        gained = gained + window(padded_portion, lane, extent_rows, extent_cols)
    return gained


def tally_volume(contribution, bubble, count):
    labels = jnp.arange(count, dtype=jnp.int32)
    layer_terms = contribution.reshape(contribution.shape[0], -1)
    layer_labels = bubble.reshape(bubble.shape[0], -1)

    def accumulate(running, layer_pair):
        terms, cell_labels = layer_pair
        indicator = (cell_labels[:, None] == labels[None, :]).astype(jnp.float32)
        summed = jnp.dot(
            terms, indicator, precision=lax.Precision.HIGHEST, preferred_element_type=jnp.float32
        )
        return (running + summed, None)

    running, _ = lax.scan(accumulate, jnp.zeros((count,), jnp.float32), (layer_terms, layer_labels))
    return running


def spread_density(gas_density, bubble):
    labels = jnp.arange(gas_density.shape[0], dtype=jnp.int32)
    layer_labels = bubble.reshape(bubble.shape[0], -1)

    def lookup(cell_labels):
        indicator = (cell_labels[:, None] == labels[None, :]).astype(jnp.float32)
        return jnp.dot(
            indicator,
            gas_density,
            precision=lax.Precision.HIGHEST,
            preferred_element_type=jnp.float32,
        )

    return lax.map(lookup, layer_labels).reshape(bubble.shape)


def total_volume(partial_volume):
    return lax.psum(partial_volume, ("gx", "gy"))


def shards(populations, cell_mass, cell_flags, bubble, conversion, rest_volume):
    extent_rows, extent_cols, extent_depth = (
        populations.shape[1],
        populations.shape[2],
        populations.shape[3],
    )
    density, velocity = moments(populations)
    fraction = jnp.clip(cell_mass / density, 0.0, 1.0)
    status = jnp.where((cell_flags == 1) & (conversion == 1), 4, cell_flags).astype(jnp.float32)
    contribution = jnp.where(cell_flags == 0, 1.0, jnp.where(cell_flags == 1, 1.0 - fraction, 0.0))
    partial_volume = tally_volume(contribution, bubble, rest_volume.shape[0])
    volume = total_volume(partial_volume)
    channels = jnp.concatenate([populations, fraction[None], status[None]], axis=0)
    padded = padded_2(channels, (("gx", 1), ("gy", 2)), 1)
    start_rows = lax.axis_index("gx") * extent_rows + jnp.arange(
        -1, extent_rows + 1, dtype=jnp.int32
    )
    start_cols = lax.axis_index("gy") * extent_cols + jnp.arange(
        -1, extent_cols + 1, dtype=jnp.int32
    )
    inside_rows = (start_rows >= 0) & (start_rows < extent_rows * lax.axis_size("gx"))
    inside_cols = (start_cols >= 0) & (start_cols < extent_cols * lax.axis_size("gy"))
    pulled, gas_side, mass_flux, targets = pull_cells(
        padded, inside_rows, inside_cols, populations, fraction
    )
    gas_density = AMBIENT + rest_volume / jnp.maximum(volume, 1.0)
    local_gas = spread_density(gas_density, bubble)
    relaxed, updated, portion = settle_cells(
        pulled,
        gas_side,
        populations,
        velocity,
        local_gas,
        cell_mass,
        cell_flags,
        conversion,
        mass_flux,
        targets,
    )
    padded_portion = padded_2(portion, (("gx", 0), ("gy", 1)), 1)
    gained = collect_spill(padded_portion, extent_rows, extent_cols)
    receiver = (cell_flags == 1) & (conversion == 0)
    new_mass = jnp.where(receiver, updated + gained, updated)
    return (relaxed, new_mass, gas_density)


def solution(mesh):
    placed = (
        P(None, "gx", "gy", None),
        P("gx", "gy", None),
        P("gx", "gy", None),
        P("gx", "gy", None),
        P("gx", "gy", None),
        P(),
    )
    return jax.shard_map(
        shards,
        mesh=mesh,
        in_specs=placed,
        out_specs=(P(None, "gx", "gy", None), P("gx", "gy", None), P()),
        check_vma=False,
    )
```

profile of v0, /device:TPU:1, one launch (start us, length us, event | category | flops | bytes accessed | tf_op | source)
XLA Modules:
  0.0 112.7 jit_solution(17620983186998840845)
XLA Ops:
  0.6 1.1 reduce_sum.36
  1.8 0.8 convert_bitcast_fusion
  2.6 3.9 %collective-permute-start = (f32[21,1,8,128]{3,2,1,0:T(8,128)S(1)}, f32[21,1,8,128]{3,2,1,0:T(8,128)S(1)}, u32[]{:S(2)}, u32[]{:S(2)}) collective-permute-start(f32[21,1,8,128]{3,2,1,0:T(8,128)S(1)} %get-tuple-element.136), channel_id=1, source_target_pairs={{0,4},{4,8},{8,12},{12,16},{16,20},{20,24},{24,28},{1,5},{5,9},{9,... | collective-permute-start | bytes 258056 | tf_op jit(solution)/shard_map/ppermute | solution.py:44
  6.6 1.3 %collective-permute-start.1 = (f32[21,1,8,128]{3,2,1,0:T(8,128)S(1)}, f32[21,1,8,128]{3,2,1,0:T(8,128)S(1)}, u32[]{:S(2)}, u32[]{:S(2)}) collective-permute-start(f32[21,1,8,128]{3,2,1,0:T(8,128)S(1)} %get-tuple-element.137), channel_id=1, source_target_pairs={{4,0},{8,4},{12,8},{16,12},{20,16},{24,20},{28,24},{5,1},{9,5},{13... | collective-permute-start | bytes 258056 | tf_op jit(solution)/shard_map/ppermute | solution.py:46
  8.1 0.6 broadcast_compare_fusion.1
  8.8 0.6 copy-done.68
  9.4 0.6 multiply_reduce_fusion.1
  10.1 0.6 copy-done.66
  10.7 0.8 fusion.15
  11.6 0.7 copy-done.58
  12.4 2.5 %while.23 = (s32[]{:T(128)}, f32[96]{0:T(128)S(1)}, f32[6,1024]{1,0:T(8,128)S(1)}, s32[6,1024]{1,0:T(8,128)S(1)}, s32[]{:T(128)}, /*index=5*/s32[]{:T(128)}) while((s32[]{:T(128)}, f32[96]{0:T(128)S(1)}, f32[6,1024]{1,0:T(8,128)S(1)}, s32[6,1024]{1,0:T(8,128)S(1)}, s32[]{:T(128)}, /*index=5*/s32[]{:T(128)}) %tuple.207), condition=%wide.region_2.3_spmd.clone, body=%wide.region_1.2_spmd.clone.sunk | while | flops 1278147 | bytes 17367 | solution.py:161
  14.9 41.1 %psum.7 = f32[96]{0:T(128)S(1)} all-reduce(f32[96]{0:T(128)S(1)} %get-tuple-element.57), channel_id=1, replica_groups=mesh['gx'=8,'gy'=4] {'gx','gy'}, use_global_device_ids=true, to_apply=%region_3.4 | all-reduce | flops 96 | bytes 768 | tf_op jit(solution)/shard_map/psum | solution.py:182
  56.0 3.5 %while.22 = (s32[]{:T(128)}, f32[6,1024]{1,0:T(8,128)S(1)}, s32[6,1024]{1,0:T(8,128)S(1)}, f32[96]{0:T(128)S(1)}, s32[]{:T(128)}, /*index=5*/s32[]{:T(128)}) while((s32[]{:T(128)}, f32[6,1024]{1,0:T(8,128)S(1)}, s32[6,1024]{1,0:T(8,128)S(1)}, f32[96]{0:T(128)S(1)}, s32[]{:T(128)}, /*index=5*/s32[]{:T(128)}) %tuple.206), condition=%wide.region_5.6_spmd.clone, body=%wide.region_4.5_spmd.clone.sunk | while | flops 1277954 | bytes 25037 | solution.py:178
  60.0 0.7 broadcast_and_fusion.3
  60.7 0.6 gather_fusion.1
  61.3 0.6 gather_fusion
  62.1 5.3 %collective-permute-start.2 = (f32[21,8,1,128]{3,2,1,0:T(1,128)S(1)}, f32[21,8,1,128]{3,2,1,0:T(1,128)S(1)}, u32[]{:S(2)}, u32[]{:S(2)}) collective-permute-start(f32[21,8,1,128]{3,2,1,0:T(1,128)S(1)} %get-tuple-element.132), channel_id=1, source_target_pairs={{0,1},{1,2},{2,3},{4,5},{5,6},{6,7},{8,9},{9,10},{10,11},{12,13},{... | collective-permute-start | bytes 258056 | tf_op jit(solution)/shard_map/ppermute | solution.py:44
  67.3 1.9 %collective-permute-start.3 = (f32[21,8,1,128]{3,2,1,0:T(1,128)S(1)}, f32[21,8,1,128]{3,2,1,0:T(1,128)S(1)}, u32[]{:S(2)}, u32[]{:S(2)}) collective-permute-start(f32[21,8,1,128]{3,2,1,0:T(1,128)S(1)} %get-tuple-element.133), channel_id=1, source_target_pairs={{1,0},{2,1},{3,2},{5,4},{6,5},{7,6},{9,8},{10,9},{11,10},{13,12},{... | collective-permute-start | bytes 258056 | tf_op jit(solution)/shard_map/ppermute | solution.py:46
  69.3 3.9 %collective-permute-done.3 = f32[21,8,1,128]{3,2,1,0:T(1,128)S(1)} collective-permute-done((f32[21,8,1,128]{3,2,1,0:T(1,128)S(1)}, f32[21,8,1,128]{3,2,1,0:T(1,128)S(1)}, u32[]{:S(2)}, u32[]{:S(2)}) %collective-permute-start.3) | collective-permute-done | bytes 86048 | tf_op jit(solution)/shard_map/ppermute | solution.py:46
  73.2 0.8 fusion.207
  73.9 0.8 fusion.208
  74.7 0.8 fusion.185
  75.5 0.7 fusion.186
  77.2 0.7 copy-done.53
  78.0 0.7 copy-done.55
  78.9 0.7 copy-done.56
  79.7 0.7 copy-done.62
  80.5 0.7 copy-done.60
  81.2 0.6 copy-done.61
  81.9 0.6 copy-done.59
  82.7 0.7 fusion.180
  83.5 0.7 bitcast_select_fusion.6
  85.0 0.6 copy-done.13
  86.4 0.7 bitcast_select_fusion
  87.1 0.8 maximum_select_fusion.4
  87.9 0.7 maximum_select_fusion.8
  88.6 3.1 %stack.91 = f32[19,6,8,128]{3,0,2,1:T(8,128)S(1)} concatenate(f32[1,6,8,128]{3,0,2,1:T(1,128)} %bitcast.312, f32[1,6,8,128]{3,0,2,1:T(1,128)} %bitcast.316, f32[1,6,8,128]{3,0,2,1:T(1,128)} %bitcast.315, f32[1,6,8,128]{3,0,2,1:T(1,128)} %bitcast.322, f32[1,6,8,128]{3,0,2,1:T(1,128)} %bitcast.321, f32[1,6,8,128]{3,0,2,1:T(1,128)} %bitcast.325, f32[1,6,8,128]{3,0,2,1:T(1,128)} %bitcast.326, ...), dimensions={0} | concatenate | bytes 933888 | tf_op jit(solution)/shard_map/stack | solution.py:108
  92.1 1.5 %fusion.178 = (f32[6,8,128]{2,1,0:T(8,128)S(1)}, f32[19,6,8,128]{3,0,2,1:T(8,128)S(1)}) fusion(f32[19,6,8,128]{3,2,1,0:T(8,128)S(1)} %copy-done, f32[19,6,8,128]{3,0,2,1:T(8,128)S(1)} %stack.91, f32[19,6,8,128]{3,2,1,0:T(8,128)S(1)} %gather_fusion.1, f32[19,6,8,128]{3,0,2,1:T(8,128)S(1)} %fusion.15, f32[19,6,8,128]{3,2,1,0:T(8,128)S(1)} %gather_fusion, ...), kind=kLoop, calls=%fused_computation.443 | loop fusion | flops 694272 | bytes 2973696 | tf_op jit(solution)/shard_map/reduce_sum | solution.py:54
  94.3 1.7 %divide_select_fusion = (f32[6,8,128]{2,1,0:T(8,128)S(1)}, f32[6,8,128]{2,1,0:T(8,128)S(1)}) fusion(f32[6,8,128]{2,1,0:T(8,128)S(1)} %get-tuple-element.110, f32[8,10,128]{2,1,0:T(8,128)S(1)} %get-tuple-element.114, pred[6,8]{1,0:T(8,128)(4,1)} %get-tuple-element.290, pred[6,8]{1,0:T(8,128)(4,1)} %get-tuple-element.284, ...), kind=kLoop, calls=%fused_computation.340 | loop fusion | flops 2463744 | bytes 1941936 | tf_op jit(solution)/shard_map/jit(_where)/select_n | solution.py:136
  96.0 3.0 %collective-permute-start.4 = (f32[1,8,128]{2,1,0:T(8,128)S(1)}, f32[1,8,128]{2,1,0:T(8,128)S(1)}, u32[]{:S(2)}, u32[]{:S(2)}) collective-permute-start(f32[1,8,128]{2,1,0:T(8,128)S(1)} %get-tuple-element.282), channel_id=1, source_target_pairs={{0,4},{4,8},{8,12},{12,16},{16,20},{20,24},{24,28},{1,5},{5,9},{9,... | collective-permute-start | bytes 12296 | tf_op jit(solution)/shard_map/ppermute | solution.py:44
  99.0 1.3 %collective-permute-start.5 = (f32[1,8,128]{2,1,0:T(8,128)S(1)}, f32[1,8,128]{2,1,0:T(8,128)S(1)}, u32[]{:S(2)}, u32[]{:S(2)}) collective-permute-start(f32[1,8,128]{2,1,0:T(8,128)S(1)} %get-tuple-element.283), channel_id=1, source_target_pairs={{4,0},{8,4},{12,8},{16,12},{20,16},{24,20},{28,24},{5,1},{9,5},{13... | collective-permute-start | bytes 12296 | tf_op jit(solution)/shard_map/ppermute | solution.py:46
  100.9 0.6 copy-done.57
  101.5 1.0 fusion.23
  102.6 0.9 copy.112
  103.4 3.2 %collective-permute-start.6 = (f32[8,1,128]{2,1,0:T(1,128)S(1)}, f32[8,1,128]{2,1,0:T(1,128)S(1)}, u32[]{:S(2)}, u32[]{:S(2)}) collective-permute-start(f32[8,1,128]{2,1,0:T(1,128)S(1)} %get-tuple-element.271), channel_id=1, source_target_pairs={{0,1},{1,2},{2,3},{4,5},{5,6},{6,7},{8,9},{9,10},{10,11},{12,13},{... | collective-permute-start | bytes 12296 | tf_op jit(solution)/shard_map/ppermute | solution.py:44
  106.7 1.9 %collective-permute-start.7 = (f32[8,1,128]{2,1,0:T(1,128)S(1)}, f32[8,1,128]{2,1,0:T(1,128)S(1)}, u32[]{:S(2)}, u32[]{:S(2)}) collective-permute-start(f32[8,1,128]{2,1,0:T(1,128)S(1)} %get-tuple-element.270), channel_id=1, source_target_pairs={{1,0},{2,1},{3,2},{5,4},{6,5},{7,6},{9,8},{10,9},{11,10},{13,12},{... | collective-permute-start | bytes 12296 | tf_op jit(solution)/shard_map/ppermute | solution.py:46
  108.8 2.8 %collective-permute-done.7 = f32[8,1,128]{2,1,0:T(1,128)S(1)} collective-permute-done((f32[8,1,128]{2,1,0:T(1,128)S(1)}, f32[8,1,128]{2,1,0:T(1,128)S(1)}, u32[]{:S(2)}, u32[]{:S(2)}) %collective-permute-start.7) | collective-permute-done | bytes 4128 | tf_op jit(solution)/shard_map/ppermute | solution.py:46
  111.9 0.8 add_select_fusion
  (238 shorter events, 11.7 us)
Async XLA Ops:
  0.6 2.0 %copy-start = (f32[19,6,8,128]{3,2,1,0:T(8,128)S(1)}, f32[19,6,8,128]{3,2,1,0:T(8,128)}, u32[]{:S(2)}) copy-start(f32[19,6,8,128]{3,2,1,0:T(8,128)} %param.19) | copy-start | bytes 1400836
  1.8 7.1 %copy-start.3 = (f32[6,8,128]{2,1,0:T(8,128)}, f32[6,8,128]{2,1,0:T(8,128)S(1)}, u32[]{:S(2)}) copy-start(f32[6,8,128]{2,1,0:T(8,128)S(1)} %reduce_sum.36) | copy-start | bytes 73732
  2.6 59.3 %collective-permute-start = (f32[21,1,8,128]{3,2,1,0:T(8,128)S(1)}, f32[21,1,8,128]{3,2,1,0:T(8,128)S(1)}, u32[]{:S(2)}, u32[]{:S(2)}) collective-permute-start(f32[21,1,8,128]{3,2,1,0:T(8,128)S(1)} %get-tuple-element.136), channel_id=1, source_target_pairs={{0,4},{4,8},{8,12},{12,16},{16,20},{20,24},{24,28},{1,5},{5,9},{9,... | collective-permute-start | bytes 258056 | tf_op jit(solution)/shard_map/ppermute | solution.py:44
  6.6 55.4 %collective-permute-start.1 = (f32[21,1,8,128]{3,2,1,0:T(8,128)S(1)}, f32[21,1,8,128]{3,2,1,0:T(8,128)S(1)}, u32[]{:S(2)}, u32[]{:S(2)}) collective-permute-start(f32[21,1,8,128]{3,2,1,0:T(8,128)S(1)} %get-tuple-element.137), channel_id=1, source_target_pairs={{4,0},{8,4},{12,8},{16,12},{20,16},{24,20},{28,24},{5,1},{9,5},{13... | collective-permute-start | bytes 258056 | tf_op jit(solution)/shard_map/ppermute | solution.py:46
  14.9 41.1 %copy-start.64 = (f32[96]{0:T(128)S(1)}, f32[96]{0:T(128)}, u32[]{:S(2)}) copy-start(f32[96]{0:T(128)} %param.24) | copy-start | bytes 1156
  62.1 7.2 %collective-permute-start.2 = (f32[21,8,1,128]{3,2,1,0:T(1,128)S(1)}, f32[21,8,1,128]{3,2,1,0:T(1,128)S(1)}, u32[]{:S(2)}, u32[]{:S(2)}) collective-permute-start(f32[21,8,1,128]{3,2,1,0:T(1,128)S(1)} %get-tuple-element.132), channel_id=1, source_target_pairs={{0,1},{1,2},{2,3},{4,5},{5,6},{6,7},{8,9},{9,10},{10,11},{12,13},{... | collective-permute-start | bytes 258056 | tf_op jit(solution)/shard_map/ppermute | solution.py:44
  67.3 5.8 %collective-permute-start.3 = (f32[21,8,1,128]{3,2,1,0:T(1,128)S(1)}, f32[21,8,1,128]{3,2,1,0:T(1,128)S(1)}, u32[]{:S(2)}, u32[]{:S(2)}) collective-permute-start(f32[21,8,1,128]{3,2,1,0:T(1,128)S(1)} %get-tuple-element.133), channel_id=1, source_target_pairs={{1,0},{2,1},{3,2},{5,4},{6,5},{7,6},{9,8},{10,9},{11,10},{13,12},{... | collective-permute-start | bytes 258056 | tf_op jit(solution)/shard_map/ppermute | solution.py:46
  88.6 3.1 %copy-start.14 = (pred[19,6,8,128]{3,2,1,0:T(8,128)(4,1)S(1)}, pred[19,6,8,128]{3,2,1,0:T(8,128)(4,1)}, u32[]{:S(2)}) copy-start(pred[19,6,8,128]{3,2,1,0:T(8,128)(4,1)} %copy-done.13) | copy-start | bytes 350212
  91.7 1.9 %copy-start.16 = (f32[6,8,1]{2,1,0:T(8,128)S(1)}, f32[6,8,1]{2,1,0:T(8,128)}, u32[]{:S(2)}) copy-start(f32[6,8,1]{2,1,0:T(8,128)} %get-tuple-element.239) | copy-start | bytes 580
  91.7 1.9 %copy-start.17 = (f32[6,8,1]{2,1,0:T(8,128)S(1)}, f32[6,8,1]{2,1,0:T(8,128)}, u32[]{:S(2)}) copy-start(f32[6,8,1]{2,1,0:T(8,128)} %get-tuple-element.240) | copy-start | bytes 580
  91.7 1.9 %copy-start.18 = (f32[6,8,1]{2,1,0:T(8,128)S(1)}, f32[6,8,1]{2,1,0:T(8,128)}, u32[]{:S(2)}) copy-start(f32[6,8,1]{2,1,0:T(8,128)} %get-tuple-element.241) | copy-start | bytes 580
  91.7 1.9 %copy-start.19 = (f32[6,8,1]{2,1,0:T(8,128)S(1)}, f32[6,8,1]{2,1,0:T(8,128)}, u32[]{:S(2)}) copy-start(f32[6,8,1]{2,1,0:T(8,128)} %get-tuple-element.242) | copy-start | bytes 580
  91.7 1.9 %copy-start.20 = (f32[6,8,1]{2,1,0:T(8,128)S(1)}, f32[6,8,1]{2,1,0:T(8,128)}, u32[]{:S(2)}) copy-start(f32[6,8,1]{2,1,0:T(8,128)} %get-tuple-element.243) | copy-start | bytes 580
  91.8 1.9 %copy-start.21 = (f32[6,8,1]{2,1,0:T(8,128)S(1)}, f32[6,8,1]{2,1,0:T(8,128)}, u32[]{:S(2)}) copy-start(f32[6,8,1]{2,1,0:T(8,128)} %get-tuple-element.244) | copy-start | bytes 580
  91.8 1.9 %copy-start.22 = (f32[6,8,1]{2,1,0:T(8,128)S(1)}, f32[6,8,1]{2,1,0:T(8,128)}, u32[]{:S(2)}) copy-start(f32[6,8,1]{2,1,0:T(8,128)} %get-tuple-element.245) | copy-start | bytes 580
  91.8 1.9 %copy-start.23 = (f32[6,8,1]{2,1,0:T(8,128)S(1)}, f32[6,8,1]{2,1,0:T(8,128)}, u32[]{:S(2)}) copy-start(f32[6,8,1]{2,1,0:T(8,128)} %get-tuple-element.246) | copy-start | bytes 580
  91.8 1.9 %copy-start.24 = (f32[6,8,127]{2,1,0:T(8,128)S(1)}, f32[6,8,127]{2,1,0:T(8,128)}, u32[]{:S(2)}) copy-start(f32[6,8,127]{2,1,0:T(8,128)} %get-tuple-element.247) | copy-start | bytes 73156
  91.8 1.9 %copy-start.25 = (f32[6,8,127]{2,1,0:T(8,128)S(1)}, f32[6,8,127]{2,1,0:T(8,128)}, u32[]{:S(2)}) copy-start(f32[6,8,127]{2,1,0:T(8,128)} %get-tuple-element.258) | copy-start | bytes 73156
  91.8 1.9 %copy-start.26 = (f32[6,8,127]{2,1,0:T(8,128)S(1)}, f32[6,8,127]{2,1,0:T(8,128)}, u32[]{:S(2)}) copy-start(f32[6,8,127]{2,1,0:T(8,128)} %get-tuple-element.259) | copy-start | bytes 73156
  91.8 1.9 %copy-start.27 = (f32[6,8,127]{2,1,0:T(8,128)S(1)}, f32[6,8,127]{2,1,0:T(8,128)}, u32[]{:S(2)}) copy-start(f32[6,8,127]{2,1,0:T(8,128)} %get-tuple-element.260) | copy-start | bytes 73156
  91.8 1.9 %copy-start.28 = (f32[6,8,127]{2,1,0:T(8,128)S(1)}, f32[6,8,127]{2,1,0:T(8,128)}, u32[]{:S(2)}) copy-start(f32[6,8,127]{2,1,0:T(8,128)} %get-tuple-element.261) | copy-start | bytes 73156
  91.8 1.9 %copy-start.29 = (f32[6,8,127]{2,1,0:T(8,128)S(1)}, f32[6,8,127]{2,1,0:T(8,128)}, u32[]{:S(2)}) copy-start(f32[6,8,127]{2,1,0:T(8,128)} %get-tuple-element.262) | copy-start | bytes 73156
  91.8 1.9 %copy-start.30 = (f32[6,8,127]{2,1,0:T(8,128)S(1)}, f32[6,8,127]{2,1,0:T(8,128)}, u32[]{:S(2)}) copy-start(f32[6,8,127]{2,1,0:T(8,128)} %get-tuple-element.263) | copy-start | bytes 73156
  91.9 1.9 %copy-start.31 = (f32[6,8,127]{2,1,0:T(8,128)S(1)}, f32[6,8,127]{2,1,0:T(8,128)}, u32[]{:S(2)}) copy-start(f32[6,8,127]{2,1,0:T(8,128)} %get-tuple-element.264) | copy-start | bytes 73156
  91.9 1.9 %copy-start.32 = (f32[6,8,127]{2,1,0:T(8,128)S(1)}, f32[6,8,127]{2,1,0:T(8,128)}, u32[]{:S(2)}) copy-start(f32[6,8,127]{2,1,0:T(8,128)} %get-tuple-element.265) | copy-start | bytes 73156
  91.9 1.9 %copy-start.33 = (f32[6,8,1]{2,1,0:T(8,128)S(1)}, f32[6,8,1]{2,1,0:T(8,128)}, u32[]{:S(2)}) copy-start(f32[6,8,1]{2,1,0:T(8,128)} %get-tuple-element.168) | copy-start | bytes 580
  91.9 1.9 %copy-start.34 = (f32[6,8,1]{2,1,0:T(8,128)S(1)}, f32[6,8,1]{2,1,0:T(8,128)}, u32[]{:S(2)}) copy-start(f32[6,8,1]{2,1,0:T(8,128)} %get-tuple-element.169) | copy-start | bytes 580
  91.9 1.9 %copy-start.35 = (f32[6,8,1]{2,1,0:T(8,128)S(1)}, f32[6,8,1]{2,1,0:T(8,128)}, u32[]{:S(2)}) copy-start(f32[6,8,1]{2,1,0:T(8,128)} %get-tuple-element.170) | copy-start | bytes 580
  91.9 1.9 %copy-start.36 = (f32[6,8,1]{2,1,0:T(8,128)S(1)}, f32[6,8,1]{2,1,0:T(8,128)}, u32[]{:S(2)}) copy-start(f32[6,8,1]{2,1,0:T(8,128)} %get-tuple-element.171) | copy-start | bytes 580
  91.9 1.9 %copy-start.37 = (f32[6,8,1]{2,1,0:T(8,128)S(1)}, f32[6,8,1]{2,1,0:T(8,128)}, u32[]{:S(2)}) copy-start(f32[6,8,1]{2,1,0:T(8,128)} %get-tuple-element.172) | copy-start | bytes 580
  91.9 1.9 %copy-start.38 = (f32[6,8,1]{2,1,0:T(8,128)S(1)}, f32[6,8,1]{2,1,0:T(8,128)}, u32[]{:S(2)}) copy-start(f32[6,8,1]{2,1,0:T(8,128)} %get-tuple-element.173) | copy-start | bytes 580
  91.9 1.9 %copy-start.39 = (f32[6,8,1]{2,1,0:T(8,128)S(1)}, f32[6,8,1]{2,1,0:T(8,128)}, u32[]{:S(2)}) copy-start(f32[6,8,1]{2,1,0:T(8,128)} %get-tuple-element.174) | copy-start | bytes 580
  91.9 1.9 %copy-start.40 = (f32[6,8,1]{2,1,0:T(8,128)S(1)}, f32[6,8,1]{2,1,0:T(8,128)}, u32[]{:S(2)}) copy-start(f32[6,8,1]{2,1,0:T(8,128)} %get-tuple-element.175) | copy-start | bytes 580
  92.0 1.9 %copy-start.41 = (f32[6,8,1]{2,1,0:T(8,128)S(1)}, f32[6,8,1]{2,1,0:T(8,128)}, u32[]{:S(2)}) copy-start(f32[6,8,1]{2,1,0:T(8,128)} %get-tuple-element.176) | copy-start | bytes 580
  92.0 1.9 %copy-start.42 = (f32[6,8,1]{2,1,0:T(8,128)S(1)}, f32[6,8,1]{2,1,0:T(8,128)}, u32[]{:S(2)}) copy-start(f32[6,8,1]{2,1,0:T(8,128)} %get-tuple-element.177) | copy-start | bytes 580
  92.0 1.9 %copy-start.43 = (f32[6,8,1]{2,1,0:T(8,128)S(1)}, f32[6,8,1]{2,1,0:T(8,128)}, u32[]{:S(2)}) copy-start(f32[6,8,1]{2,1,0:T(8,128)} %get-tuple-element.320) | copy-start | bytes 580
  92.0 1.9 %copy-start.44 = (f32[6,8,127]{2,1,0:T(8,128)S(1)}, f32[6,8,127]{2,1,0:T(8,128)}, u32[]{:S(2)}) copy-start(f32[6,8,127]{2,1,0:T(8,128)} %get-tuple-element.178) | copy-start | bytes 73156
  92.0 1.9 %copy-start.45 = (f32[6,8,127]{2,1,0:T(8,128)S(1)}, f32[6,8,127]{2,1,0:T(8,128)}, u32[]{:S(2)}) copy-start(f32[6,8,127]{2,1,0:T(8,128)} %get-tuple-element.179) | copy-start | bytes 73156
  92.0 1.9 %copy-start.46 = (f32[6,8,127]{2,1,0:T(8,128)S(1)}, f32[6,8,127]{2,1,0:T(8,128)}, u32[]{:S(2)}) copy-start(f32[6,8,127]{2,1,0:T(8,128)} %get-tuple-element.180) | copy-start | bytes 73156
  92.0 1.9 %copy-start.47 = (f32[6,8,127]{2,1,0:T(8,128)S(1)}, f32[6,8,127]{2,1,0:T(8,128)}, u32[]{:S(2)}) copy-start(f32[6,8,127]{2,1,0:T(8,128)} %get-tuple-element.181) | copy-start | bytes 73156
  92.0 1.9 %copy-start.48 = (f32[6,8,127]{2,1,0:T(8,128)S(1)}, f32[6,8,127]{2,1,0:T(8,128)}, u32[]{:S(2)}) copy-start(f32[6,8,127]{2,1,0:T(8,128)} %get-tuple-element.182) | copy-start | bytes 73156
  92.0 1.9 %copy-start.49 = (f32[6,8,127]{2,1,0:T(8,128)S(1)}, f32[6,8,127]{2,1,0:T(8,128)}, u32[]{:S(2)}) copy-start(f32[6,8,127]{2,1,0:T(8,128)} %get-tuple-element.183) | copy-start | bytes 73156
  92.0 1.9 %copy-start.50 = (f32[6,8,127]{2,1,0:T(8,128)S(1)}, f32[6,8,127]{2,1,0:T(8,128)}, u32[]{:S(2)}) copy-start(f32[6,8,127]{2,1,0:T(8,128)} %get-tuple-element.184) | copy-start | bytes 73156
  96.0 4.3 %copy-start.69 = (f32[3,19,1,1]{1,0,3,2:T(4,128)S(1)}, f32[3,19,1,1]{1,0,3,2:T(4,128)}, u32[]{:S(2)}) copy-start(f32[3,19,1,1]{1,0,3,2:T(4,128)} %constant.139) | copy-start | bytes 688
  96.0 7.4 %collective-permute-start.4 = (f32[1,8,128]{2,1,0:T(8,128)S(1)}, f32[1,8,128]{2,1,0:T(8,128)S(1)}, u32[]{:S(2)}, u32[]{:S(2)}) collective-permute-start(f32[1,8,128]{2,1,0:T(8,128)S(1)} %get-tuple-element.282), channel_id=1, source_target_pairs={{0,4},{4,8},{8,12},{12,16},{16,20},{20,24},{24,28},{1,5},{5,9},{9,... | collective-permute-start | bytes 12296 | tf_op jit(solution)/shard_map/ppermute | solution.py:44
  99.0 4.4 %collective-permute-start.5 = (f32[1,8,128]{2,1,0:T(8,128)S(1)}, f32[1,8,128]{2,1,0:T(8,128)S(1)}, u32[]{:S(2)}, u32[]{:S(2)}) collective-permute-start(f32[1,8,128]{2,1,0:T(8,128)S(1)} %get-tuple-element.283), channel_id=1, source_target_pairs={{4,0},{8,4},{12,8},{16,12},{20,16},{24,20},{28,24},{5,1},{9,5},{13... | collective-permute-start | bytes 12296 | tf_op jit(solution)/shard_map/ppermute | solution.py:46
  103.4 5.3 %collective-permute-start.6 = (f32[8,1,128]{2,1,0:T(1,128)S(1)}, f32[8,1,128]{2,1,0:T(1,128)S(1)}, u32[]{:S(2)}, u32[]{:S(2)}) collective-permute-start(f32[8,1,128]{2,1,0:T(1,128)S(1)} %get-tuple-element.271), channel_id=1, source_target_pairs={{0,1},{1,2},{2,3},{4,5},{5,6},{6,7},{8,9},{9,10},{10,11},{12,13},{... | collective-permute-start | bytes 12296 | tf_op jit(solution)/shard_map/ppermute | solution.py:44
  106.7 4.9 %collective-permute-start.7 = (f32[8,1,128]{2,1,0:T(1,128)S(1)}, f32[8,1,128]{2,1,0:T(1,128)S(1)}, u32[]{:S(2)}, u32[]{:S(2)}) collective-permute-start(f32[8,1,128]{2,1,0:T(1,128)S(1)} %get-tuple-element.270), channel_id=1, source_target_pairs={{1,0},{2,1},{3,2},{5,4},{6,5},{7,6},{9,8},{10,9},{11,10},{13,12},{... | collective-permute-start | bytes 12296 | tf_op jit(solution)/shard_map/ppermute | solution.py:46
  (32 other events, 24.7 us)
where the time goes:
time: 114 us; the launch traced here: 113 us
  blocking collectives  41.1 us (36%)
  starting transfers between devices  21.8 us (19%)
  local copies, waits for them, and re-layouts  19.9 us (17%)
  other arithmetic  13 us (11%)
  matrix products  7.83 us (7%)
  waiting for transfers between devices  6.69 us (6%)
  between operations  1.85 us (2%)
    psum x1, blocking collectives, total_volume(): return lax.psum(partial_volume, ('gx', 'gy'))  41.1 us
    ppermute x4, starting transfers between devices, padded_2(): lax.ppermute(tail, axis, [(i, (i + 1) % count) for i in range(ends)])  15.4 us
    unnamed x150, local copies, waits for them, and re-layouts  10.6 us
    ppermute x4, waiting for transfers between devices, padded_2(): lax.ppermute(head, axis, [((i + 1) % count, i) for i in range(ends)])  6.68 us
    ppermute x4, starting transfers between devices, padded_2(): lax.ppermute(head, axis, [((i + 1) % count, i) for i in range(ends)])  6.43 us
    slice x20, local copies, waits for them, and re-layouts, window(): jnp.roll(layer[begin_rows:begin_rows + extent_rows, begin_cols:begin_cols...  4.09 us
    another operation x1, local copies, waits for them, and re-layouts, pull_cells(): return (jnp.stack(pulled), jnp.stack(gas_side), mass_flux, targets)  3.12 us
    select_n x4, other arithmetic, pull_cells(): pulled.append(jnp.where(in_domain, source, bounced))  2.9 us
  transfers between devices with their start and end apart: 8, of which 2 were waited for; matrix products, arithmetic and copies ran while one was open for 11% of the time, Pallas kernels for 0%

commit v1 on v0

v1 whole, which is shorter than its diff:
```python
import functools

import jax
import jax.numpy as jnp
import numpy as np
from jax import lax
from jax.experimental import pallas as pl
from jax.experimental.pallas import tpu as pltpu
from jax.sharding import PartitionSpec as P

VELOCITIES = np.array(
    [
        [0, 0, 0],
        [1, 0, 0],
        [-1, 0, 0],
        [0, 1, 0],
        [0, -1, 0],
        [0, 0, 1],
        [0, 0, -1],
        [1, 1, 0],
        [-1, -1, 0],
        [1, -1, 0],
        [-1, 1, 0],
        [1, 0, 1],
        [-1, 0, -1],
        [1, 0, -1],
        [-1, 0, 1],
        [0, 1, 1],
        [0, -1, -1],
        [0, 1, -1],
        [0, -1, 1],
    ]
)
OPPOSITE = [0, 2, 1, 4, 3, 6, 5, 8, 7, 10, 9, 12, 11, 14, 13, 16, 15, 18, 17]
WEIGHTS = [1.0 / 3.0] + [1.0 / 18.0] * 6 + [1.0 / 36.0] * 12
RELAX = 1.0 / 0.6
AMBIENT = 2.0
LANES = 19
MASS, FRAC, CODE, BUB = 19, 20, 21, 22
CHANNELS = 23
WALL, GAS, FACE, LIQUID, FILLING = 0.0, 1.0, 2.0, 3.0, 5.0


def heading(axis, sign):
    return [q for q in range(LANES) if VELOCITIES[q][axis] == sign]


def heading_both(rows, cols):
    return [q for q in range(LANES) if VELOCITIES[q][0] == rows and VELOCITIES[q][1] == cols][0]


def outer(axis, sign):
    return heading(axis, sign) + [FRAC, CODE]


def roll(x, shift):
    return pltpu.roll(x, shift % x.shape[-1], x.ndim - 1)


def first_kernel(
    rows, cols, chunks, copies,
    pops, mass, flags, bubble, conversion,
    aux, low, high, left, right, tally,
):
    block = rows * cols
    masses, fractions, codes = [], [], []
    contributions = []
    for r in range(rows):
        at = pl.ds(r * cols, cols)
        density = pops[at, :]
        for q in range(1, LANES):
            density = density + pops[pl.ds(q * block + r * cols, cols), :]
        m = mass[at, :]
        flag = flags[at, :]
        fraction = jnp.clip(m / density, 0.0, 1.0)
        code = jnp.where(
            (flag == 1) & (conversion[at, :] == 1), FILLING, flag.astype(jnp.float32) + 1.0
        )
        aux[at, :] = m
        aux[pl.ds(block + r * cols, cols), :] = fraction
        aux[pl.ds(2 * block + r * cols, cols), :] = code
        aux[pl.ds(3 * block + r * cols, cols), :] = bubble[at, :].astype(jnp.float32)
        contributions.append(
            jnp.where(flag == 0, 1.0, jnp.where(flag == 1, 1.0 - fraction, 0.0))
        )

    def tile(channel, r):
        ref, base = (pops, channel) if channel < LANES else (aux, channel - LANES)
        return ref[pl.ds(base * block + r * cols, cols), :]

    def column(channel, c):
        ref, base = (pops, channel) if channel < LANES else (aux, channel - LANES)
        return ref[pl.ds(base * block + c, rows, stride=cols), :]

    for out, inner_row, outer_row, sign in ((low, 0, 1, -1), (high, rows - 1, rows - 2, 1)):
        for channel in range(CHANNELS):
            out[pl.ds(channel * cols, cols), :] = tile(channel, inner_row)
        for k, channel in enumerate(outer(0, sign)):
            out[pl.ds((CHANNELS + k) * cols, cols), :] = tile(channel, outer_row)
    tall = rows + 2
    for out, inner_col, outer_col, sign in ((left, 0, 1, -1), (right, cols - 1, cols - 2, 1)):
        for channel in range(CHANNELS):
            out[pl.ds(channel * tall + 1, rows), :] = column(channel, inner_col)
        for k, channel in enumerate(outer(1, sign)):
            out[pl.ds((CHANNELS + k) * tall + 1, rows), :] = column(channel, outer_col)

    ones = jnp.ones((8, 128), jnp.float32)
    lane_count = mass.shape[-1]

    def count(chunk):
        labels = lax.broadcasted_iota(jnp.int32, (128, lane_count), 0) + chunk * 128
        total = jnp.zeros((128, lane_count), jnp.float32)
        for r in range(rows):
            for c in range(cols):
                row = bubble[pl.ds(r * cols + c, 1), :]
                term = contributions[r][c : c + 1, :]
                total = total + jnp.where(labels == row, term, 0.0)
        return lax.dot_general(
            jnp.ones((8, lane_count), jnp.float32),
            total,
            (((1,), (1,)), ((), ())),
            precision=lax.Precision.HIGHEST,
            preferred_element_type=jnp.float32,
        )

    del ones
    for chunk in range(chunks):
        summed = count(chunk)
        for k in range(copies):
            tally[k, chunk] = summed


def second_kernel(rows, cols, low, high, left, right, left_out, right_out):
    tall = rows + 2
    for part, out, inner_col, outer_col, sign in (
        (left, left_out, 0, 1, -1),
        (right, right_out, cols - 1, cols - 2, 1),
    ):
        carried = (CHANNELS + len(outer(1, sign))) * tall
        out[pl.ds(0, carried), :] = part[pl.ds(0, carried), :]
        spare = carried
        for halo, row, towards in ((low, 0, 1), (high, tall - 1, -1)):
            out[pl.ds(row, CHANNELS, stride=tall), :] = halo[
                pl.ds(inner_col, CHANNELS, stride=cols), :
            ]
            for k, channel in enumerate(outer(1, sign)):
                out[pl.ds((CHANNELS + k) * tall + row, 1), :] = halo[
                    pl.ds(channel * cols + outer_col, 1), :
                ]
            beyond = outer(0, towards)
            out[pl.ds(spare, len(beyond)), :] = halo[
                pl.ds(CHANNELS * cols + inner_col, len(beyond), stride=cols), :
            ]
            spare += len(beyond)
            for channel in (heading_both(towards, sign), FRAC, CODE):
                k = beyond.index(channel)
                out[pl.ds(spare, 1), :] = halo[pl.ds((CHANNELS + k) * cols + outer_col, 1), :]
                spare += 1


def side_tiles(rows):
    tall = rows + 2
    used = (CHANNELS + 7) * tall + 2 * (7 + 3)
    return -(-used // 8) * 8


def third_kernel(
    rows, cols, chunks, copies, labels,
    pops, aux, low, high, left, right, tally, rest,
    relaxed_out, new_mass_out, gas_out,
    cells, near, sums, table, relaxed_stage, mass_stage, wet_sem, mass_sem,
):
    block = rows * cols
    tall = rows + 2
    high_rows = rows + 4
    wide = cols + 4
    total_rows = wide * high_rows

    for chunk in range(chunks):
        volume = tally[0, chunk]
        for k in range(1, copies):
            volume = volume + tally[k, chunk]
        here = min(128, labels - chunk * 128)
        gas = AMBIENT + rest[0:1, pl.ds(chunk * 128, here)] / jnp.maximum(volume[0:1, :here], 1.0)
        gas_out[0:1, pl.ds(chunk * 128, here)] = gas
        table[chunk, :, pl.ds(0, here)] = jnp.broadcast_to(gas, (8, here))

    for channel in range(CHANNELS):
        ref, base = (pops, channel) if channel < LANES else (aux, channel - LANES)
        for c in range(cols):
            cells[channel, pl.ds((c + 2) * high_rows + 2, rows), :] = ref[
                pl.ds(base * block + c, rows, stride=cols), :
            ]
    for halo, inner_row, outer_row, towards in (
        (low, 1, 0, 1),
        (high, high_rows - 2, high_rows - 1, -1),
    ):
        for channel in range(CHANNELS):
            cells[channel, pl.ds(2 * high_rows + inner_row, cols, stride=high_rows), :] = halo[
                pl.ds(channel * cols, cols), :
            ]
        for k, channel in enumerate(outer(0, towards)):
            cells[channel, pl.ds(2 * high_rows + outer_row, cols, stride=high_rows), :] = halo[
                pl.ds((CHANNELS + k) * cols, cols), :
            ]
    for halo, inner_col, outer_col, sign in (
        (left, 1, 0, 1),
        (right, wide - 2, wide - 1, -1),
    ):
        for channel in range(CHANNELS):
            cells[channel, pl.ds(inner_col * high_rows + 1, tall), :] = halo[
                pl.ds(channel * tall, tall), :
            ]
        for k, channel in enumerate(outer(1, sign)):
            cells[channel, pl.ds(outer_col * high_rows + 1, tall), :] = halo[
                pl.ds((CHANNELS + k) * tall, tall), :
            ]
        spare = (CHANNELS + 7) * tall
        for row, towards in ((0, 1), (high_rows - 1, -1)):
            for channel in outer(0, towards):
                cells[channel, pl.ds(inner_col * high_rows + row, 1), :] = halo[
                    pl.ds(spare, 1), :
                ]
                spare += 1
            for channel in (heading_both(towards, sign), FRAC, CODE):
                cells[channel, pl.ds(outer_col * high_rows + row, 1), :] = halo[
                    pl.ds(spare, 1), :
                ]
                spare += 1

    for begin in range(0, total_rows, 8):
        at = pl.ds(begin, min(8, total_rows - begin))
        code = cells[CODE, at, :]
        fraction = cells[FRAC, at, :]
        face = (code == FACE) | (code == FILLING)
        u = jnp.where(code == LIQUID, 1.0, jnp.where(face, 0.5 * fraction, 0.0))
        v = jnp.where(face, 0.5, 0.0)
        free = jnp.where(code == FACE, 1.0, 0.0)
        for depth in (-1, 0, 1):
            for k, value in enumerate((code, u, v)):
                near[k * 3 + depth + 1, at, :] = roll(value, depth) if depth else value
        ends = roll(free, 1) + roll(free, -1)
        near[9, at, :] = free
        near[10, at, :] = ends
        near[11, at, :] = free + ends

    def moments(tiles):
        density = tiles[0]
        for t in tiles[1:]:
            density = density + t
        flux = []
        for axis in range(3):
            plus = [tiles[q] for q in heading(axis, 1)]
            minus = [tiles[q] for q in heading(axis, -1)]
            j = plus[0] - minus[0]
            for a, b in zip(plus[1:], minus[1:]):
                j = j + (a - b)
            flux.append(j)
        inverse = 1.0 / density
        return density, [j * inverse for j in flux]

    def projection(velocity, q):
        terms = [
            velocity[axis] if VELOCITIES[q][axis] > 0 else -velocity[axis]
            for axis in range(3)
            if VELOCITIES[q][axis]
        ]
        out = terms[0]
        for t in terms[1:]:
            out = out + t
        return out

    updates, portions = [], []
    for c in range(-1, cols + 1):
        base = (c + 2) * high_rows + 1
        inside = 0 <= c < cols

        def source(array, q, cells=cells, base=base):
            begin = base - int(VELOCITIES[q][1]) * high_rows - int(VELOCITIES[q][0])
            return array[pl.ds(begin, tall), :]

        own = [cells[q, pl.ds(base, tall), :] for q in range(LANES)]
        mass = cells[MASS, pl.ds(base, tall), :]
        fraction = cells[FRAC, pl.ds(base, tall), :]
        code = cells[CODE, pl.ds(base, tall), :]
        bubble = cells[BUB, pl.ds(base, tall), :].astype(jnp.int32)
        gas = None
        for chunk in range(chunks):
            index = bubble - chunk * 128
            valid = (index >= 0) & (index < 128)
            found = jnp.take_along_axis(
                table[chunk, pl.ds(0, tall), :], jnp.where(valid, index, 0), axis=1
            )
            gas = found if gas is None else jnp.where(valid, found, gas)
        _, velocity = moments(own)
        still = 1.0 - 1.5 * (
            velocity[0] * velocity[0] + velocity[1] * velocity[1] + velocity[2] * velocity[2]
        )
        flow = None
        passed = [own[0]] + [None] * (LANES - 1)
        for first in range(1, LANES, 2):
            project = projection(velocity, first)
            pressed = gas * (2.0 * WEIGHTS[first]) * (still + 4.5 * project * project)
            for q in (first, first + 1):
                depth = int(VELOCITIES[q][2])
                moved = source(cells.at[q], q)
                if depth:
                    moved = roll(moved, depth)
                bounced = own[OPPOSITE[q]]
                kind = source(near.at[depth + 1], q)
                weight = source(near.at[3 + depth + 1], q) + source(near.at[6 + depth + 1], q) * fraction
                term = weight * (moved - bounced)
                flow = term if flow is None else flow + term
                passed[q] = jnp.where(
                    kind == GAS, pressed - bounced, jnp.where(kind == WALL, bounced, moved)
                )
        targets = near[10, pl.ds(base, tall), :]
        for dr in (-1, 0, 1):
            for dc in (-1, 0, 1):
                if dr or dc:
                    plane = 9 if dr and dc else 11
                    targets = targets + near[plane, pl.ds(base + dc * high_rows + dr, tall), :]
        filling = code == FILLING
        if inside:
            density, moved_velocity = moments(passed)
        else:
            density = passed[0]
            for t in passed[1:]:
                density = density + t
        taken = mass + flow
        portion = jnp.where(filling, (taken - density) / jnp.maximum(targets, 1.0), 0.0)
        portions.append(portion)
        if inside:
            updates.append(
                jnp.where(
                    code == FACE,
                    taken,
                    jnp.where((code == LIQUID) | filling, density, mass),
                )
            )
            dry = code == GAS
            still = 1.0 - 1.5 * (
                moved_velocity[0] * moved_velocity[0]
                + moved_velocity[1] * moved_velocity[1]
                + moved_velocity[2] * moved_velocity[2]
            )
            scaled = RELAX * density

            def put(q, value, own=own, c=c, dry=dry):
                relaxed_stage[pl.ds(q * tall * cols + c, tall, stride=cols), :] = jnp.where(
                    dry, own[q], value
                )

            put(0, (1.0 - RELAX) * passed[0] + (scaled * WEIGHTS[0]) * still)
            for first in range(1, LANES, 2):
                project = projection(moved_velocity, first)
                even = still + 4.5 * project * project
                odd = 3.0 * project
                share = scaled * WEIGHTS[first]
                put(first, (1.0 - RELAX) * passed[first] + share * (even + odd))
                put(first + 1, (1.0 - RELAX) * passed[first + 1] + share * (even - odd))

    relaxed_copies = [
        pltpu.make_async_copy(
            relaxed_stage.at[pl.ds((q * tall + 1) * cols, block), :],
            relaxed_out.at[pl.ds(q * block, block), :],
            wet_sem.at[q],
        )
        for q in range(LANES)
    ]
    for copy in relaxed_copies:
        copy.start()

    ends = [roll(p, 1) + roll(p, -1) for p in portions]
    full = [p + e for p, e in zip(portions, ends)]
    for c in range(cols):
        beside = ends[c + 1] + full[c] + full[c + 2]
        stacked = full[c + 1] + portions[c] + portions[c + 2]
        sums[pl.ds(8, tall), :] = stacked
        gained = beside + sums[pl.ds(7, tall), :] + sums[pl.ds(9, tall), :]
        code = cells[CODE, pl.ds((c + 2) * high_rows + 1, tall), :]
        mass_stage[pl.ds(c, tall, stride=cols), :] = jnp.where(
            code == FACE, updates[c] + gained, updates[c]
        )
    mass_copy = pltpu.make_async_copy(
        mass_stage.at[pl.ds(cols, block), :], new_mass_out, mass_sem
    )
    mass_copy.start()
    for copy in relaxed_copies:
        copy.wait()
    mass_copy.wait()


def shards(gx_size, gy_size, populations, cell_mass, cell_flags, bubble, conversion, rest_volume):
    rows, cols, depth = populations.shape[1:]
    labels = rest_volume.shape[0]
    block = rows * cols
    tall = rows + 2
    devices = gx_size * gy_size
    chunks = -(-labels // 128)
    direct = devices * chunks <= 64
    copies = devices if direct else 1
    f32 = jnp.float32
    vmem = pl.BlockSpec(memory_space=pltpu.VMEM)

    pops = populations.reshape(LANES * block, depth)
    flat = [a.reshape(block, depth) for a in (cell_mass, cell_flags, bubble, conversion)]
    end_rows = (CHANNELS + 7) * cols
    side_rows = side_tiles(rows)

    aux, low, high, left, right, tally = pl.pallas_call(
        functools.partial(first_kernel, rows, cols, chunks, copies),
        out_shape=[
            jax.ShapeDtypeStruct((4 * block, depth), f32),
            jax.ShapeDtypeStruct((end_rows, depth), f32),
            jax.ShapeDtypeStruct((end_rows, depth), f32),
            jax.ShapeDtypeStruct((side_rows, depth), f32),
            jax.ShapeDtypeStruct((side_rows, depth), f32),
            jax.ShapeDtypeStruct((copies, chunks, 8, 128), f32),
        ],
        in_specs=[vmem] * 5,
        out_specs=[vmem] * 6,
        cost_estimate=pl.CostEstimate(flops=2000000, bytes_accessed=2000000, transcendentals=0),
        name="pack",
    )(pops, *flat)

    def shifted(x, axis, size, up):
        pairs = [(i, i + 1) if up else (i + 1, i) for i in range(size - 1)]
        return lax.ppermute(x, axis, pairs)

    from_below = shifted(high, "gx", gx_size, True)
    from_above = shifted(low, "gx", gx_size, False)
    if direct:
        tallies = lax.all_to_all(
            tally.reshape(devices, chunks * 8, 128), ("gx", "gy"), 0, 0
        ).reshape(devices, chunks, 8, 128)
    else:
        tallies = lax.psum(tally[0, :, 0], ("gx", "gy"))
        tallies = jnp.broadcast_to(tallies[None, :, None, :], (1, chunks, 8, 128))

    left, right = pl.pallas_call(
        functools.partial(second_kernel, rows, cols),
        out_shape=[jax.ShapeDtypeStruct((side_rows, depth), f32)] * 2,
        in_specs=[vmem] * 4,
        out_specs=[vmem] * 2,
        name="relay",
    )(from_below, from_above, left, right)
    from_left = shifted(right, "gy", gy_size, True)
    from_right = shifted(left, "gy", gy_size, False)

    relaxed, new_mass, gas = pl.pallas_call(
        functools.partial(third_kernel, rows, cols, chunks, copies, labels),
        out_shape=[
            jax.ShapeDtypeStruct((LANES * block, depth), f32),
            jax.ShapeDtypeStruct((block, depth), f32),
            jax.ShapeDtypeStruct((1, labels), f32),
        ],
        in_specs=[vmem] * 8,
        out_specs=[
            pl.BlockSpec(memory_space=pl.ANY),
            pl.BlockSpec(memory_space=pl.ANY),
            vmem,
        ],
        scratch_shapes=[
            pltpu.VMEM((CHANNELS, (cols + 4) * (rows + 4), depth), f32),
            pltpu.VMEM((12, (cols + 4) * (rows + 4), depth), f32),
            pltpu.VMEM((24, depth), f32),
            pltpu.VMEM((chunks, 8, 128), f32),
            pltpu.VMEM((LANES * tall * cols, depth), f32),
            pltpu.VMEM((tall * cols, depth), f32),
            pltpu.SemaphoreType.DMA((LANES,)),
            pltpu.SemaphoreType.DMA,
        ],
        cost_estimate=pl.CostEstimate(flops=5000000, bytes_accessed=3000000, transcendentals=0),
        name="settle",
    )(pops, aux, from_below, from_above, from_left, from_right, tallies, rest_volume.reshape(1, labels))
    return (
        relaxed.reshape(LANES, rows, cols, depth),
        new_mass.reshape(rows, cols, depth),
        gas.reshape(labels),
    )


def solution(mesh):
    placed = (
        P(None, "gx", "gy", None),
        P("gx", "gy", None),
        P("gx", "gy", None),
        P("gx", "gy", None),
        P("gx", "gy", None),
        P(),
    )
    return jax.shard_map(
        functools.partial(shards, mesh.shape["gx"], mesh.shape["gy"]),
        mesh=mesh,
        in_specs=placed,
        out_specs=(P(None, "gx", "gy", None), P("gx", "gy", None), P()),
        check_vma=False,
    )
```

time: 114 us -> 33.3 us (0.29)
  blocking collectives: 41.1 us -> 0 us
  local copies, waits for them, and re-layouts: 19.9 us -> 1.32 us
  other arithmetic: 13 us -> 0 us
  Pallas kernels: 0 us -> 8.01 us
  matrix products: 7.83 us -> 0 us
  starting transfers between devices: 21.8 us -> 18.4 us
  waiting for transfers between devices: 6.69 us -> 4.61 us
  between operations: 1.85 us -> 0.71 us
    psum x1 -> x0, blocking collectives: 41.1 us -> none  [total_volume(): return lax.psum(partial_volume, ('gx', 'gy'))]
    ppermute x8 -> x4, starting transfers between devices: 21.8 us -> 10.7 us  [shifted(): return lax.ppermute(x, axis, pairs)]
    unnamed x150 -> x10, local copies, waits for them, and re-layouts: 10.6 us -> 1.32 us
    pallas_call x0 -> x3, Pallas kernels: none -> 8.01 us  [the longest x1 3.71 us: shards(): pl.pallas_call(functools.partial(third_kernel, rows, cols, chunks, copies...]
    dot_general x16 -> x0, matrix products: 7.83 us -> none  [the longest x6 2.66 us: lookup(): jnp.dot(indicator, gas_density, precision=lax.Precision.HIGHEST, preferre...]
    all_to_all x0 -> x1, starting transfers between devices: none -> 7.7 us  [shards(): lax.all_to_all(tally.reshape(devices, chunks * 8, 128), ('gx', 'gy'), 0, 0)]
    select_n x6 -> x0, other arithmetic: 5.36 us -> none  [the longest x4 2.9 us: pull_cells(): pulled.append(jnp.where(in_domain, source, bounced))]
    slice x23 -> x0, local copies, waits for them, and re-layouts: 4.26 us -> none  [the longest x20 4.09 us: window(): jnp.roll(layer[begin_rows:begin_rows + extent_rows, begin_cols:begin_cols...]
  transfers between devices with their start and end apart: 8 -> 5, of which waited for: 2 -> 3; matrix products, arithmetic and copies ran while one was open for 11% -> 0% of each run, Pallas kernels for 0% -> 6%
where the time goes in v1:
time: 33.3 us; the launch traced here: 33 us
  starting transfers between devices  18.4 us (55%)
  Pallas kernels  8.01 us (24%)
  waiting for transfers between devices  4.61 us (14%)
  local copies, waits for them, and re-layouts  1.32 us (4%)
  between operations  0.71 us (2%)
    ppermute x4, starting transfers between devices, shifted(): return lax.ppermute(x, axis, pairs)  10.7 us
    all_to_all x1, starting transfers between devices, shards(): lax.all_to_all(tally.reshape(devices, chunks * 8, 128), ('gx', 'gy'), 0, 0)  7.7 us
    ppermute x4, waiting for transfers between devices, shifted(): return lax.ppermute(x, axis, pairs)  4.46 us
    pallas_call x1, Pallas kernels, shards(): pl.pallas_call(functools.partial(third_kernel, rows, cols, chunks, copies...  3.71 us
    pallas_call x1, Pallas kernels, shards(): pl.pallas_call(functools.partial(first_kernel, rows, cols, chunks, copies...  2.45 us
    pallas_call x1, Pallas kernels, shards(): pl.pallas_call(functools.partial(second_kernel, rows, cols), out_shape=[j...  1.84 us
    unnamed x10, local copies, waits for them, and re-layouts  1.32 us
  transfers between devices with their start and end apart: 5, of which 3 were waited for; matrix products, arithmetic and copies ran while one was open for 0% of the time, Pallas kernels for 6%

profile of v1, /device:TPU:1, one launch (start us, length us, event | category | flops | bytes accessed | tf_op | source)
XLA Modules:
  0.0 33.0 jit_solution(18420238591716041645)
XLA Ops:
  0.6 2.5 %pack.1 = (f32[192,128]{1,0:T(8,128)}, f32[240,128]{1,0:T(8,128)}, f32[240,128]{1,0:T(8,128)}, f32[264,128]{1,0:T(8,128)}, f32[264,128]{1,0:T(8,128)}, /*index=5*/f32[32,1,8,128]{3,2,1,0:T(8,128)}) custom-call(f32[912,128]{1,0:T(8,128)} %bitcast.11, f32[48,128]{1,0:T(8,128)} %bitcast.15, s32[48,128]{1,0:T(8,128)} %bitcast.16, s32[48,128]{1,0:T(8,128)} %bitcast.17, ...), custom_call_target="tpu_custom_call" | custom-call | flops 2000000 | bytes 2000000 | tf_op jit(solution)/shard_map/pack/pallas_call | solution.py:411
  3.1 3.9 %collective-permute-start = (f32[240,128]{1,0:T(8,128)}, f32[240,128]{1,0:T(8,128)S(1)}, u32[]{:S(2)}, u32[]{:S(2)}) collective-permute-start(f32[240,128]{1,0:T(8,128)} %get-tuple-element.15), channel_id=1, source_target_pairs={{0,4},{4,8},{8,12},{12,16},{16,20},{20,24},{24,28},{1,5},{5,9},{9,... | collective-permute-start | bytes 368648 | tf_op jit(solution)/shard_map/ppermute | solution.py:429
  7.0 1.3 %collective-permute-start.1 = (f32[240,128]{1,0:T(8,128)}, f32[240,128]{1,0:T(8,128)S(1)}, u32[]{:S(2)}, u32[]{:S(2)}) collective-permute-start(f32[240,128]{1,0:T(8,128)} %get-tuple-element.16), channel_id=1, source_target_pairs={{4,0},{8,4},{12,8},{16,12},{20,16},{24,20},{28,24},{5,1},{9,5},{13... | collective-permute-start | bytes 368648 | tf_op jit(solution)/shard_map/ppermute | solution.py:429
  8.3 7.7 %all-to-all-start = ((f32[32,8,128]{2,1,0:T(8,128)}), f32[32,8,128]{2,1,0:T(8,128)S(1)}, u32[]{:S(2)}, u32[]{:S(2)}) async-start(f32[32,8,128]{2,1,0:T(8,128)} %bitcast.14), calls=%async_computation | async-start | bytes 262144 | tf_op jit(solution)/shard_map/all_to_all | solution.py:434
  16.0 0.0 collective-permute-done.low
  16.0 0.0 copy-start.1
  16.0 0.0 collective-permute-done.1.high
  16.1 0.0 copy-start.2
  16.1 0.6 %copy-done.1 = f32[240,128]{1,0:T(8,128)} copy-done((f32[240,128]{1,0:T(8,128)}, f32[240,128]{1,0:T(8,128)S(1)}, u32[]{:S(2)}) %copy-start.1) | copy-done | bytes 122904
  16.7 0.0 copy-done.2
  16.7 1.8 %relay.1 = (f32[264,128]{1,0:T(8,128)}, f32[264,128]{1,0:T(8,128)}) custom-call(f32[240,128]{1,0:T(8,128)} %copy-done.1, f32[240,128]{1,0:T(8,128)} %copy-done.2, f32[264,128]{1,0:T(8,128)} %get-tuple-element.17.left, f32[264,128]{1,0:T(8,128)} %get-tuple-element.18.right), custom_call_target="tpu_custom_call" | custom-call | tf_op jit(solution)/shard_map/relay/pallas_call | solution.py:441
  18.6 3.5 %collective-permute-start.2 = (f32[264,128]{1,0:T(8,128)}, f32[264,128]{1,0:T(8,128)S(1)}, u32[]{:S(2)}, u32[]{:S(2)}) collective-permute-start(f32[264,128]{1,0:T(8,128)} %get-tuple-element.19), channel_id=1, source_target_pairs={{0,1},{1,2},{2,3},{4,5},{5,6},{6,7},{8,9},{9,10},{10,11},{12,13},{... | collective-permute-start | bytes 405512 | tf_op jit(solution)/shard_map/ppermute | solution.py:429
  22.1 1.9 %collective-permute-start.3 = (f32[264,128]{1,0:T(8,128)}, f32[264,128]{1,0:T(8,128)S(1)}, u32[]{:S(2)}, u32[]{:S(2)}) collective-permute-start(f32[264,128]{1,0:T(8,128)} %get-tuple-element.20), channel_id=1, source_target_pairs={{1,0},{2,1},{3,2},{5,4},{6,5},{7,6},{9,8},{10,9},{11,10},{13,12},{... | collective-permute-start | bytes 405512 | tf_op jit(solution)/shard_map/ppermute | solution.py:429
  24.0 0.2 all-to-all-done
  24.2 0.0 copy-start
  24.2 0.2 collective-permute-done.2.left
  24.4 0.0 copy-start.3
  24.4 4.3 %collective-permute-done.3.right = f32[264,128]{1,0:T(8,128)S(1)} collective-permute-done((f32[264,128]{1,0:T(8,128)}, f32[264,128]{1,0:T(8,128)S(1)}, u32[]{:S(2)}, u32[]{:S(2)}) %collective-permute-start.3) | collective-permute-done | bytes 135200 | tf_op jit(solution)/shard_map/ppermute | solution.py:429
  28.7 0.0 copy-start.4
  28.7 0.0 copy-done
  28.7 0.0 copy-done.3
  28.7 0.6 %copy-done.4 = f32[264,128]{1,0:T(8,128)} copy-done((f32[264,128]{1,0:T(8,128)}, f32[264,128]{1,0:T(8,128)S(1)}, u32[]{:S(2)}) %copy-start.4) | copy-done | bytes 135192
  29.3 3.7 %settle.1 = (f32[912,128]{1,0:T(8,128)}, f32[48,128]{1,0:T(8,128)}, f32[1,96]{1,0:T(1,128)}) custom-call(f32[912,128]{1,0:T(8,128)} %bitcast.12, f32[192,128]{1,0:T(8,128)} %get-tuple-element.14.aux, f32[240,128]{1,0:T(8,128)} %copy-done.1, f32[240,128]{1,0:T(8,128)} %copy-done.2, f32[264,128]{1,0:T(8,128)} %copy-done.3, f32[264,128]{1,0:T(8,128)} %copy-done.4, ...), custom_call_target="tpu_custom_call" | custom-call | flops 5000000 | bytes 3000000 | tf_op jit(solution)/shard_map/settle/pallas_call | solution.py:451
Async XLA Ops:
  3.1 12.9 %collective-permute-start = (f32[240,128]{1,0:T(8,128)}, f32[240,128]{1,0:T(8,128)S(1)}, u32[]{:S(2)}, u32[]{:S(2)}) collective-permute-start(f32[240,128]{1,0:T(8,128)} %get-tuple-element.15), channel_id=1, source_target_pairs={{0,4},{4,8},{8,12},{12,16},{16,20},{20,24},{24,28},{1,5},{5,9},{9,... | collective-permute-start | bytes 368648 | tf_op jit(solution)/shard_map/ppermute | solution.py:429
  7.0 9.0 %collective-permute-start.1 = (f32[240,128]{1,0:T(8,128)}, f32[240,128]{1,0:T(8,128)S(1)}, u32[]{:S(2)}, u32[]{:S(2)}) collective-permute-start(f32[240,128]{1,0:T(8,128)} %get-tuple-element.16), channel_id=1, source_target_pairs={{4,0},{8,4},{12,8},{16,12},{20,16},{24,20},{28,24},{5,1},{9,5},{13... | collective-permute-start | bytes 368648 | tf_op jit(solution)/shard_map/ppermute | solution.py:429
  8.3 15.9 %all-to-all-start = ((f32[32,8,128]{2,1,0:T(8,128)}), f32[32,8,128]{2,1,0:T(8,128)S(1)}, u32[]{:S(2)}, u32[]{:S(2)}) async-start(f32[32,8,128]{2,1,0:T(8,128)} %bitcast.14), calls=%async_computation | async-start | bytes 262144 | tf_op jit(solution)/shard_map/all_to_all | solution.py:434
  16.0 0.7 %copy-start.1 = (f32[240,128]{1,0:T(8,128)}, f32[240,128]{1,0:T(8,128)S(1)}, u32[]{:S(2)}) copy-start(f32[240,128]{1,0:T(8,128)S(1)} %collective-permute-done.low) | copy-start | bytes 368644
  16.1 0.7 %copy-start.2 = (f32[240,128]{1,0:T(8,128)}, f32[240,128]{1,0:T(8,128)S(1)}, u32[]{:S(2)}) copy-start(f32[240,128]{1,0:T(8,128)S(1)} %collective-permute-done.1.high) | copy-start | bytes 368644
  18.6 5.8 %collective-permute-start.2 = (f32[264,128]{1,0:T(8,128)}, f32[264,128]{1,0:T(8,128)S(1)}, u32[]{:S(2)}, u32[]{:S(2)}) collective-permute-start(f32[264,128]{1,0:T(8,128)} %get-tuple-element.19), channel_id=1, source_target_pairs={{0,1},{1,2},{2,3},{4,5},{5,6},{6,7},{8,9},{9,10},{10,11},{12,13},{... | collective-permute-start | bytes 405512 | tf_op jit(solution)/shard_map/ppermute | solution.py:429
  22.1 6.5 %collective-permute-start.3 = (f32[264,128]{1,0:T(8,128)}, f32[264,128]{1,0:T(8,128)S(1)}, u32[]{:S(2)}, u32[]{:S(2)}) collective-permute-start(f32[264,128]{1,0:T(8,128)} %get-tuple-element.20), channel_id=1, source_target_pairs={{1,0},{2,1},{3,2},{5,4},{6,5},{7,6},{9,8},{10,9},{11,10},{13,12},{... | collective-permute-start | bytes 405512 | tf_op jit(solution)/shard_map/ppermute | solution.py:429
  24.2 4.5 %copy-start = (f32[32,8,128]{2,1,0:T(8,128)}, f32[32,8,128]{2,1,0:T(8,128)S(1)}, u32[]{:S(2)}) copy-start(f32[32,8,128]{2,1,0:T(8,128)S(1)} %all-to-all-done) | copy-start | bytes 393220
  24.4 4.3 %copy-start.3 = (f32[264,128]{1,0:T(8,128)}, f32[264,128]{1,0:T(8,128)S(1)}, u32[]{:S(2)}) copy-start(f32[264,128]{1,0:T(8,128)S(1)} %collective-permute-done.2.left) | copy-start | bytes 405508
  28.7 0.7 %copy-start.4 = (f32[264,128]{1,0:T(8,128)}, f32[264,128]{1,0:T(8,128)S(1)}, u32[]{:S(2)}) copy-start(f32[264,128]{1,0:T(8,128)S(1)} %collective-permute-done.3.right) | copy-start | bytes 405508

commit v2 on v1

--- a/solution.py
+++ b/solution.py
@@ -57,12 +57,54 @@
     return pltpu.roll(x, shift % x.shape[-1], x.ndim - 1)
 
 
+def by_parity(axis, use, even, odd):
+    odd_device = lax.rem(lax.axis_index(axis), 2) == 1
+
+    @pl.when(odd_device)
+    def _():
+        use(even, odd)
+
+    @pl.when(jnp.logical_not(odd_device))
+    def _():
+        use(odd, even)
+
+
+def paired(size, odd):
+    pairs = []
+    for i in range(1 if odd else 0, size - 1, 2):
+        pairs += [(i, i + 1), (i + 1, i)]
+    return pairs
+
+
 def first_kernel(
     rows, cols, chunks, copies,
-    pops, mass, flags, bubble, conversion,
-    aux, low, high, left, right, tally,
+    pops_in, mass_in, flags_in, bubble_in, conversion_in, rest,
+    aux, across_even, across_odd, beside_even, beside_odd, rest_table, tally,
+    pops, mass, flags, bubble, conversion, sems,
 ):
     block = rows * cols
+    copies_in = [
+        pltpu.make_async_copy(a, b, sems.at[k])
+        for k, (a, b) in enumerate(
+            (
+                (pops_in, pops),
+                (mass_in, mass),
+                (flags_in, flags),
+                (bubble_in, bubble),
+                (conversion_in, conversion),
+            )
+        )
+    ]
+    for copy in copies_in:
+        copy.start()
+    labels_all = rest.shape[-1]
+    for chunk in range(chunks):
+        here = min(128, labels_all - chunk * 128)
+        rest_table[chunk, :, pl.ds(0, here)] = jnp.broadcast_to(
+            rest[0:1, pl.ds(chunk * 128, here)], (8, here)
+        )
+    for copy in copies_in:
+        copy.wait()
     masses, fractions, codes = [], [], []
     contributions = []
     for r in range(rows):
@@ -92,19 +134,31 @@
         ref, base = (pops, channel) if channel < LANES else (aux, channel - LANES)
         return ref[pl.ds(base * block + c, rows, stride=cols), :]
 
-    for out, inner_row, outer_row, sign in ((low, 0, 1, -1), (high, rows - 1, rows - 2, 1)):
+    tall = rows + 2
+
+    def send_rows(out, inner_row, outer_row, sign):
         for channel in range(CHANNELS):
             out[pl.ds(channel * cols, cols), :] = tile(channel, inner_row)
         for k, channel in enumerate(outer(0, sign)):
             out[pl.ds((CHANNELS + k) * cols, cols), :] = tile(channel, outer_row)
-    tall = rows + 2
-    for out, inner_col, outer_col, sign in ((left, 0, 1, -1), (right, cols - 1, cols - 2, 1)):
+
+    def send_cols(out, inner_col, outer_col, sign):
         for channel in range(CHANNELS):
             out[pl.ds(channel * tall + 1, rows), :] = column(channel, inner_col)
         for k, channel in enumerate(outer(1, sign)):
             out[pl.ds((CHANNELS + k) * tall + 1, rows), :] = column(channel, outer_col)
 
-    ones = jnp.ones((8, 128), jnp.float32)
+    def low_high(low, high):
+        send_rows(low, 0, 1, -1)
+        send_rows(high, rows - 1, rows - 2, 1)
+
+    def left_right(left, right):
+        send_cols(left, 0, 1, -1)
+        send_cols(right, cols - 1, cols - 2, 1)
+
+    by_parity("gx", low_high, across_even, across_odd)
+    by_parity("gy", left_right, beside_even, beside_odd)
+
     lane_count = mass.shape[-1]
 
     def count(chunk):
@@ -123,14 +177,23 @@
             preferred_element_type=jnp.float32,
         )
 
-    del ones
     for chunk in range(chunks):
         summed = count(chunk)
         for k in range(copies):
             tally[k, chunk] = summed
 
 
-def second_kernel(rows, cols, low, high, left, right, left_out, right_out):
+def second_kernel(rows, cols, across_even, across_odd, beside_even, beside_odd, even_out, odd_out):
+    def with_rows(low, high):
+        def with_cols(left_pair, right_pair):
+            relay(rows, cols, low, high, *left_pair, *right_pair)
+
+        by_parity("gy", with_cols, (beside_even, even_out), (beside_odd, odd_out))
+
+    by_parity("gx", with_rows, across_even, across_odd)
+
+
+def relay(rows, cols, low, high, left, left_out, right, right_out):
     tall = rows + 2
     for part, out, inner_col, outer_col, sign in (
         (left, left_out, 0, 1, -1),
@@ -166,7 +229,7 @@
 
 def third_kernel(
     rows, cols, chunks, copies, labels,
-    pops, aux, low, high, left, right, tally, rest,
+    pops, aux, across_even, across_odd, beside_even, beside_odd, tally, rest,
     relaxed_out, new_mass_out, gas_out,
     cells, near, sums, table, relaxed_stage, mass_stage, wet_sem, mass_sem,
 ):
@@ -181,9 +244,9 @@
         for k in range(1, copies):
             volume = volume + tally[k, chunk]
         here = min(128, labels - chunk * 128)
-        gas = AMBIENT + rest[0:1, pl.ds(chunk * 128, here)] / jnp.maximum(volume[0:1, :here], 1.0)
-        gas_out[0:1, pl.ds(chunk * 128, here)] = gas
-        table[chunk, :, pl.ds(0, here)] = jnp.broadcast_to(gas, (8, here))
+        gas = AMBIENT + rest[chunk] / jnp.maximum(volume, 1.0)
+        gas_out[0:1, pl.ds(chunk * 128, here)] = gas[0:1, :here]
+        table[chunk] = gas
 
     for channel in range(CHANNELS):
         ref, base = (pops, channel) if channel < LANES else (aux, channel - LANES)
@@ -191,42 +254,48 @@
             cells[channel, pl.ds((c + 2) * high_rows + 2, rows), :] = ref[
                 pl.ds(base * block + c, rows, stride=cols), :
             ]
-    for halo, inner_row, outer_row, towards in (
-        (low, 1, 0, 1),
-        (high, high_rows - 2, high_rows - 1, -1),
-    ):
-        for channel in range(CHANNELS):
-            cells[channel, pl.ds(2 * high_rows + inner_row, cols, stride=high_rows), :] = halo[
-                pl.ds(channel * cols, cols), :
-            ]
-        for k, channel in enumerate(outer(0, towards)):
-            cells[channel, pl.ds(2 * high_rows + outer_row, cols, stride=high_rows), :] = halo[
-                pl.ds((CHANNELS + k) * cols, cols), :
-            ]
-    for halo, inner_col, outer_col, sign in (
-        (left, 1, 0, 1),
-        (right, wide - 2, wide - 1, -1),
-    ):
-        for channel in range(CHANNELS):
-            cells[channel, pl.ds(inner_col * high_rows + 1, tall), :] = halo[
-                pl.ds(channel * tall, tall), :
-            ]
-        for k, channel in enumerate(outer(1, sign)):
-            cells[channel, pl.ds(outer_col * high_rows + 1, tall), :] = halo[
-                pl.ds((CHANNELS + k) * tall, tall), :
-            ]
-        spare = (CHANNELS + 7) * tall
-        for row, towards in ((0, 1), (high_rows - 1, -1)):
-            for channel in outer(0, towards):
-                cells[channel, pl.ds(inner_col * high_rows + row, 1), :] = halo[
-                    pl.ds(spare, 1), :
+    def fill_rows(low, high):
+        for halo, inner_row, outer_row, towards in (
+            (low, 1, 0, 1),
+            (high, high_rows - 2, high_rows - 1, -1),
+        ):
+            for channel in range(CHANNELS):
+                cells[channel, pl.ds(2 * high_rows + inner_row, cols, stride=high_rows), :] = halo[
+                    pl.ds(channel * cols, cols), :
                 ]
-                spare += 1
-            for channel in (heading_both(towards, sign), FRAC, CODE):
-                cells[channel, pl.ds(outer_col * high_rows + row, 1), :] = halo[
-                    pl.ds(spare, 1), :
+            for k, channel in enumerate(outer(0, towards)):
+                cells[channel, pl.ds(2 * high_rows + outer_row, cols, stride=high_rows), :] = halo[
+                    pl.ds((CHANNELS + k) * cols, cols), :
                 ]
-                spare += 1
+
+    def fill_cols(left, right):
+        for halo, inner_col, outer_col, sign in (
+            (left, 1, 0, 1),
+            (right, wide - 2, wide - 1, -1),
+        ):
+            for channel in range(CHANNELS):
+                cells[channel, pl.ds(inner_col * high_rows + 1, tall), :] = halo[
+                    pl.ds(channel * tall, tall), :
+                ]
+            for k, channel in enumerate(outer(1, sign)):
+                cells[channel, pl.ds(outer_col * high_rows + 1, tall), :] = halo[
+                    pl.ds((CHANNELS + k) * tall, tall), :
+                ]
+            spare = (CHANNELS + 7) * tall
+            for row, towards in ((0, 1), (high_rows - 1, -1)):
+                for channel in outer(0, towards):
+                    cells[channel, pl.ds(inner_col * high_rows + row, 1), :] = halo[
+                        pl.ds(spare, 1), :
+                    ]
+                    spare += 1
+                for channel in (heading_both(towards, sign), FRAC, CODE):
+                    cells[channel, pl.ds(outer_col * high_rows + row, 1), :] = halo[
+                        pl.ds(spare, 1), :
+                    ]
+                    spare += 1
+
+    by_parity("gx", fill_rows, across_even, across_odd)
+    by_parity("gy", fill_cols, beside_even, beside_odd)
 
     for begin in range(0, total_rows, 8):
         at = pl.ds(begin, min(8, total_rows - begin))
@@ -402,13 +471,14 @@
     copies = devices if direct else 1
     f32 = jnp.float32
     vmem = pl.BlockSpec(memory_space=pltpu.VMEM)
+    hbm = pl.BlockSpec(memory_space=pltpu.HBM)
 
     pops = populations.reshape(LANES * block, depth)
     flat = [a.reshape(block, depth) for a in (cell_mass, cell_flags, bubble, conversion)]
     end_rows = (CHANNELS + 7) * cols
     side_rows = side_tiles(rows)
 
-    aux, low, high, left, right, tally = pl.pallas_call(
+    aux, across_even, across_odd, beside_even, beside_odd, rest, tally = pl.pallas_call(
         functools.partial(first_kernel, rows, cols, chunks, copies),
         out_shape=[
             jax.ShapeDtypeStruct((4 * block, depth), f32),
@@ -416,20 +486,29 @@
             jax.ShapeDtypeStruct((end_rows, depth), f32),
             jax.ShapeDtypeStruct((side_rows, depth), f32),
             jax.ShapeDtypeStruct((side_rows, depth), f32),
+            jax.ShapeDtypeStruct((chunks, 8, 128), f32),
             jax.ShapeDtypeStruct((copies, chunks, 8, 128), f32),
         ],
-        in_specs=[vmem] * 5,
-        out_specs=[vmem] * 6,
+        in_specs=[hbm] * 5 + [vmem],
+        out_specs=[vmem] * 7,
+        scratch_shapes=[
+            pltpu.VMEM((LANES * block, depth), f32),
+            pltpu.VMEM((block, depth), f32),
+            pltpu.VMEM((block, depth), jnp.int32),
+            pltpu.VMEM((block, depth), jnp.int32),
+            pltpu.VMEM((block, depth), jnp.int32),
+            pltpu.SemaphoreType.DMA((5,)),
+        ],
         cost_estimate=pl.CostEstimate(flops=2000000, bytes_accessed=2000000, transcendentals=0),
+        compiler_params=pltpu.CompilerParams(vmem_limit_bytes=67043328),
         name="pack",
-    )(pops, *flat)
-
-    def shifted(x, axis, size, up):
-        pairs = [(i, i + 1) if up else (i + 1, i) for i in range(size - 1)]
-        return lax.ppermute(x, axis, pairs)
-
-    from_below = shifted(high, "gx", gx_size, True)
-    from_above = shifted(low, "gx", gx_size, False)
+    )(pops, *flat, rest_volume.reshape(1, labels))
+
+    def swapped(x, axis, size, odd):
+        return lax.ppermute(x, axis, paired(size, odd))
+
+    across_odd = swapped(across_odd, "gx", gx_size, True)
+    across_even = swapped(across_even, "gx", gx_size, False)
     if direct:
         tallies = lax.all_to_all(
             tally.reshape(devices, chunks * 8, 128), ("gx", "gy"), 0, 0
@@ -438,15 +517,16 @@
         tallies = lax.psum(tally[0, :, 0], ("gx", "gy"))
         tallies = jnp.broadcast_to(tallies[None, :, None, :], (1, chunks, 8, 128))
 
-    left, right = pl.pallas_call(
+    beside_even, beside_odd = pl.pallas_call(
         functools.partial(second_kernel, rows, cols),
         out_shape=[jax.ShapeDtypeStruct((side_rows, depth), f32)] * 2,
         in_specs=[vmem] * 4,
         out_specs=[vmem] * 2,
+        compiler_params=pltpu.CompilerParams(vmem_limit_bytes=4 << 20),
         name="relay",
-    )(from_below, from_above, left, right)
-    from_left = shifted(right, "gy", gy_size, True)
-    from_right = shifted(left, "gy", gy_size, False)
+    )(across_even, across_odd, beside_even, beside_odd)
+    beside_odd = swapped(beside_odd, "gy", gy_size, True)
+    beside_even = swapped(beside_even, "gy", gy_size, False)
 
     relaxed, new_mass, gas = pl.pallas_call(
         functools.partial(third_kernel, rows, cols, chunks, copies, labels),
@@ -472,8 +552,9 @@
             pltpu.SemaphoreType.DMA,
         ],
         cost_estimate=pl.CostEstimate(flops=5000000, bytes_accessed=3000000, transcendentals=0),
+        compiler_params=pltpu.CompilerParams(vmem_limit_bytes=12 << 20),
         name="settle",
-    )(pops, aux, from_below, from_above, from_left, from_right, tallies, rest_volume.reshape(1, labels))
+    )(pops, aux, across_even, across_odd, beside_even, beside_odd, tallies, rest)
     return (
         relaxed.reshape(LANES, rows, cols, depth),
         new_mass.reshape(rows, cols, depth),

time: 33.3 us -> 26.3 us (0.79)
  starting transfers between devices: 18.4 us -> 14.8 us
  Pallas kernels: 8.01 us -> 5.74 us
  waiting for transfers between devices: 4.61 us -> 3.01 us
  local copies, waits for them, and re-layouts: 1.32 us -> 1.82 us
    ppermute x4, starting transfers between devices: 10.7 us -> 6.45 us  [swapped(): return lax.ppermute(x, axis, paired(size, odd))]
    ppermute x4, waiting for transfers between devices: 4.46 us -> 0.47 us  [swapped(): return lax.ppermute(x, axis, paired(size, odd))]
    all_to_all x1, waiting for transfers between devices: 0.16 us -> 2.54 us  [shards(): lax.all_to_all(tally.reshape(devices, chunks * 8, 128), ('gx', 'gy'), 0, 0)]
    pallas_call x1, Pallas kernels: 1.84 us -> 0.05 us  [shards(): pl.pallas_call(functools.partial(second_kernel, rows, cols), out_shape=[j...]
    pallas_call x1, Pallas kernels: 3.71 us -> 2.55 us  [shards(): pl.pallas_call(functools.partial(third_kernel, rows, cols, chunks, copies...]
    pallas_call x1, Pallas kernels: 2.45 us -> 3.14 us  [shards(): pl.pallas_call(functools.partial(first_kernel, rows, cols, chunks, copies...]
    all_to_all x1, starting transfers between devices: 7.7 us -> 8.33 us  [shards(): lax.all_to_all(tally.reshape(devices, chunks * 8, 128), ('gx', 'gy'), 0, 0)]
    unnamed x10, local copies, waits for them, and re-layouts: 1.32 us -> 1.82 us
  transfers between devices with their start and end apart: 5 -> 5, of which waited for: 3 -> 2; matrix products, arithmetic and copies ran while one was open for 0% -> 0% of each run, Pallas kernels for 6% -> 0%
where the time goes in v2:
time: 26.3 us; the launch traced here: 26.1 us
  starting transfers between devices  14.8 us (56%)
  Pallas kernels  5.74 us (22%)
  waiting for transfers between devices  3.01 us (11%)
  local copies, waits for them, and re-layouts  1.82 us (7%)
  between operations  0.72 us (3%)
    all_to_all x1, starting transfers between devices, shards(): lax.all_to_all(tally.reshape(devices, chunks * 8, 128), ('gx', 'gy'), 0, 0)  8.33 us
    ppermute x4, starting transfers between devices, swapped(): return lax.ppermute(x, axis, paired(size, odd))  6.45 us
    pallas_call x1, Pallas kernels, shards(): pl.pallas_call(functools.partial(first_kernel, rows, cols, chunks, copies...  3.14 us
    pallas_call x1, Pallas kernels, shards(): pl.pallas_call(functools.partial(third_kernel, rows, cols, chunks, copies...  2.55 us
    all_to_all x1, waiting for transfers between devices, shards(): lax.all_to_all(tally.reshape(devices, chunks * 8, 128), ('gx', 'gy'), 0, 0)  2.54 us
    unnamed x10, local copies, waits for them, and re-layouts  1.82 us
  transfers between devices with their start and end apart: 5, of which 2 were waited for; matrix products, arithmetic and copies ran while one was open for 0% of the time, Pallas kernels for 0%

profile of v2, /device:TPU:1, one launch (start us, length us, event | category | flops | bytes accessed | tf_op | source)
XLA Modules:
  0.0 26.1 jit_solution(17547053978490289060)
XLA Ops:
  0.6 3.1 %pack.1 = (f32[192,128]{1,0:T(8,128)}, f32[240,128]{1,0:T(8,128)}, f32[240,128]{1,0:T(8,128)}, f32[264,128]{1,0:T(8,128)}, f32[264,128]{1,0:T(8,128)}, /*index=5*/f32[1,8,128]{2,1,0:T(8,128)}, f32[32,1,8,128]{3,2,1,0:T(8,128)}) custom-call(f32[912,128]{1,0:T(8,128)} %bitcast.11, f32[48,128]{1,0:T(8,128)} %bitcast.15, s32[48,128]{1,0:T(8,128)} %bitcast.16, ...), custom_call_target="tpu_custom_call" | custom-call | flops 2000000 | bytes 2000000 | tf_op jit(solution)/shard_map/pack/pallas_call | solution.py:481
  3.8 0.0 copy-start
  3.8 2.1 %collective-permute-start = (f32[240,128]{1,0:T(8,128)}, f32[240,128]{1,0:T(8,128)S(1)}, u32[]{:S(2)}, u32[]{:S(2)}) collective-permute-start(f32[240,128]{1,0:T(8,128)} %get-tuple-element.16), channel_id=1, source_target_pairs={{0,4},{4,0},{8,12},{12,8},{16,20},{20,16},{24,28},{28,24},{1,5},{5... | collective-permute-start | bytes 368648 | tf_op jit(solution)/shard_map/ppermute | solution.py:508
  5.9 0.7 %collective-permute-start.1 = (f32[240,128]{1,0:T(8,128)}, f32[240,128]{1,0:T(8,128)S(1)}, u32[]{:S(2)}, u32[]{:S(2)}) collective-permute-start(f32[240,128]{1,0:T(8,128)} %get-tuple-element.17), channel_id=1, source_target_pairs={{4,8},{8,4},{12,16},{16,12},{20,24},{24,20},{5,9},{9,5},{13,17},{1... | collective-permute-start | bytes 368648 | tf_op jit(solution)/shard_map/ppermute | solution.py:508
  6.5 8.3 %all-to-all-start = ((f32[32,8,128]{2,1,0:T(8,128)}), f32[32,8,128]{2,1,0:T(8,128)S(1)}, u32[]{:S(2)}, u32[]{:S(2)}) async-start(f32[32,8,128]{2,1,0:T(8,128)} %bitcast.14), calls=%async_computation | async-start | bytes 262144 | tf_op jit(solution)/shard_map/all_to_all | solution.py:513
  14.9 0.0 collective-permute-done.across_even
  14.9 0.0 collective-permute-done.1.across_odd
  14.9 0.0 copy-start.1
  14.9 0.9 %copy-done.1 = f32[264,128]{1,0:T(8,128)S(1)} copy-done((f32[264,128]{1,0:T(8,128)S(1)}, f32[264,128]{1,0:T(8,128)}, u32[]{:S(2)}) %copy-start.1) | copy-done | bytes 135192
  15.8 0.0 copy-start.2
  15.8 0.9 %copy-done.2 = f32[264,128]{1,0:T(8,128)S(1)} copy-done((f32[264,128]{1,0:T(8,128)S(1)}, f32[264,128]{1,0:T(8,128)}, u32[]{:S(2)}) %copy-start.2) | copy-done | bytes 135192
  16.7 0.0 copy-start.3
  16.7 0.1 relay.1
  16.8 0.0 copy-start.4
  16.8 0.3 %collective-permute-start.2 = (f32[264,128]{1,0:T(8,128)S(1)}, f32[264,128]{1,0:T(8,128)S(1)}, u32[]{:S(2)}, u32[]{:S(2)}) collective-permute-start(f32[264,128]{1,0:T(8,128)S(1)} %get-tuple-element.20), channel_id=1, source_target_pairs={{0,1},{1,0},{2,3},{3,2},{4,5},{5,4},{6,7},{7,6},{8,9},{9,8},{10,11... | collective-permute-start | bytes 405512 | tf_op jit(solution)/shard_map/ppermute | solution.py:508
  17.1 3.4 %collective-permute-start.3 = (f32[264,128]{1,0:T(8,128)S(1)}, f32[264,128]{1,0:T(8,128)S(1)}, u32[]{:S(2)}, u32[]{:S(2)}) collective-permute-start(f32[264,128]{1,0:T(8,128)S(1)} %get-tuple-element.21), channel_id=1, source_target_pairs={{1,2},{2,1},{5,6},{6,5},{9,10},{10,9},{13,14},{14,13},{17,18},{18,... | collective-permute-start | bytes 405512 | tf_op jit(solution)/shard_map/ppermute | solution.py:508
  20.5 2.5 %all-to-all-done = f32[32,8,128]{2,1,0:T(8,128)S(1)} async-done(((f32[32,8,128]{2,1,0:T(8,128)}), f32[32,8,128]{2,1,0:T(8,128)S(1)}, u32[]{:S(2)}, u32[]{:S(2)}) %all-to-all-start) | async-done | bytes 131104 | tf_op jit(solution)/shard_map/all_to_all | solution.py:513
  23.0 0.0 collective-permute-done.2.beside_even
  23.0 0.5 %collective-permute-done.3.beside_odd = f32[264,128]{1,0:T(8,128)S(1)} collective-permute-done((f32[264,128]{1,0:T(8,128)S(1)}, f32[264,128]{1,0:T(8,128)S(1)}, u32[]{:S(2)}, u32[]{:S(2)}) %collective-permute-start.3) | collective-permute-done | bytes 135200 | tf_op jit(solution)/shard_map/ppermute | solution.py:508
  23.5 0.0 copy-done
  23.5 0.0 copy-done.3
  23.5 0.0 copy-done.4
  23.5 2.5 %settle.1 = (f32[912,128]{1,0:T(8,128)}, f32[48,128]{1,0:T(8,128)}, f32[1,96]{1,0:T(1,128)}) custom-call(f32[912,128]{1,0:T(8,128)S(1)} %bitcast.12, f32[192,128]{1,0:T(8,128)S(1)} %copy-done.3, f32[240,128]{1,0:T(8,128)S(1)} %collective-permute-done.across_even, f32[240,128]{1,0:T(8,128)S(1)} %collective-permute-done.1.across_odd, ...), custom_call_target="tpu_custom_call" | custom-call | flops 5000000 | bytes 3000000 | tf_op jit(solution)/shard_map/settle/pallas_call | solution.py:531
Async XLA Ops:
  3.8 19.7 %copy-start = (f32[19,6,8,128]{3,2,1,0:T(8,128)S(1)}, f32[19,6,8,128]{3,2,1,0:T(8,128)}, u32[]{:S(2)}) copy-start(f32[19,6,8,128]{3,2,1,0:T(8,128)} %param.6) | copy-start | bytes 1400836
  3.8 11.1 %collective-permute-start = (f32[240,128]{1,0:T(8,128)}, f32[240,128]{1,0:T(8,128)S(1)}, u32[]{:S(2)}, u32[]{:S(2)}) collective-permute-start(f32[240,128]{1,0:T(8,128)} %get-tuple-element.16), channel_id=1, source_target_pairs={{0,4},{4,0},{8,12},{12,8},{16,20},{20,16},{24,28},{28,24},{1,5},{5... | collective-permute-start | bytes 368648 | tf_op jit(solution)/shard_map/ppermute | solution.py:508
  5.9 9.0 %collective-permute-start.1 = (f32[240,128]{1,0:T(8,128)}, f32[240,128]{1,0:T(8,128)S(1)}, u32[]{:S(2)}, u32[]{:S(2)}) collective-permute-start(f32[240,128]{1,0:T(8,128)} %get-tuple-element.17), channel_id=1, source_target_pairs={{4,8},{8,4},{12,16},{16,12},{20,24},{24,20},{5,9},{9,5},{13,17},{1... | collective-permute-start | bytes 368648 | tf_op jit(solution)/shard_map/ppermute | solution.py:508
  6.5 16.5 %all-to-all-start = ((f32[32,8,128]{2,1,0:T(8,128)}), f32[32,8,128]{2,1,0:T(8,128)S(1)}, u32[]{:S(2)}, u32[]{:S(2)}) async-start(f32[32,8,128]{2,1,0:T(8,128)} %bitcast.14), calls=%async_computation | async-start | bytes 262144 | tf_op jit(solution)/shard_map/all_to_all | solution.py:513
  14.9 0.9 %copy-start.1 = (f32[264,128]{1,0:T(8,128)S(1)}, f32[264,128]{1,0:T(8,128)}, u32[]{:S(2)}) copy-start(f32[264,128]{1,0:T(8,128)} %get-tuple-element.18.beside_even) | copy-start | bytes 405508
  15.8 0.9 %copy-start.2 = (f32[264,128]{1,0:T(8,128)S(1)}, f32[264,128]{1,0:T(8,128)}, u32[]{:S(2)}) copy-start(f32[264,128]{1,0:T(8,128)} %get-tuple-element.19.beside_odd) | copy-start | bytes 405508
  16.7 6.8 %copy-start.3 = (f32[192,128]{1,0:T(8,128)S(1)}, f32[192,128]{1,0:T(8,128)}, u32[]{:S(2)}) copy-start(f32[192,128]{1,0:T(8,128)} %get-tuple-element.15.aux) | copy-start | bytes 294916
  16.8 6.7 %copy-start.4 = (f32[1,8,128]{2,1,0:T(8,128)S(1)}, f32[1,8,128]{2,1,0:T(8,128)}, u32[]{:S(2)}) copy-start(f32[1,8,128]{2,1,0:T(8,128)} %get-tuple-element.23.rest) | copy-start | bytes 12292
  16.8 6.3 %collective-permute-start.2 = (f32[264,128]{1,0:T(8,128)S(1)}, f32[264,128]{1,0:T(8,128)S(1)}, u32[]{:S(2)}, u32[]{:S(2)}) collective-permute-start(f32[264,128]{1,0:T(8,128)S(1)} %get-tuple-element.20), channel_id=1, source_target_pairs={{0,1},{1,0},{2,3},{3,2},{4,5},{5,4},{6,7},{7,6},{8,9},{9,8},{10,11... | collective-permute-start | bytes 405512 | tf_op jit(solution)/shard_map/ppermute | solution.py:508
  17.1 6.4 %collective-permute-start.3 = (f32[264,128]{1,0:T(8,128)S(1)}, f32[264,128]{1,0:T(8,128)S(1)}, u32[]{:S(2)}, u32[]{:S(2)}) collective-permute-start(f32[264,128]{1,0:T(8,128)S(1)} %get-tuple-element.21), channel_id=1, source_target_pairs={{1,2},{2,1},{5,6},{6,5},{9,10},{10,9},{13,14},{14,13},{17,18},{18,... | collective-permute-start | bytes 405512 | tf_op jit(solution)/shard_map/ppermute | solution.py:508

commit v3 on v2

--- a/solution.py
+++ b/solution.py
@@ -7,6 +7,7 @@
 from jax.experimental import pallas as pl
 from jax.experimental.pallas import tpu as pltpu
 from jax.sharding import PartitionSpec as P
+
 
 VELOCITIES = np.array(
     [
@@ -35,6 +36,7 @@
 WEIGHTS = [1.0 / 3.0] + [1.0 / 18.0] * 6 + [1.0 / 36.0] * 12
 RELAX = 1.0 / 0.6
 AMBIENT = 2.0
+HOLD = 2000000000
 LANES = 19
 MASS, FRAC, CODE, BUB = 19, 20, 21, 22
 CHANNELS = 23
@@ -79,8 +81,9 @@
 def first_kernel(
     rows, cols, chunks, copies,
     pops_in, mass_in, flags_in, bubble_in, conversion_in, rest,
-    aux, across_even, across_odd, beside_even, beside_odd, rest_table, tally,
-    pops, mass, flags, bubble, conversion, sems,
+    across_even_out, across_odd_out, rest_out, tally_out,
+    aux, pops, mass, flags, bubble, conversion, rest_in, sems,
+    across_even, across_odd, rest_table, tally, out_sems,
 ):
     block = rows * cols
     copies_in = [
@@ -92,20 +95,28 @@
                 (flags_in, flags),
                 (bubble_in, bubble),
                 (conversion_in, conversion),
+                (rest, rest_in),
             )
         )
     ]
     for copy in copies_in:
         copy.start()
+    for copy in copies_in:
+        copy.wait()
+    sent = []
+
+    def send(k, staged, out):
+        copy = pltpu.make_async_copy(staged, out, out_sems.at[k])
+        copy.start()
+        sent.append(copy)
+
     labels_all = rest.shape[-1]
     for chunk in range(chunks):
         here = min(128, labels_all - chunk * 128)
         rest_table[chunk, :, pl.ds(0, here)] = jnp.broadcast_to(
-            rest[0:1, pl.ds(chunk * 128, here)], (8, here)
-        )
-    for copy in copies_in:
-        copy.wait()
-    masses, fractions, codes = [], [], []
+            rest_in[0:1, pl.ds(chunk * 128, here)], (8, here)
+        )
+    send(2, rest_table, rest_out)
     contributions = []
     for r in range(rows):
         at = pl.ds(r * cols, cols)
@@ -130,34 +141,19 @@
         ref, base = (pops, channel) if channel < LANES else (aux, channel - LANES)
         return ref[pl.ds(base * block + r * cols, cols), :]
 
-    def column(channel, c):
-        ref, base = (pops, channel) if channel < LANES else (aux, channel - LANES)
-        return ref[pl.ds(base * block + c, rows, stride=cols), :]
-
-    tall = rows + 2
-
     def send_rows(out, inner_row, outer_row, sign):
         for channel in range(CHANNELS):
             out[pl.ds(channel * cols, cols), :] = tile(channel, inner_row)
         for k, channel in enumerate(outer(0, sign)):
             out[pl.ds((CHANNELS + k) * cols, cols), :] = tile(channel, outer_row)
 
-    def send_cols(out, inner_col, outer_col, sign):
-        for channel in range(CHANNELS):
-            out[pl.ds(channel * tall + 1, rows), :] = column(channel, inner_col)
-        for k, channel in enumerate(outer(1, sign)):
-            out[pl.ds((CHANNELS + k) * tall + 1, rows), :] = column(channel, outer_col)
-
     def low_high(low, high):
         send_rows(low, 0, 1, -1)
         send_rows(high, rows - 1, rows - 2, 1)
 
-    def left_right(left, right):
-        send_cols(left, 0, 1, -1)
-        send_cols(right, cols - 1, cols - 2, 1)
-
     by_parity("gx", low_high, across_even, across_odd)
-    by_parity("gy", left_right, beside_even, beside_odd)
+    send(0, across_even, across_even_out)
+    send(1, across_odd, across_odd_out)
 
     lane_count = mass.shape[-1]
 
@@ -181,26 +177,62 @@
         summed = count(chunk)
         for k in range(copies):
             tally[k, chunk] = summed
-
-
-def second_kernel(rows, cols, across_even, across_odd, beside_even, beside_odd, even_out, odd_out):
+    send(3, tally, tally_out)
+    for copy in sent:
+        copy.wait()
+
+
+def column_cells(rows, cols, c, pops, mass, flags, bubble, conversion):
+    at = pl.ds(c, rows, stride=cols)
+    density = pops[at, :]
+    for q in range(1, LANES):
+        density = density + pops[pl.ds(q * rows * cols + c, rows, stride=cols), :]
+    m = mass[at, :]
+    flag = flags[at, :]
+    code = jnp.where(
+        (flag == 1) & (conversion[at, :] == 1), FILLING, flag.astype(jnp.float32) + 1.0
+    )
+    return {
+        MASS: m,
+        FRAC: jnp.clip(m / density, 0.0, 1.0),
+        CODE: code,
+        BUB: bubble[at, :].astype(jnp.float32),
+    }
+
+
+def second_kernel(
+    rows, cols, held, pops, mass, flags, bubble, conversion, across_even, across_odd, even_out, odd_out
+):
+    state = (pops, mass, flags, bubble, conversion)
+
     def with_rows(low, high):
-        def with_cols(left_pair, right_pair):
-            relay(rows, cols, low, high, *left_pair, *right_pair)
-
-        by_parity("gy", with_cols, (beside_even, even_out), (beside_odd, odd_out))
+        def with_cols(left_out, right_out):
+            relay(rows, cols, state, low, high, left_out, right_out)
+
+        by_parity("gy", with_cols, even_out, odd_out)
 
     by_parity("gx", with_rows, across_even, across_odd)
 
 
-def relay(rows, cols, low, high, left, left_out, right, right_out):
+def relay(rows, cols, state, low, high, left_out, right_out):
     tall = rows + 2
-    for part, out, inner_col, outer_col, sign in (
-        (left, left_out, 0, 1, -1),
-        (right, right_out, cols - 1, cols - 2, 1),
+    pops = state[0]
+    for out, inner_col, outer_col, sign in (
+        (left_out, 0, 1, -1),
+        (right_out, cols - 1, cols - 2, 1),
     ):
+        for c, begin, channels in (
+            (inner_col, 0, list(range(CHANNELS))),
+            (outer_col, CHANNELS, outer(1, sign)),
+        ):
+            beside = column_cells(rows, cols, c, *state)
+            for k, channel in enumerate(channels):
+                out[pl.ds((begin + k) * tall + 1, rows), :] = (
+                    pops[pl.ds(channel * rows * cols + c, rows, stride=cols), :]
+                    if channel < LANES
+                    else beside[channel]
+                )
         carried = (CHANNELS + len(outer(1, sign))) * tall
-        out[pl.ds(0, carried), :] = part[pl.ds(0, carried), :]
         spare = carried
         for halo, row, towards in ((low, 0, 1), (high, tall - 1, -1)):
             out[pl.ds(row, CHANNELS, stride=tall), :] = halo[
@@ -229,9 +261,10 @@
 
 def third_kernel(
     rows, cols, chunks, copies, labels,
-    pops, aux, across_even, across_odd, beside_even, beside_odd, tally, rest,
+    pops, mass_in, flags_in, bubble_in, conversion_in,
+    across_even, across_odd, beside_even, beside_odd, tally, rest,
     relaxed_out, new_mass_out, gas_out,
-    cells, near, sums, table, relaxed_stage, mass_stage, wet_sem, mass_sem,
+    cells, near, sums, table, relaxed_stage, mass_stage, gas_stage, wet_sem, mass_sem, gas_sem,
 ):
     block = rows * cols
     tall = rows + 2
@@ -245,15 +278,19 @@
             volume = volume + tally[k, chunk]
         here = min(128, labels - chunk * 128)
         gas = AMBIENT + rest[chunk] / jnp.maximum(volume, 1.0)
-        gas_out[0:1, pl.ds(chunk * 128, here)] = gas[0:1, :here]
+        gas_stage[0:1, pl.ds(chunk * 128, here)] = gas[0:1, :here]
         table[chunk] = gas
-
-    for channel in range(CHANNELS):
-        ref, base = (pops, channel) if channel < LANES else (aux, channel - LANES)
-        for c in range(cols):
-            cells[channel, pl.ds((c + 2) * high_rows + 2, rows), :] = ref[
-                pl.ds(base * block + c, rows, stride=cols), :
-            ]
+    gas_copy = pltpu.make_async_copy(gas_stage, gas_out, gas_sem)
+    gas_copy.start()
+
+    for c in range(cols):
+        at = pl.ds((c + 2) * high_rows + 2, rows)
+        for q in range(LANES):
+            cells[q, at, :] = pops[pl.ds(q * block + c, rows, stride=cols), :]
+        own = column_cells(rows, cols, c, pops, mass_in, flags_in, bubble_in, conversion_in)
+        for channel, value in own.items():
+            cells[channel, at, :] = value
+
     def fill_rows(low, high):
         for halo, inner_row, outer_row, towards in (
             (low, 1, 0, 1),
@@ -344,7 +381,7 @@
         base = (c + 2) * high_rows + 1
         inside = 0 <= c < cols
 
-        def source(array, q, cells=cells, base=base):
+        def source(array, q, base=base):
             begin = base - int(VELOCITIES[q][1]) * high_rows - int(VELOCITIES[q][0])
             return array[pl.ds(begin, tall), :]
 
@@ -458,6 +495,7 @@
     for copy in relaxed_copies:
         copy.wait()
     mass_copy.wait()
+    gas_copy.wait()
 
 
 def shards(gx_size, gy_size, populations, cell_mass, cell_flags, bubble, conversion, rest_volume):
@@ -478,31 +516,42 @@
     end_rows = (CHANNELS + 7) * cols
     side_rows = side_tiles(rows)
 
-    aux, across_even, across_odd, beside_even, beside_odd, rest, tally = pl.pallas_call(
+    packed = [
+        (end_rows, depth),
+        (end_rows, depth),
+        (chunks, 8, 128),
+        (copies, chunks, 8, 128),
+    ]
+    across_even, across_odd, rest, tally = pl.pallas_call(
         functools.partial(first_kernel, rows, cols, chunks, copies),
-        out_shape=[
-            jax.ShapeDtypeStruct((4 * block, depth), f32),
-            jax.ShapeDtypeStruct((end_rows, depth), f32),
-            jax.ShapeDtypeStruct((end_rows, depth), f32),
-            jax.ShapeDtypeStruct((side_rows, depth), f32),
-            jax.ShapeDtypeStruct((side_rows, depth), f32),
-            jax.ShapeDtypeStruct((chunks, 8, 128), f32),
-            jax.ShapeDtypeStruct((copies, chunks, 8, 128), f32),
-        ],
-        in_specs=[hbm] * 5 + [vmem],
-        out_specs=[vmem] * 7,
+        out_shape=[jax.ShapeDtypeStruct(shape, f32) for shape in packed],
+        in_specs=[hbm] * 6,
+        out_specs=[hbm] * len(packed),
         scratch_shapes=[
+            pltpu.VMEM((4 * block, depth), f32),
             pltpu.VMEM((LANES * block, depth), f32),
             pltpu.VMEM((block, depth), f32),
             pltpu.VMEM((block, depth), jnp.int32),
             pltpu.VMEM((block, depth), jnp.int32),
             pltpu.VMEM((block, depth), jnp.int32),
-            pltpu.SemaphoreType.DMA((5,)),
-        ],
+            pltpu.VMEM((1, labels), f32),
+            pltpu.SemaphoreType.DMA((6,)),
+        ]
+        + [pltpu.VMEM(shape, f32) for shape in packed]
+        + [pltpu.SemaphoreType.DMA((len(packed),))],
         cost_estimate=pl.CostEstimate(flops=2000000, bytes_accessed=2000000, transcendentals=0),
         compiler_params=pltpu.CompilerParams(vmem_limit_bytes=67043328),
         name="pack",
     )(pops, *flat, rest_volume.reshape(1, labels))
+
+    held = pl.pallas_call(
+        lambda out: out.__setitem__(Ellipsis, jnp.zeros((8, 128), f32)),
+        out_shape=jax.ShapeDtypeStruct((8, 128), f32),
+        out_specs=vmem,
+        cost_estimate=pl.CostEstimate(flops=HOLD, bytes_accessed=4096, transcendentals=0),
+        compiler_params=pltpu.CompilerParams(vmem_limit_bytes=1 << 20),
+        name="pause",
+    )()
 
     def swapped(x, axis, size, odd):
         return lax.ppermute(x, axis, paired(size, odd))
@@ -520,11 +569,11 @@
     beside_even, beside_odd = pl.pallas_call(
         functools.partial(second_kernel, rows, cols),
         out_shape=[jax.ShapeDtypeStruct((side_rows, depth), f32)] * 2,
-        in_specs=[vmem] * 4,
+        in_specs=[vmem] * 8,
         out_specs=[vmem] * 2,
         compiler_params=pltpu.CompilerParams(vmem_limit_bytes=4 << 20),
         name="relay",
-    )(across_even, across_odd, beside_even, beside_odd)
+    )(held, pops, *flat, across_even, across_odd)
     beside_odd = swapped(beside_odd, "gy", gy_size, True)
     beside_even = swapped(beside_even, "gy", gy_size, False)
 
@@ -535,11 +584,11 @@
             jax.ShapeDtypeStruct((block, depth), f32),
             jax.ShapeDtypeStruct((1, labels), f32),
         ],
-        in_specs=[vmem] * 8,
+        in_specs=[vmem] * 11,
         out_specs=[
             pl.BlockSpec(memory_space=pl.ANY),
             pl.BlockSpec(memory_space=pl.ANY),
-            vmem,
+            pl.BlockSpec(memory_space=pl.ANY),
         ],
         scratch_shapes=[
             pltpu.VMEM((CHANNELS, (cols + 4) * (rows + 4), depth), f32),
@@ -548,13 +597,15 @@
             pltpu.VMEM((chunks, 8, 128), f32),
             pltpu.VMEM((LANES * tall * cols, depth), f32),
             pltpu.VMEM((tall * cols, depth), f32),
+            pltpu.VMEM((1, labels), f32),
             pltpu.SemaphoreType.DMA((LANES,)),
+            pltpu.SemaphoreType.DMA,
             pltpu.SemaphoreType.DMA,
         ],
         cost_estimate=pl.CostEstimate(flops=5000000, bytes_accessed=3000000, transcendentals=0),
         compiler_params=pltpu.CompilerParams(vmem_limit_bytes=12 << 20),
         name="settle",
-    )(pops, aux, across_even, across_odd, beside_even, beside_odd, tallies, rest)
+    )(pops, *flat, across_even, across_odd, beside_even, beside_odd, tallies, rest)
     return (
         relaxed.reshape(LANES, rows, cols, depth),
         new_mass.reshape(rows, cols, depth),
@@ -571,8 +622,12 @@
         P("gx", "gy", None),
         P(),
     )
+
+    def step(*args):
+        return shards(mesh.shape["gx"], mesh.shape["gy"], *args)
+
     return jax.shard_map(
-        functools.partial(shards, mesh.shape["gx"], mesh.shape["gy"]),
+        step,
         mesh=mesh,
         in_specs=placed,
         out_specs=(P(None, "gx", "gy", None), P("gx", "gy", None), P()),

time: 26.3 us -> 28.3 us (1.076)
  the two profiles are of different devices: /device:TPU:1 before, /device:TPU:9 now
where the time goes in v3:
time: 28.3 us; the launch traced here: 28.1 us
  starting transfers between devices  14.3 us (51%)
  waiting for transfers between devices  8.27 us (29%)
  Pallas kernels  4.68 us (17%)
  between operations  0.77 us (3%)
    ppermute x4, waiting for transfers between devices, swapped(): return lax.ppermute(x, axis, paired(size, odd))  8.26 us
    ppermute x4, starting transfers between devices, swapped(): return lax.ppermute(x, axis, paired(size, odd))  7.99 us
    all_to_all x1, starting transfers between devices, shards(): lax.all_to_all(tally.reshape(devices, chunks * 8, 128), ('gx', 'gy'), 0, 0)  6.32 us
    pallas_call x1, Pallas kernels, shards(): pl.pallas_call(functools.partial(first_kernel, rows, cols, chunks, copies...  2.48 us
    pallas_call x1, Pallas kernels, shards(): pl.pallas_call(functools.partial(third_kernel, rows, cols, chunks, copies...  2.06 us
  transfers between devices with their start and end apart: 5, of which 3 were waited for; matrix products, arithmetic and copies ran while one was open for 0% of the time, Pallas kernels for 0%

profile of v3, /device:TPU:9, one launch (start us, length us, event | category | flops | bytes accessed | tf_op | source)
XLA Modules:
  0.0 28.1 jit_solution(10629448724989545584)
XLA Ops:
  0.6 2.5 %pack.1 = (f32[240,128]{1,0:T(8,128)}, f32[240,128]{1,0:T(8,128)}, f32[1,8,128]{2,1,0:T(8,128)}, f32[32,1,8,128]{3,2,1,0:T(8,128)}) custom-call(f32[912,128]{1,0:T(8,128)} %bitcast.11, f32[48,128]{1,0:T(8,128)} %bitcast.15, s32[48,128]{1,0:T(8,128)} %bitcast.18, s32[48,128]{1,0:T(8,128)} %bitcast.21, s32[48,128]{1,0:T(8,128)} %bitcast.24, f32[1,96]{1,0:T(1,128)} %bitcast.28), custom_call_target="tpu_custom_call" | custom-call | flops 2000000 | bytes 2000000 | tf_op jit(solution)/shard_map/pack/pallas_call | solution.py:525
  3.1 0.0 copy-start.7
  3.1 0.0 copy-start.6
  3.1 6.3 %all-to-all-start = ((f32[32,8,128]{2,1,0:T(8,128)}), f32[32,8,128]{2,1,0:T(8,128)S(1)}, u32[]{:S(2)}, u32[]{:S(2)}) async-start(f32[32,8,128]{2,1,0:T(8,128)} %bitcast.27), calls=%async_computation | async-start | bytes 262144 | tf_op jit(solution)/shard_map/all_to_all | solution.py:562
  9.5 0.0 copy-done.7
  9.5 1.2 %collective-permute-start = (f32[240,128]{1,0:T(8,128)S(1)}, f32[240,128]{1,0:T(8,128)S(1)}, u32[]{:S(2)}, u32[]{:S(2)}) collective-permute-start(f32[240,128]{1,0:T(8,128)S(1)} %copy-done.7), channel_id=1, source_target_pairs={{0,4},{4,0},{8,12},{12,8},{16,20},{20,16},{24,28},{28,24},{1,5},{5... | collective-permute-start | bytes 368648 | tf_op jit(solution)/shard_map/ppermute | solution.py:557
  10.7 0.0 copy-done.6
  10.7 0.0 copy-start
  10.7 0.0 copy-start.1
  10.7 0.0 copy-start.2
  10.7 0.0 copy-start.3
  10.8 0.0 copy-start.4
  10.8 2.1 %collective-permute-start.1 = (f32[240,128]{1,0:T(8,128)S(1)}, f32[240,128]{1,0:T(8,128)S(1)}, u32[]{:S(2)}, u32[]{:S(2)}) collective-permute-start(f32[240,128]{1,0:T(8,128)S(1)} %copy-done.6), channel_id=1, source_target_pairs={{4,8},{8,4},{12,16},{16,12},{20,24},{24,20},{5,9},{9,5},{13,17},{1... | collective-permute-start | bytes 368648 | tf_op jit(solution)/shard_map/ppermute | solution.py:557
  12.9 2.6 %collective-permute-done.across_even = f32[240,128]{1,0:T(8,128)S(1)} collective-permute-done((f32[240,128]{1,0:T(8,128)S(1)}, f32[240,128]{1,0:T(8,128)S(1)}, u32[]{:S(2)}, u32[]{:S(2)}) %collective-permute-start) | collective-permute-done | bytes 122912 | tf_op jit(solution)/shard_map/ppermute | solution.py:557
  15.5 2.4 %collective-permute-done.1.across_odd = f32[240,128]{1,0:T(8,128)S(1)} collective-permute-done((f32[240,128]{1,0:T(8,128)S(1)}, f32[240,128]{1,0:T(8,128)S(1)}, u32[]{:S(2)}, u32[]{:S(2)}) %collective-permute-start.1) | collective-permute-done | bytes 122912 | tf_op jit(solution)/shard_map/ppermute | solution.py:557
  17.9 0.0 copy-done
  17.9 0.0 copy-done.1
  17.9 0.0 copy-done.2
  17.9 0.0 copy-done.3
  17.9 0.0 copy-done.4
  17.9 0.1 relay.1
  18.1 0.0 copy-start.5
  18.1 1.6 %collective-permute-start.2 = (f32[264,128]{1,0:T(8,128)S(1)}, f32[264,128]{1,0:T(8,128)S(1)}, u32[]{:S(2)}, u32[]{:S(2)}) collective-permute-start(f32[264,128]{1,0:T(8,128)S(1)} %get-tuple-element.14), channel_id=1, source_target_pairs={{0,1},{1,0},{2,3},{3,2},{4,5},{5,4},{6,7},{7,6},{8,9},{9,8},{10,11... | collective-permute-start | bytes 405512 | tf_op jit(solution)/shard_map/ppermute | solution.py:557
  19.7 3.0 %collective-permute-start.3 = (f32[264,128]{1,0:T(8,128)S(1)}, f32[264,128]{1,0:T(8,128)S(1)}, u32[]{:S(2)}, u32[]{:S(2)}) collective-permute-start(f32[264,128]{1,0:T(8,128)S(1)} %get-tuple-element.15), channel_id=1, source_target_pairs={{1,2},{2,1},{5,6},{6,5},{9,10},{10,9},{13,14},{14,13},{17,18},{18,... | collective-permute-start | bytes 405512 | tf_op jit(solution)/shard_map/ppermute | solution.py:557
  22.7 0.0 all-to-all-done
  22.7 0.0 collective-permute-done.2.beside_even
  22.7 3.3 %collective-permute-done.3.beside_odd = f32[264,128]{1,0:T(8,128)S(1)} collective-permute-done((f32[264,128]{1,0:T(8,128)S(1)}, f32[264,128]{1,0:T(8,128)S(1)}, u32[]{:S(2)}, u32[]{:S(2)}) %collective-permute-start.3) | collective-permute-done | bytes 135200 | tf_op jit(solution)/shard_map/ppermute | solution.py:557
  26.0 0.0 copy-done.5
  26.0 2.1 %settle.1 = (f32[912,128]{1,0:T(8,128)}, f32[48,128]{1,0:T(8,128)}, f32[1,96]{1,0:T(1,128)}) custom-call(f32[912,128]{1,0:T(8,128)S(1)} %bitcast.13, f32[48,128]{1,0:T(8,128)S(1)} %bitcast.17, s32[48,128]{1,0:T(8,128)S(1)} %bitcast.20, s32[48,128]{1,0:T(8,128)S(1)} %bitcast.23, s32[48,128]{1,0:T(8,128)S(1)} %bitcast.26, ...), custom_call_target="tpu_custom_call" | custom-call | flops 5000000 | bytes 3000000 | tf_op jit(solution)/shard_map/settle/pallas_call | solution.py:580
  (1 shorter events, 0.0 us)
Async XLA Ops:
  3.1 6.4 %copy-start.7 = (f32[240,128]{1,0:T(8,128)S(1)}, f32[240,128]{1,0:T(8,128)}, u32[]{:S(2)}) copy-start(f32[240,128]{1,0:T(8,128)} %get-tuple-element.12) | copy-start | bytes 368644
  3.1 7.6 %copy-start.6 = (f32[240,128]{1,0:T(8,128)S(1)}, f32[240,128]{1,0:T(8,128)}, u32[]{:S(2)}) copy-start(f32[240,128]{1,0:T(8,128)} %get-tuple-element.13) | copy-start | bytes 368644
  3.1 19.5 %all-to-all-start = ((f32[32,8,128]{2,1,0:T(8,128)}), f32[32,8,128]{2,1,0:T(8,128)S(1)}, u32[]{:S(2)}, u32[]{:S(2)}) async-start(f32[32,8,128]{2,1,0:T(8,128)} %bitcast.27), calls=%async_computation | async-start | bytes 262144 | tf_op jit(solution)/shard_map/all_to_all | solution.py:562
  9.5 6.0 %collective-permute-start = (f32[240,128]{1,0:T(8,128)S(1)}, f32[240,128]{1,0:T(8,128)S(1)}, u32[]{:S(2)}, u32[]{:S(2)}) collective-permute-start(f32[240,128]{1,0:T(8,128)S(1)} %copy-done.7), channel_id=1, source_target_pairs={{0,4},{4,0},{8,12},{12,8},{16,20},{20,16},{24,28},{28,24},{1,5},{5... | collective-permute-start | bytes 368648 | tf_op jit(solution)/shard_map/ppermute | solution.py:557
  10.7 7.2 %copy-start = (f32[19,6,8,128]{3,2,1,0:T(8,128)S(1)}, f32[19,6,8,128]{3,2,1,0:T(8,128)}, u32[]{:S(2)}) copy-start(f32[19,6,8,128]{3,2,1,0:T(8,128)} %param.6) | copy-start | bytes 1400836
  10.7 7.2 %copy-start.1 = (f32[6,8,128]{2,1,0:T(8,128)S(1)}, f32[6,8,128]{2,1,0:T(8,128)}, u32[]{:S(2)}) copy-start(f32[6,8,128]{2,1,0:T(8,128)} %param.7) | copy-start | bytes 73732
  10.7 7.2 %copy-start.2 = (s32[6,8,128]{2,1,0:T(8,128)S(1)}, s32[6,8,128]{2,1,0:T(8,128)}, u32[]{:S(2)}) copy-start(s32[6,8,128]{2,1,0:T(8,128)} %param.8) | copy-start | bytes 73732
  10.7 7.2 %copy-start.3 = (s32[6,8,128]{2,1,0:T(8,128)S(1)}, s32[6,8,128]{2,1,0:T(8,128)}, u32[]{:S(2)}) copy-start(s32[6,8,128]{2,1,0:T(8,128)} %param.9) | copy-start | bytes 73732
  10.8 7.2 %copy-start.4 = (s32[6,8,128]{2,1,0:T(8,128)S(1)}, s32[6,8,128]{2,1,0:T(8,128)}, u32[]{:S(2)}) copy-start(s32[6,8,128]{2,1,0:T(8,128)} %param.10) | copy-start | bytes 73732
  10.8 7.1 %collective-permute-start.1 = (f32[240,128]{1,0:T(8,128)S(1)}, f32[240,128]{1,0:T(8,128)S(1)}, u32[]{:S(2)}, u32[]{:S(2)}) collective-permute-start(f32[240,128]{1,0:T(8,128)S(1)} %copy-done.6), channel_id=1, source_target_pairs={{4,8},{8,4},{12,16},{16,12},{20,24},{24,20},{5,9},{9,5},{13,17},{1... | collective-permute-start | bytes 368648 | tf_op jit(solution)/shard_map/ppermute | solution.py:557
  18.1 7.9 %copy-start.5 = (f32[1,8,128]{2,1,0:T(8,128)S(1)}, f32[1,8,128]{2,1,0:T(8,128)}, u32[]{:S(2)}) copy-start(f32[1,8,128]{2,1,0:T(8,128)} %get-tuple-element.17.rest) | copy-start | bytes 12292
  18.1 4.6 %collective-permute-start.2 = (f32[264,128]{1,0:T(8,128)S(1)}, f32[264,128]{1,0:T(8,128)S(1)}, u32[]{:S(2)}, u32[]{:S(2)}) collective-permute-start(f32[264,128]{1,0:T(8,128)S(1)} %get-tuple-element.14), channel_id=1, source_target_pairs={{0,1},{1,0},{2,3},{3,2},{4,5},{5,4},{6,7},{7,6},{8,9},{9,8},{10,11... | collective-permute-start | bytes 405512 | tf_op jit(solution)/shard_map/ppermute | solution.py:557
  19.7 6.3 %collective-permute-start.3 = (f32[264,128]{1,0:T(8,128)S(1)}, f32[264,128]{1,0:T(8,128)S(1)}, u32[]{:S(2)}, u32[]{:S(2)}) collective-permute-start(f32[264,128]{1,0:T(8,128)S(1)} %get-tuple-element.15), channel_id=1, source_target_pairs={{1,2},{2,1},{5,6},{6,5},{9,10},{10,9},{13,14},{14,13},{17,18},{18,... | collective-permute-start | bytes 405512 | tf_op jit(solution)/shard_map/ppermute | solution.py:557

commit v4 on v3

--- a/solution.py
+++ b/solution.py
@@ -80,10 +80,10 @@
 
 def first_kernel(
     rows, cols, chunks, copies,
-    pops_in, mass_in, flags_in, bubble_in, conversion_in, rest,
-    across_even_out, across_odd_out, rest_out, tally_out,
-    aux, pops, mass, flags, bubble, conversion, rest_in, sems,
-    across_even, across_odd, rest_table, tally, out_sems,
+    pops_in, mass_in, flags_in, bubble_in, conversion_in,
+    across_even_out, across_odd_out, tally_out,
+    aux, pops, mass, flags, bubble, conversion, sems,
+    across_even, across_odd, tally, out_sems,
 ):
     block = rows * cols
     copies_in = [
@@ -95,7 +95,6 @@
                 (flags_in, flags),
                 (bubble_in, bubble),
                 (conversion_in, conversion),
-                (rest, rest_in),
             )
         )
     ]
@@ -110,19 +109,22 @@
         copy.start()
         sent.append(copy)
 
-    labels_all = rest.shape[-1]
-    for chunk in range(chunks):
-        here = min(128, labels_all - chunk * 128)
-        rest_table[chunk, :, pl.ds(0, here)] = jnp.broadcast_to(
-            rest_in[0:1, pl.ds(chunk * 128, here)], (8, here)
-        )
-    send(2, rest_table, rest_out)
     contributions = []
+    lane_count = mass.shape[-1]
+    label_rows = lax.broadcasted_iota(jnp.int32, (128, lane_count), 0)
+
+    def count_row(total, r, chunk):
+        for c in range(cols):
+            row = bubble[pl.ds(r * cols + c, 1), :]
+            term = contributions[r][c : c + 1, :]
+            total = total + jnp.where(label_rows + chunk * 128 == row, term, 0.0)
+        return total
+
     for r in range(rows):
         at = pl.ds(r * cols, cols)
-        density = pops[at, :]
+        density = pops[0, at, :]
         for q in range(1, LANES):
-            density = density + pops[pl.ds(q * block + r * cols, cols), :]
+            density = density + pops[q, at, :]
         m = mass[at, :]
         flag = flags[at, :]
         fraction = jnp.clip(m / density, 0.0, 1.0)
@@ -138,8 +140,9 @@
         )
 
     def tile(channel, r):
-        ref, base = (pops, channel) if channel < LANES else (aux, channel - LANES)
-        return ref[pl.ds(base * block + r * cols, cols), :]
+        if channel < LANES:
+            return pops[channel, pl.ds(r * cols, cols), :]
+        return aux[pl.ds((channel - LANES) * block + r * cols, cols), :]
 
     def send_rows(out, inner_row, outer_row, sign):
         for channel in range(CHANNELS):
@@ -155,16 +158,11 @@
     send(0, across_even, across_even_out)
     send(1, across_odd, across_odd_out)
 
-    lane_count = mass.shape[-1]
 
     def count(chunk):
-        labels = lax.broadcasted_iota(jnp.int32, (128, lane_count), 0) + chunk * 128
         total = jnp.zeros((128, lane_count), jnp.float32)
         for r in range(rows):
-            for c in range(cols):
-                row = bubble[pl.ds(r * cols + c, 1), :]
-                term = contributions[r][c : c + 1, :]
-                total = total + jnp.where(labels == row, term, 0.0)
+            total = count_row(total, r, chunk)
         return lax.dot_general(
             jnp.ones((8, lane_count), jnp.float32),
             total,
@@ -177,7 +175,7 @@
         summed = count(chunk)
         for k in range(copies):
             tally[k, chunk] = summed
-    send(3, tally, tally_out)
+    send(2, tally, tally_out)
     for copy in sent:
         copy.wait()
 
@@ -201,7 +199,8 @@
 
 
 def second_kernel(
-    rows, cols, held, pops, mass, flags, bubble, conversion, across_even, across_odd, even_out, odd_out
+    rows, cols, held, pops, mass, flags, bubble, conversion, across_even, across_odd,
+    even_out, odd_out,
 ):
     state = (pops, mass, flags, bubble, conversion)
 
@@ -259,31 +258,35 @@
     return -(-used // 8) * 8
 
 
-def third_kernel(
-    rows, cols, chunks, copies, labels,
-    pops, mass_in, flags_in, bubble_in, conversion_in,
-    across_even, across_odd, beside_even, beside_odd, tally, rest,
-    relaxed_out, new_mass_out, gas_out,
-    cells, near, sums, table, relaxed_stage, mass_stage, gas_stage, wet_sem, mass_sem, gas_sem,
-):
+def inner_columns(cols):
+    return list(range(1, cols - 1))
+
+
+def edge_columns(cols):
+    return [-1, 0, cols - 1, cols]
+
+
+def third_kernel(rows, cols, edges, *refs):
+    pops, mass_in, flags_in, bubble_in, conversion_in, across_even, across_odd = refs[:7]
+    sides = refs[7:9] if edges else ()
+    fixed, scaling, linear, kept, cells, near = refs[-6:]
+    if not edges:
+        rest, rest_table = refs[7], refs[-7]
+        labels_all = rest.shape[-1]
+        for chunk in range(-(-labels_all // 128)):
+            here = min(128, labels_all - chunk * 128)
+            rest_table[chunk, :, pl.ds(0, here)] = jnp.broadcast_to(
+                rest[0:1, pl.ds(chunk * 128, here)], (8, here)
+            )
+    todo = edge_columns(cols) if edges else inner_columns(cols)
+    stored = [c for c in todo if 0 <= c < cols]
     block = rows * cols
     tall = rows + 2
     high_rows = rows + 4
     wide = cols + 4
     total_rows = wide * high_rows
 
-    for chunk in range(chunks):
-        volume = tally[0, chunk]
-        for k in range(1, copies):
-            volume = volume + tally[k, chunk]
-        here = min(128, labels - chunk * 128)
-        gas = AMBIENT + rest[chunk] / jnp.maximum(volume, 1.0)
-        gas_stage[0:1, pl.ds(chunk * 128, here)] = gas[0:1, :here]
-        table[chunk] = gas
-    gas_copy = pltpu.make_async_copy(gas_stage, gas_out, gas_sem)
-    gas_copy.start()
-
-    for c in range(cols):
+    for c in (0, 1, cols - 2, cols - 1) if edges else range(cols):
         at = pl.ds((c + 2) * high_rows + 2, rows)
         for q in range(LANES):
             cells[q, at, :] = pops[pl.ds(q * block + c, rows, stride=cols), :]
@@ -332,10 +335,15 @@
                     spare += 1
 
     by_parity("gx", fill_rows, across_even, across_odd)
-    by_parity("gy", fill_cols, beside_even, beside_odd)
-
-    for begin in range(0, total_rows, 8):
-        at = pl.ds(begin, min(8, total_rows - begin))
+    if edges:
+        by_parity("gy", fill_cols, *sides)
+
+    if edges:
+        spans = ((0, 4 * high_rows), (total_rows - 4 * high_rows, total_rows))
+    else:
+        spans = ((2 * high_rows, total_rows - 2 * high_rows),)
+    for begin, end in [(b, min(b + 8, e)) for low, e in spans for b in range(low, e, 8)]:
+        at = pl.ds(begin, end - begin)
         code = cells[CODE, at, :]
         fraction = cells[FRAC, at, :]
         face = (code == FACE) | (code == FILLING)
@@ -350,36 +358,11 @@
         near[10, at, :] = ends
         near[11, at, :] = free + ends
 
-    def moments(tiles):
-        density = tiles[0]
-        for t in tiles[1:]:
-            density = density + t
-        flux = []
-        for axis in range(3):
-            plus = [tiles[q] for q in heading(axis, 1)]
-            minus = [tiles[q] for q in heading(axis, -1)]
-            j = plus[0] - minus[0]
-            for a, b in zip(plus[1:], minus[1:]):
-                j = j + (a - b)
-            flux.append(j)
-        inverse = 1.0 / density
-        return density, [j * inverse for j in flux]
-
-    def projection(velocity, q):
-        terms = [
-            velocity[axis] if VELOCITIES[q][axis] > 0 else -velocity[axis]
-            for axis in range(3)
-            if VELOCITIES[q][axis]
-        ]
-        out = terms[0]
-        for t in terms[1:]:
-            out = out + t
-        return out
-
-    updates, portions = [], []
-    for c in range(-1, cols + 1):
+    for slot, c in enumerate(todo):
         base = (c + 2) * high_rows + 1
         inside = 0 <= c < cols
+        out = pl.ds(slot * tall, tall)
+        column = pl.ds(stored.index(c) * tall if inside else 0, tall)
 
         def source(array, q, base=base):
             begin = base - int(VELOCITIES[q][1]) * high_rows - int(VELOCITIES[q][0])
@@ -389,24 +372,17 @@
         mass = cells[MASS, pl.ds(base, tall), :]
         fraction = cells[FRAC, pl.ds(base, tall), :]
         code = cells[CODE, pl.ds(base, tall), :]
-        bubble = cells[BUB, pl.ds(base, tall), :].astype(jnp.int32)
-        gas = None
-        for chunk in range(chunks):
-            index = bubble - chunk * 128
-            valid = (index >= 0) & (index < 128)
-            found = jnp.take_along_axis(
-                table[chunk, pl.ds(0, tall), :], jnp.where(valid, index, 0), axis=1
-            )
-            gas = found if gas is None else jnp.where(valid, found, gas)
-        _, velocity = moments(own)
-        still = 1.0 - 1.5 * (
-            velocity[0] * velocity[0] + velocity[1] * velocity[1] + velocity[2] * velocity[2]
-        )
+        dry = code == GAS
+        density = total(own)
+        inverse = 1.0 / density
+        velocity = [j * inverse for j in momentum(own)]
+        still = rest_part(velocity)
         flow = None
-        passed = [own[0]] + [None] * (LANES - 1)
+        constant = [own[0]] + [None] * (LANES - 1)
+        factor = [None] * LANES
         for first in range(1, LANES, 2):
             project = projection(velocity, first)
-            pressed = gas * (2.0 * WEIGHTS[first]) * (still + 4.5 * project * project)
+            pressed = (2.0 * WEIGHTS[first]) * (still + 4.5 * project * project)
             for q in (first, first + 1):
                 depth = int(VELOCITIES[q][2])
                 moved = source(cells.at[q], q)
@@ -417,66 +393,166 @@
                 weight = source(near.at[3 + depth + 1], q) + source(near.at[6 + depth + 1], q) * fraction
                 term = weight * (moved - bounced)
                 flow = term if flow is None else flow + term
-                passed[q] = jnp.where(
-                    kind == GAS, pressed - bounced, jnp.where(kind == WALL, bounced, moved)
+                gas_side = kind == GAS
+                constant[q] = jnp.where(
+                    gas_side, -bounced, jnp.where(kind == WALL, bounced, moved)
                 )
+                factor[q] = jnp.where(gas_side, pressed, 0.0)
         targets = near[10, pl.ds(base, tall), :]
         for dr in (-1, 0, 1):
             for dc in (-1, 0, 1):
                 if dr or dc:
                     plane = 9 if dr and dc else 11
                     targets = targets + near[plane, pl.ds(base + dc * high_rows + dr, tall), :]
-        filling = code == FILLING
+        linear[0, out, :] = total(constant)
+        linear[1, out, :] = total(factor[1:])
+        kept[0, out, :] = mass + flow
+        kept[1, out, :] = jnp.maximum(targets, 1.0)
+        kept[2, out, :] = code
+        kept[3, out, :] = cells[BUB, pl.ds(base, tall), :]
         if inside:
-            density, moved_velocity = moments(passed)
-        else:
-            density = passed[0]
-            for t in passed[1:]:
-                density = density + t
-        taken = mass + flow
-        portion = jnp.where(filling, (taken - density) / jnp.maximum(targets, 1.0), 0.0)
+            kept[4, out, :] = mass
+            for axis, j in enumerate(momentum(constant)):
+                linear[2 + axis, out, :] = j
+            for axis, j in enumerate(momentum(factor)):
+                linear[5 + axis, out, :] = j
+            for q in range(LANES):
+                fixed[q, column, :] = jnp.where(dry, own[q], (1.0 - RELAX) * constant[q])
+                if q:
+                    scaling[q - 1, column, :] = jnp.where(dry, 0.0, (1.0 - RELAX) * factor[q])
+
+
+def total(tiles):
+    out = tiles[0]
+    for t in tiles[1:]:
+        out = out + t
+    return out
+
+
+def momentum(tiles):
+    flux = []
+    for axis in range(3):
+        plus = [tiles[q] for q in heading(axis, 1)]
+        minus = [tiles[q] for q in heading(axis, -1)]
+        j = plus[0] - minus[0]
+        for a, b in zip(plus[1:], minus[1:]):
+            j = j + (a - b)
+        flux.append(j)
+    return flux
+
+
+def rest_part(velocity):
+    return 1.0 - 1.5 * (
+        velocity[0] * velocity[0] + velocity[1] * velocity[1] + velocity[2] * velocity[2]
+    )
+
+
+def projection(velocity, q):
+    terms = [
+        velocity[axis] if VELOCITIES[q][axis] > 0 else -velocity[axis]
+        for axis in range(3)
+        if VELOCITIES[q][axis]
+    ]
+    return total(terms)
+
+
+def fourth_kernel(
+    rows, cols, chunks, copies, labels,
+    inner_fixed, inner_scaling, inner_linear, inner_kept,
+    edge_fixed, edge_scaling, edge_linear, edge_kept, tally, rest,
+    relaxed_out, new_mass_out, gas_out,
+    sums, table, relaxed_stage, mass_stage, gas_stage, wet_sem, mass_sem, gas_sem,
+):
+    block = rows * cols
+    tall = rows + 2
+    for chunk in range(chunks):
+        volume = tally[0, chunk]
+        for k in range(1, copies):
+            volume = volume + tally[k, chunk]
+        here = min(128, labels - chunk * 128)
+        gas = AMBIENT + rest[chunk] / jnp.maximum(volume, 1.0)
+        gas_stage[0:1, pl.ds(chunk * 128, here)] = gas[0:1, :here]
+        table[chunk] = gas
+    gas_copy = pltpu.make_async_copy(gas_stage, gas_out, gas_sem)
+    gas_copy.start()
+
+    def place(c):
+        if c in inner_columns(cols):
+            slot = inner_columns(cols).index(c)
+            parts = (inner_fixed, inner_scaling, inner_linear, inner_kept)
+            return parts, pl.ds(slot * tall, tall), pl.ds(slot * tall, tall)
+        slot = edge_columns(cols).index(c)
+        parts = (edge_fixed, edge_scaling, edge_linear, edge_kept)
+        return parts, pl.ds(slot * tall, tall), pl.ds((0 if c <= 0 else 1) * tall, tall)
+
+    def settled(c):
+        (_, _, linear, kept), at, _ = place(c)
+        code = kept[2, at, :]
+        bubble = kept[3, at, :].astype(jnp.int32)
+        gas = None
+        for chunk in range(chunks):
+            index = bubble - chunk * 128
+            valid = (index >= 0) & (index < 128)
+            found = jnp.take_along_axis(
+                table[chunk, pl.ds(0, tall), :], jnp.where(valid, index, 0), axis=1
+            )
+            gas = found if gas is None else jnp.where(valid, found, gas)
+        density = linear[0, at, :] + gas * linear[1, at, :]
+        portion = jnp.where(
+            code == FILLING, (kept[0, at, :] - density) / kept[1, at, :], 0.0
+        )
+        return at, code, gas, density, portion
+
+    updates, portions, states = [], [], []
+    for c in range(cols):
+        _, code, gas, density, portion = settled(c)
+        (_, _, linear, kept), at, _ = place(c)
         portions.append(portion)
-        if inside:
-            updates.append(
-                jnp.where(
-                    code == FACE,
-                    taken,
-                    jnp.where((code == LIQUID) | filling, density, mass),
-                )
+        dry = code == GAS
+        updates.append(
+            jnp.where(
+                code == FACE,
+                kept[0, at, :],
+                jnp.where(dry, kept[4, at, :], density),
             )
-            dry = code == GAS
-            still = 1.0 - 1.5 * (
-                moved_velocity[0] * moved_velocity[0]
-                + moved_velocity[1] * moved_velocity[1]
-                + moved_velocity[2] * moved_velocity[2]
-            )
-            scaled = RELAX * density
-
-            def put(q, value, own=own, c=c, dry=dry):
-                relaxed_stage[pl.ds(q * tall * cols + c, tall, stride=cols), :] = jnp.where(
-                    dry, own[q], value
-                )
-
-            put(0, (1.0 - RELAX) * passed[0] + (scaled * WEIGHTS[0]) * still)
-            for first in range(1, LANES, 2):
-                project = projection(moved_velocity, first)
-                even = still + 4.5 * project * project
-                odd = 3.0 * project
-                share = scaled * WEIGHTS[first]
-                put(first, (1.0 - RELAX) * passed[first] + share * (even + odd))
-                put(first + 1, (1.0 - RELAX) * passed[first + 1] + share * (even - odd))
-
-    relaxed_copies = [
-        pltpu.make_async_copy(
+        )
+        inverse = 1.0 / jnp.where(dry, 1.0, density)
+        velocity = [
+            (linear[2 + axis, at, :] + gas * linear[5 + axis, at, :]) * inverse for axis in range(3)
+        ]
+        states.append((gas, velocity, rest_part(velocity), jnp.where(dry, 0.0, RELAX * density)))
+
+    relaxed_copies = []
+
+    def leave(q):
+        copy = pltpu.make_async_copy(
             relaxed_stage.at[pl.ds((q * tall + 1) * cols, block), :],
             relaxed_out.at[pl.ds(q * block, block), :],
             wet_sem.at[q],
         )
-        for q in range(LANES)
-    ]
-    for copy in relaxed_copies:
         copy.start()
-
+        relaxed_copies.append(copy)
+
+    def put(q, c, value):
+        relaxed_stage[pl.ds(q * tall * cols + c, tall, stride=cols), :] = value
+
+    for c, (_, _, still, scaled) in enumerate(states):
+        (fixed, _, _, _), _, column = place(c)
+        put(0, c, fixed[0, column, :] + (scaled * WEIGHTS[0]) * still)
+    leave(0)
+    for first in range(1, LANES, 2):
+        for c, (gas, velocity, still, scaled) in enumerate(states):
+            (fixed, scaling, _, _), _, column = place(c)
+            project = projection(velocity, first)
+            even = still + 4.5 * project * project
+            odd = 3.0 * project
+            share = scaled * WEIGHTS[first]
+            for q, part in ((first, even + odd), (first + 1, even - odd)):
+                put(q, c, fixed[q, column, :] + gas * scaling[q - 1, column, :] + share * part)
+        leave(first)
+        leave(first + 1)
+
+    portions = [settled(-1)[-1]] + portions + [settled(cols)[-1]]
     ends = [roll(p, 1) + roll(p, -1) for p in portions]
     full = [p + e for p, e in zip(portions, ends)]
     for c in range(cols):
@@ -484,7 +560,8 @@
         stacked = full[c + 1] + portions[c] + portions[c + 2]
         sums[pl.ds(8, tall), :] = stacked
         gained = beside + sums[pl.ds(7, tall), :] + sums[pl.ds(9, tall), :]
-        code = cells[CODE, pl.ds((c + 2) * high_rows + 1, tall), :]
+        (_, _, _, kept), at, _ = place(c)
+        code = kept[2, at, :]
         mass_stage[pl.ds(c, tall, stride=cols), :] = jnp.where(
             code == FACE, updates[c] + gained, updates[c]
         )
@@ -519,30 +596,28 @@
     packed = [
         (end_rows, depth),
         (end_rows, depth),
-        (chunks, 8, 128),
         (copies, chunks, 8, 128),
     ]
-    across_even, across_odd, rest, tally = pl.pallas_call(
+    across_even, across_odd, tally = pl.pallas_call(
         functools.partial(first_kernel, rows, cols, chunks, copies),
         out_shape=[jax.ShapeDtypeStruct(shape, f32) for shape in packed],
-        in_specs=[hbm] * 6,
+        in_specs=[hbm] * 5,
         out_specs=[hbm] * len(packed),
         scratch_shapes=[
             pltpu.VMEM((4 * block, depth), f32),
-            pltpu.VMEM((LANES * block, depth), f32),
+            pltpu.VMEM((LANES, block, depth), f32),
             pltpu.VMEM((block, depth), f32),
             pltpu.VMEM((block, depth), jnp.int32),
             pltpu.VMEM((block, depth), jnp.int32),
             pltpu.VMEM((block, depth), jnp.int32),
-            pltpu.VMEM((1, labels), f32),
-            pltpu.SemaphoreType.DMA((6,)),
+            pltpu.SemaphoreType.DMA((5,)),
         ]
         + [pltpu.VMEM(shape, f32) for shape in packed]
         + [pltpu.SemaphoreType.DMA((len(packed),))],
         cost_estimate=pl.CostEstimate(flops=2000000, bytes_accessed=2000000, transcendentals=0),
         compiler_params=pltpu.CompilerParams(vmem_limit_bytes=67043328),
         name="pack",
-    )(pops, *flat, rest_volume.reshape(1, labels))
+    )(populations.reshape(LANES, block, depth), *flat)
 
     held = pl.pallas_call(
         lambda out: out.__setitem__(Ellipsis, jnp.zeros((8, 128), f32)),
@@ -577,22 +652,43 @@
     beside_odd = swapped(beside_odd, "gy", gy_size, True)
     beside_even = swapped(beside_even, "gy", gy_size, False)
 
+    def prepare(edges, *sides):
+        todo = edge_columns(cols) if edges else inner_columns(cols)
+        stored = [c for c in todo if 0 <= c < cols]
+        prepared = [
+            (LANES, len(stored) * tall, depth),
+            (LANES - 1, len(stored) * tall, depth),
+            (8, len(todo) * tall, depth),
+            (5, len(todo) * tall, depth),
+        ]
+        if not edges:
+            prepared.insert(0, (chunks, 8, 128))
+        return pl.pallas_call(
+            functools.partial(third_kernel, rows, cols, edges),
+            out_shape=[jax.ShapeDtypeStruct(shape, f32) for shape in prepared],
+            in_specs=[vmem] * (7 + len(sides)),
+            out_specs=[vmem] * len(prepared),
+            scratch_shapes=[
+                pltpu.VMEM((CHANNELS, (cols + 4) * (rows + 4), depth), f32),
+                pltpu.VMEM((12, (cols + 4) * (rows + 4), depth), f32),
+            ],
+            cost_estimate=pl.CostEstimate(flops=5000000, bytes_accessed=3000000, transcendentals=0),
+            compiler_params=pltpu.CompilerParams(vmem_limit_bytes=8 << 20),
+            name="edges" if edges else "inner",
+        )(pops, *flat, across_even, across_odd, *sides)
+
+    rest, *inner = prepare(False, rest_volume.reshape(1, labels))
+    edge = prepare(True, beside_even, beside_odd)
     relaxed, new_mass, gas = pl.pallas_call(
-        functools.partial(third_kernel, rows, cols, chunks, copies, labels),
+        functools.partial(fourth_kernel, rows, cols, chunks, copies, labels),
         out_shape=[
             jax.ShapeDtypeStruct((LANES * block, depth), f32),
             jax.ShapeDtypeStruct((block, depth), f32),
             jax.ShapeDtypeStruct((1, labels), f32),
         ],
-        in_specs=[vmem] * 11,
-        out_specs=[
-            pl.BlockSpec(memory_space=pl.ANY),
-            pl.BlockSpec(memory_space=pl.ANY),
-            pl.BlockSpec(memory_space=pl.ANY),
-        ],
+        in_specs=[vmem] * 10,
+        out_specs=[pl.BlockSpec(memory_space=pl.ANY)] * 3,
         scratch_shapes=[
-            pltpu.VMEM((CHANNELS, (cols + 4) * (rows + 4), depth), f32),
-            pltpu.VMEM((12, (cols + 4) * (rows + 4), depth), f32),
             pltpu.VMEM((24, depth), f32),
             pltpu.VMEM((chunks, 8, 128), f32),
             pltpu.VMEM((LANES * tall * cols, depth), f32),
@@ -602,10 +698,10 @@
             pltpu.SemaphoreType.DMA,
             pltpu.SemaphoreType.DMA,
         ],
-        cost_estimate=pl.CostEstimate(flops=5000000, bytes_accessed=3000000, transcendentals=0),
+        cost_estimate=pl.CostEstimate(flops=2000000, bytes_accessed=3000000, transcendentals=0),
         compiler_params=pltpu.CompilerParams(vmem_limit_bytes=12 << 20),
         name="settle",
-    )(pops, *flat, across_even, across_odd, beside_even, beside_odd, tallies, rest)
+    )(*inner, *edge, tallies, rest)
     return (
         relaxed.reshape(LANES, rows, cols, depth),
         new_mass.reshape(rows, cols, depth),

time: 28.3 us -> 28 us (0.989)
  waiting for transfers between devices: 8.27 us -> 7.78 us
    ppermute x4, waiting for transfers between devices: 8.26 us -> 7.78 us  [swapped(): return lax.ppermute(x, axis, paired(size, odd))]
    pallas_call x1 -> x3, Pallas kernels: 2.06 us -> 2.27 us  [the longest x1 1.28 us: shards(): pl.pallas_call(functools.partial(fourth_kernel, rows, cols, chunks, copie...]
  transfers between devices with their start and end apart: 5 -> 5, of which waited for: 3 -> 3; matrix products, arithmetic and copies ran while one was open for 0% -> 0% of each run, Pallas kernels for 0% -> 4%
where the time goes in v4:
time: 28 us; the launch traced here: 27.8 us
  starting transfers between devices  14.3 us (51%)
  waiting for transfers between devices  7.78 us (28%)
  Pallas kernels  4.88 us (17%)
  between operations  0.78 us (3%)
    ppermute x4, starting transfers between devices, swapped(): return lax.ppermute(x, axis, paired(size, odd))  8 us
    ppermute x4, waiting for transfers between devices, swapped(): return lax.ppermute(x, axis, paired(size, odd))  7.78 us
    all_to_all x1, starting transfers between devices, shards(): lax.all_to_all(tally.reshape(devices, chunks * 8, 128), ('gx', 'gy'), 0, 0)  6.32 us
    pallas_call x1, Pallas kernels, shards(): pl.pallas_call(functools.partial(first_kernel, rows, cols, chunks, copies...  2.48 us
    pallas_call x1, Pallas kernels, shards(): pl.pallas_call(functools.partial(fourth_kernel, rows, cols, chunks, copie...  1.28 us
    pallas_call x2, Pallas kernels, prepare(): pl.pallas_call(functools.partial(third_kernel, rows, cols, edges), out_sh...  0.99 us
  transfers between devices with their start and end apart: 5, of which 3 were waited for; matrix products, arithmetic and copies ran while one was open for 0% of the time, Pallas kernels for 4%

profile of v4, /device:TPU:9, one launch (start us, length us, event | category | flops | bytes accessed | tf_op | source)
XLA Modules:
  0.0 27.8 jit_solution(17078474191143866525)
XLA Ops:
  0.6 2.5 %pack.1 = (f32[240,128]{1,0:T(8,128)}, f32[240,128]{1,0:T(8,128)}, f32[32,1,8,128]{3,2,1,0:T(8,128)}) custom-call(f32[19,48,128]{2,1,0:T(8,128)} %bitcast.12, f32[48,128]{1,0:T(8,128)} %bitcast.17, s32[48,128]{1,0:T(8,128)} %bitcast.21, s32[48,128]{1,0:T(8,128)} %bitcast.25, s32[48,128]{1,0:T(8,128)} %bitcast.29), custom_call_target="tpu_custom_call" | custom-call | flops 2000000 | bytes 2000000 | tf_op jit(solution)/shard_map/pack/pallas_call | solution.py:601
  3.1 0.0 copy-start.7
  3.1 0.0 copy-start.6
  3.1 6.3 %all-to-all-start = ((f32[32,8,128]{2,1,0:T(8,128)}), f32[32,8,128]{2,1,0:T(8,128)S(1)}, u32[]{:S(2)}, u32[]{:S(2)}) async-start(f32[32,8,128]{2,1,0:T(8,128)} %bitcast.34), calls=%async_computation | async-start | bytes 262144 | tf_op jit(solution)/shard_map/all_to_all | solution.py:637
  9.5 0.0 copy-done.7
  9.5 1.2 %collective-permute-start = (f32[240,128]{1,0:T(8,128)S(1)}, f32[240,128]{1,0:T(8,128)S(1)}, u32[]{:S(2)}, u32[]{:S(2)}) collective-permute-start(f32[240,128]{1,0:T(8,128)S(1)} %copy-done.7), channel_id=1, source_target_pairs={{0,4},{4,0},{8,12},{12,8},{16,20},{20,16},{24,28},{28,24},{1,5},{5... | collective-permute-start | bytes 368648 | tf_op jit(solution)/shard_map/ppermute | solution.py:632
  10.7 0.0 copy-done.6
  10.7 0.0 copy-start
  10.7 0.0 copy-start.1
  10.7 0.0 copy-start.2
  10.7 0.0 copy-start.3
  10.7 0.0 copy-start.4
  10.8 2.1 %collective-permute-start.1 = (f32[240,128]{1,0:T(8,128)S(1)}, f32[240,128]{1,0:T(8,128)S(1)}, u32[]{:S(2)}, u32[]{:S(2)}) collective-permute-start(f32[240,128]{1,0:T(8,128)S(1)} %copy-done.6), channel_id=1, source_target_pairs={{4,8},{8,4},{12,16},{16,12},{20,24},{24,20},{5,9},{9,5},{13,17},{1... | collective-permute-start | bytes 368648 | tf_op jit(solution)/shard_map/ppermute | solution.py:632
  12.9 2.6 %collective-permute-done.refs_5_.across_even = f32[240,128]{1,0:T(8,128)S(1)} collective-permute-done((f32[240,128]{1,0:T(8,128)S(1)}, f32[240,128]{1,0:T(8,128)S(1)}, u32[]{:S(2)}, u32[]{:S(2)}) %collective-permute-start) | collective-permute-done | bytes 122912 | tf_op jit(solution)/shard_map/ppermute | solution.py:632
  15.5 2.4 %collective-permute-done.1.refs_6_.across_odd = f32[240,128]{1,0:T(8,128)S(1)} collective-permute-done((f32[240,128]{1,0:T(8,128)S(1)}, f32[240,128]{1,0:T(8,128)S(1)}, u32[]{:S(2)}, u32[]{:S(2)}) %collective-permute-start.1) | collective-permute-done | bytes 122912 | tf_op jit(solution)/shard_map/ppermute | solution.py:632
  17.9 0.0 copy-done
  17.9 0.0 copy-done.1
  17.9 0.0 copy-done.2
  17.9 0.0 copy-done.3
  17.9 0.0 copy-done.4
  17.9 0.1 relay.1
  18.1 1.6 %collective-permute-start.2 = (f32[264,128]{1,0:T(8,128)S(1)}, f32[264,128]{1,0:T(8,128)S(1)}, u32[]{:S(2)}, u32[]{:S(2)}) collective-permute-start(f32[264,128]{1,0:T(8,128)S(1)} %get-tuple-element.26), channel_id=1, source_target_pairs={{0,1},{1,0},{2,3},{3,2},{4,5},{5,4},{6,7},{7,6},{8,9},{9,8},{10,11... | collective-permute-start | bytes 405512 | tf_op jit(solution)/shard_map/ppermute | solution.py:632
  19.7 0.0 copy-start.5
  19.7 3.0 %collective-permute-start.3 = (f32[264,128]{1,0:T(8,128)S(1)}, f32[264,128]{1,0:T(8,128)S(1)}, u32[]{:S(2)}, u32[]{:S(2)}) collective-permute-start(f32[264,128]{1,0:T(8,128)S(1)} %get-tuple-element.27), channel_id=1, source_target_pairs={{1,2},{2,1},{5,6},{6,5},{9,10},{10,9},{13,14},{14,13},{17,18},{18,... | collective-permute-start | bytes 405512 | tf_op jit(solution)/shard_map/ppermute | solution.py:632
  22.7 0.0 copy-done.5
  22.7 0.6 %inner.1 = (f32[1,8,128]{2,1,0:T(8,128)S(1)}, f32[19,48,128]{2,1,0:T(8,128)S(1)}, f32[18,48,128]{2,1,0:T(8,128)S(1)}, f32[8,48,128]{2,1,0:T(8,128)S(1)}, f32[5,48,128]{2,1,0:T(8,128)S(1)}) custom-call(f32[912,128]{1,0:T(8,128)S(1)} %bitcast.14, f32[48,128]{1,0:T(8,128)S(1)} %bitcast.19, s32[48,128]{1,0:T(8,128)S(1)} %bitcast.23, s32[48,128]{1,0:T(8,128)S(1)} %bitcast.27, ...), custom_call_target="tpu_custom_call" | custom-call | flops 5000000 | bytes 3000000 | tf_op jit(solution)/shard_map/inner/pallas_call | solution.py:666
  23.3 0.0 collective-permute-done.2.refs_7_
  23.3 2.8 %collective-permute-done.3.refs_8_ = f32[264,128]{1,0:T(8,128)S(1)} collective-permute-done((f32[264,128]{1,0:T(8,128)S(1)}, f32[264,128]{1,0:T(8,128)S(1)}, u32[]{:S(2)}, u32[]{:S(2)}) %collective-permute-start.3) | collective-permute-done | bytes 135200 | tf_op jit(solution)/shard_map/ppermute | solution.py:632
  26.1 0.4 %edges.1 = (f32[19,16,128]{2,1,0:T(8,128)S(1)}, f32[18,16,128]{2,1,0:T(8,128)S(1)}, f32[8,32,128]{2,1,0:T(8,128)S(1)}, f32[5,32,128]{2,1,0:T(8,128)S(1)}) custom-call(f32[912,128]{1,0:T(8,128)S(1)} %bitcast.15, f32[48,128]{1,0:T(8,128)S(1)} %bitcast.20, s32[48,128]{1,0:T(8,128)S(1)} %bitcast.24, s32[48,128]{1,0:T(8,128)S(1)} %bitcast.28, ...), custom_call_target="tpu_custom_call" | custom-call | flops 5000000 | bytes 3000000 | tf_op jit(solution)/shard_map/edges/pallas_call | solution.py:666
  26.5 0.0 all-to-all-done
  26.5 1.3 %settle.1 = (f32[912,128]{1,0:T(8,128)}, f32[48,128]{1,0:T(8,128)}, f32[1,96]{1,0:T(1,128)}) custom-call(f32[19,48,128]{2,1,0:T(8,128)S(1)} %get-tuple-element.22.inner_fixed, f32[18,48,128]{2,1,0:T(8,128)S(1)} %get-tuple-element.23.inner_scaling, f32[8,48,128]{2,1,0:T(8,128)S(1)} %get-tuple-element.24.inner_linear, ...), custom_call_target="tpu_custom_call" | custom-call | flops 2000000 | bytes 3000000 | tf_op jit(solution)/shard_map/settle/pallas_call | solution.py:682
  (1 shorter events, 0.0 us)
Async XLA Ops:
  3.1 6.3 %copy-start.7 = (f32[240,128]{1,0:T(8,128)S(1)}, f32[240,128]{1,0:T(8,128)}, u32[]{:S(2)}) copy-start(f32[240,128]{1,0:T(8,128)} %get-tuple-element.20) | copy-start | bytes 368644
  3.1 7.6 %copy-start.6 = (f32[240,128]{1,0:T(8,128)S(1)}, f32[240,128]{1,0:T(8,128)}, u32[]{:S(2)}) copy-start(f32[240,128]{1,0:T(8,128)} %get-tuple-element.21) | copy-start | bytes 368644
  3.1 23.4 %all-to-all-start = ((f32[32,8,128]{2,1,0:T(8,128)}), f32[32,8,128]{2,1,0:T(8,128)S(1)}, u32[]{:S(2)}, u32[]{:S(2)}) async-start(f32[32,8,128]{2,1,0:T(8,128)} %bitcast.34), calls=%async_computation | async-start | bytes 262144 | tf_op jit(solution)/shard_map/all_to_all | solution.py:637
  9.5 6.0 %collective-permute-start = (f32[240,128]{1,0:T(8,128)S(1)}, f32[240,128]{1,0:T(8,128)S(1)}, u32[]{:S(2)}, u32[]{:S(2)}) collective-permute-start(f32[240,128]{1,0:T(8,128)S(1)} %copy-done.7), channel_id=1, source_target_pairs={{0,4},{4,0},{8,12},{12,8},{16,20},{20,16},{24,28},{28,24},{1,5},{5... | collective-permute-start | bytes 368648 | tf_op jit(solution)/shard_map/ppermute | solution.py:632
  10.7 7.2 %copy-start = (f32[19,6,8,128]{3,2,1,0:T(8,128)S(1)}, f32[19,6,8,128]{3,2,1,0:T(8,128)}, u32[]{:S(2)}) copy-start(f32[19,6,8,128]{3,2,1,0:T(8,128)} %param.6) | copy-start | bytes 1400836
  10.7 7.2 %copy-start.1 = (f32[6,8,128]{2,1,0:T(8,128)S(1)}, f32[6,8,128]{2,1,0:T(8,128)}, u32[]{:S(2)}) copy-start(f32[6,8,128]{2,1,0:T(8,128)} %param.7) | copy-start | bytes 73732
  10.7 7.2 %copy-start.2 = (s32[6,8,128]{2,1,0:T(8,128)S(1)}, s32[6,8,128]{2,1,0:T(8,128)}, u32[]{:S(2)}) copy-start(s32[6,8,128]{2,1,0:T(8,128)} %param.8) | copy-start | bytes 73732
  10.7 7.2 %copy-start.3 = (s32[6,8,128]{2,1,0:T(8,128)S(1)}, s32[6,8,128]{2,1,0:T(8,128)}, u32[]{:S(2)}) copy-start(s32[6,8,128]{2,1,0:T(8,128)} %param.9) | copy-start | bytes 73732
  10.7 7.2 %copy-start.4 = (s32[6,8,128]{2,1,0:T(8,128)S(1)}, s32[6,8,128]{2,1,0:T(8,128)}, u32[]{:S(2)}) copy-start(s32[6,8,128]{2,1,0:T(8,128)} %param.10) | copy-start | bytes 73732
  10.8 7.1 %collective-permute-start.1 = (f32[240,128]{1,0:T(8,128)S(1)}, f32[240,128]{1,0:T(8,128)S(1)}, u32[]{:S(2)}, u32[]{:S(2)}) collective-permute-start(f32[240,128]{1,0:T(8,128)S(1)} %copy-done.6), channel_id=1, source_target_pairs={{4,8},{8,4},{12,16},{16,12},{20,24},{24,20},{5,9},{9,5},{13,17},{1... | collective-permute-start | bytes 368648 | tf_op jit(solution)/shard_map/ppermute | solution.py:632
  18.1 5.2 %collective-permute-start.2 = (f32[264,128]{1,0:T(8,128)S(1)}, f32[264,128]{1,0:T(8,128)S(1)}, u32[]{:S(2)}, u32[]{:S(2)}) collective-permute-start(f32[264,128]{1,0:T(8,128)S(1)} %get-tuple-element.26), channel_id=1, source_target_pairs={{0,1},{1,0},{2,3},{3,2},{4,5},{5,4},{6,7},{7,6},{8,9},{9,8},{10,11... | collective-permute-start | bytes 405512 | tf_op jit(solution)/shard_map/ppermute | solution.py:632
  19.7 3.0 %copy-start.5 = (f32[96]{0:T(128)S(1)}, f32[96]{0:T(128)}, u32[]{:S(2)}) copy-start(f32[96]{0:T(128)} %param.11) | copy-start | bytes 1156
  19.7 6.5 %collective-permute-start.3 = (f32[264,128]{1,0:T(8,128)S(1)}, f32[264,128]{1,0:T(8,128)S(1)}, u32[]{:S(2)}, u32[]{:S(2)}) collective-permute-start(f32[264,128]{1,0:T(8,128)S(1)} %get-tuple-element.27), channel_id=1, source_target_pairs={{1,2},{2,1},{5,6},{6,5},{9,10},{10,9},{13,14},{14,13},{17,18},{18,... | collective-permute-start | bytes 405512 | tf_op jit(solution)/shard_map/ppermute | solution.py:632

commit v5 on v4

--- a/solution.py
+++ b/solution.py
@@ -173,8 +173,11 @@
 
     for chunk in range(chunks):
         summed = count(chunk)
-        for k in range(copies):
-            tally[k, chunk] = summed
+        if chunks == 1:
+            tally[...] = jnp.broadcast_to(summed[0:1], tally.shape)
+        else:
+            for k in range(copies):
+                tally[pl.ds(k * chunks + chunk, 1), :] = summed[0:1]
     send(2, tally, tally_out)
     for copy in sent:
         copy.wait()
@@ -466,9 +469,8 @@
     block = rows * cols
     tall = rows + 2
     for chunk in range(chunks):
-        volume = tally[0, chunk]
-        for k in range(1, copies):
-            volume = volume + tally[k, chunk]
+        rows_of = pl.ds(chunk, copies, stride=chunks) if chunks > 1 else pl.ds(0, copies)
+        volume = jnp.sum(tally[rows_of, :], axis=0, keepdims=True)
         here = min(128, labels - chunk * 128)
         gas = AMBIENT + rest[chunk] / jnp.maximum(volume, 1.0)
         gas_stage[0:1, pl.ds(chunk * 128, here)] = gas[0:1, :here]
@@ -596,7 +598,7 @@
     packed = [
         (end_rows, depth),
         (end_rows, depth),
-        (copies, chunks, 8, 128),
+        (copies * chunks, 128),
     ]
     across_even, across_odd, tally = pl.pallas_call(
         functools.partial(first_kernel, rows, cols, chunks, copies),
@@ -634,12 +636,9 @@
     across_odd = swapped(across_odd, "gx", gx_size, True)
     across_even = swapped(across_even, "gx", gx_size, False)
     if direct:
-        tallies = lax.all_to_all(
-            tally.reshape(devices, chunks * 8, 128), ("gx", "gy"), 0, 0
-        ).reshape(devices, chunks, 8, 128)
+        tallies = lax.all_to_all(tally, ("gx", "gy"), 0, 0, tiled=True)
     else:
-        tallies = lax.psum(tally[0, :, 0], ("gx", "gy"))
-        tallies = jnp.broadcast_to(tallies[None, :, None, :], (1, chunks, 8, 128))
+        tallies = lax.psum(tally, ("gx", "gy"))
 
     beside_even, beside_odd = pl.pallas_call(
         functools.partial(second_kernel, rows, cols),

time: 28 us -> 30.4 us (1.086)
  the two profiles are of different devices: /device:TPU:9 before, /device:TPU:0 now
where the time goes in v5:
time: 30.4 us; the launch traced here: 30.2 us
  starting transfers between devices  15.8 us (52%)
  waiting for transfers between devices  8.11 us (27%)
  Pallas kernels  4.8 us (16%)
  between operations  0.76 us (2%)
  local copies, waits for them, and re-layouts  0.67 us (2%)
    all_to_all x1, starting transfers between devices, shards(): tallies = lax.all_to_all(tally, ('gx', 'gy'), 0, 0, tiled=True)  11.3 us
    all_to_all x1, waiting for transfers between devices, shards(): tallies = lax.all_to_all(tally, ('gx', 'gy'), 0, 0, tiled=True)  5.41 us
    ppermute x4, starting transfers between devices, swapped(): return lax.ppermute(x, axis, paired(size, odd))  4.56 us
    ppermute x4, waiting for transfers between devices, swapped(): return lax.ppermute(x, axis, paired(size, odd))  2.7 us
    pallas_call x1, Pallas kernels, shards(): pl.pallas_call(functools.partial(first_kernel, rows, cols, chunks, copies...  2.42 us
    pallas_call x1, Pallas kernels, shards(): pl.pallas_call(functools.partial(fourth_kernel, rows, cols, chunks, copie...  1.25 us
    pallas_call x2, Pallas kernels, prepare(): pl.pallas_call(functools.partial(third_kernel, rows, cols, edges), out_sh...  1 us
    unnamed x12, local copies, waits for them, and re-layouts  0.67 us
  transfers between devices with their start and end apart: 5, of which 2 were waited for; matrix products, arithmetic and copies ran while one was open for 0% of the time, Pallas kernels for 3%

profile of v5, /device:TPU:0, one launch (start us, length us, event | category | flops | bytes accessed | tf_op | source)
XLA Modules:
  0.0 30.2 jit_solution(6216033049013800475)
XLA Ops:
  0.6 2.4 %pack.1 = (f32[240,128]{1,0:T(8,128)}, f32[240,128]{1,0:T(8,128)}, f32[32,128]{1,0:T(8,128)}) custom-call(f32[19,48,128]{2,1,0:T(8,128)} %bitcast.14, f32[48,128]{1,0:T(8,128)} %bitcast.18, s32[48,128]{1,0:T(8,128)} %bitcast.22, s32[48,128]{1,0:T(8,128)} %bitcast.26, s32[48,128]{1,0:T(8,128)} %bitcast.30), custom_call_target="tpu_custom_call" | custom-call | flops 2000000 | bytes 2000000 | tf_op jit(solution)/shard_map/pack/pallas_call | solution.py:603
  3.1 3.0 %collective-permute-start = (f32[240,128]{1,0:T(8,128)}, f32[240,128]{1,0:T(8,128)S(1)}, u32[]{:S(2)}, u32[]{:S(2)}) collective-permute-start(f32[240,128]{1,0:T(8,128)} %get-tuple-element.20), channel_id=1, source_target_pairs={{0,4},{4,0},{8,12},{12,8},{16,20},{20,16},{24,28},{28,24},{1,5},{5... | collective-permute-start | bytes 368648 | tf_op jit(solution)/shard_map/ppermute | solution.py:634
  6.1 0.0 copy-start
  6.1 0.0 copy-start.1
  6.1 0.0 copy-start.2
  6.1 0.0 copy-start.3
  6.1 0.0 copy-start.4
  6.1 0.8 %collective-permute-start.1 = (f32[240,128]{1,0:T(8,128)}, f32[240,128]{1,0:T(8,128)S(1)}, u32[]{:S(2)}, u32[]{:S(2)}) collective-permute-start(f32[240,128]{1,0:T(8,128)} %get-tuple-element.21), channel_id=1, source_target_pairs={{4,8},{8,4},{12,16},{16,12},{20,24},{24,20},{5,9},{9,5},{13,17},{1... | collective-permute-start | bytes 368648 | tf_op jit(solution)/shard_map/ppermute | solution.py:634
  6.9 2.7 %collective-permute-done.refs_5_.across_even = f32[240,128]{1,0:T(8,128)S(1)} collective-permute-done((f32[240,128]{1,0:T(8,128)}, f32[240,128]{1,0:T(8,128)S(1)}, u32[]{:S(2)}, u32[]{:S(2)}) %collective-permute-start) | collective-permute-done | bytes 122912 | tf_op jit(solution)/shard_map/ppermute | solution.py:634
  9.6 0.0 collective-permute-done.1.refs_6_.across_odd
  9.6 0.0 copy-done
  9.6 0.0 copy-done.1
  9.6 0.0 copy-done.2
  9.6 0.0 copy-done.3
  9.6 0.0 copy-done.4
  9.6 0.1 relay.1
  9.8 0.1 collective-permute-start.2
  9.9 0.7 %collective-permute-start.3 = (f32[264,128]{1,0:T(8,128)S(1)}, f32[264,128]{1,0:T(8,128)S(1)}, u32[]{:S(2)}, u32[]{:S(2)}) collective-permute-start(f32[264,128]{1,0:T(8,128)S(1)} %get-tuple-element.27), channel_id=1, source_target_pairs={{1,2},{2,1},{5,6},{6,5},{9,10},{10,9},{13,14},{14,13},{17,18},{18,... | collective-permute-start | bytes 405512 | tf_op jit(solution)/shard_map/ppermute | solution.py:634
  10.5 11.3 %all-to-all-start = ((f32[32,1,128]{2,1,0:T(1,128)}), f32[32,1,128]{2,1,0:T(1,128)S(1)}, u32[]{:S(2)}, u32[]{:S(2)}) async-start(f32[32,1,128]{2,1,0:T(1,128)} %bitcast.8), calls=%async_computation | async-start | bytes 32768 | tf_op jit(solution)/shard_map/all_to_all | solution.py:639
  21.8 0.0 copy-start.5
  21.8 0.6 %copy-done.5 = f32[96]{0:T(128)S(1)} copy-done((f32[96]{0:T(128)S(1)}, f32[96]{0:T(128)}, u32[]{:S(2)}) %copy-start.5) | copy-done | bytes 408
  22.5 0.6 %inner.1 = (f32[1,8,128]{2,1,0:T(8,128)S(1)}, f32[19,48,128]{2,1,0:T(8,128)S(1)}, f32[18,48,128]{2,1,0:T(8,128)S(1)}, f32[8,48,128]{2,1,0:T(8,128)S(1)}, f32[5,48,128]{2,1,0:T(8,128)S(1)}) custom-call(f32[912,128]{1,0:T(8,128)S(1)} %bitcast.16, f32[48,128]{1,0:T(8,128)S(1)} %bitcast.20, s32[48,128]{1,0:T(8,128)S(1)} %bitcast.24, s32[48,128]{1,0:T(8,128)S(1)} %bitcast.28, ...), custom_call_target="tpu_custom_call" | custom-call | flops 5000000 | bytes 3000000 | tf_op jit(solution)/shard_map/inner/pallas_call | solution.py:665
  23.1 0.0 collective-permute-done.2.refs_7_
  23.1 0.0 collective-permute-done.3.refs_8_
  23.1 0.4 %edges.1 = (f32[19,16,128]{2,1,0:T(8,128)S(1)}, f32[18,16,128]{2,1,0:T(8,128)S(1)}, f32[8,32,128]{2,1,0:T(8,128)S(1)}, f32[5,32,128]{2,1,0:T(8,128)S(1)}) custom-call(f32[912,128]{1,0:T(8,128)S(1)} %bitcast.17, f32[48,128]{1,0:T(8,128)S(1)} %bitcast.21, s32[48,128]{1,0:T(8,128)S(1)} %bitcast.25, s32[48,128]{1,0:T(8,128)S(1)} %bitcast.29, ...), custom_call_target="tpu_custom_call" | custom-call | flops 5000000 | bytes 3000000 | tf_op jit(solution)/shard_map/edges/pallas_call | solution.py:665
  23.5 5.4 %all-to-all-done = f32[32,1,128]{2,1,0:T(1,128)S(1)} async-done(((f32[32,1,128]{2,1,0:T(1,128)}), f32[32,1,128]{2,1,0:T(1,128)S(1)}, u32[]{:S(2)}, u32[]{:S(2)}) %all-to-all-start) | async-done | bytes 16416 | tf_op jit(solution)/shard_map/all_to_all | solution.py:639
  28.9 1.3 %settle.1 = (f32[912,128]{1,0:T(8,128)}, f32[48,128]{1,0:T(8,128)}, f32[1,96]{1,0:T(1,128)}) custom-call(f32[19,48,128]{2,1,0:T(8,128)S(1)} %get-tuple-element.22.inner_fixed, f32[18,48,128]{2,1,0:T(8,128)S(1)} %get-tuple-element.23.inner_scaling, f32[8,48,128]{2,1,0:T(8,128)S(1)} %get-tuple-element.24.inner_linear, ...), custom_call_target="tpu_custom_call" | custom-call | flops 2000000 | bytes 3000000 | tf_op jit(solution)/shard_map/settle/pallas_call | solution.py:681
  (1 shorter events, 0.0 us)
Async XLA Ops:
  3.1 6.6 %collective-permute-start = (f32[240,128]{1,0:T(8,128)}, f32[240,128]{1,0:T(8,128)S(1)}, u32[]{:S(2)}, u32[]{:S(2)}) collective-permute-start(f32[240,128]{1,0:T(8,128)} %get-tuple-element.20), channel_id=1, source_target_pairs={{0,4},{4,0},{8,12},{12,8},{16,20},{20,16},{24,28},{28,24},{1,5},{5... | collective-permute-start | bytes 368648 | tf_op jit(solution)/shard_map/ppermute | solution.py:634
  6.1 3.5 %copy-start = (f32[19,6,8,128]{3,2,1,0:T(8,128)S(1)}, f32[19,6,8,128]{3,2,1,0:T(8,128)}, u32[]{:S(2)}) copy-start(f32[19,6,8,128]{3,2,1,0:T(8,128)} %param.6) | copy-start | bytes 1400836
  6.1 3.5 %copy-start.1 = (f32[6,8,128]{2,1,0:T(8,128)S(1)}, f32[6,8,128]{2,1,0:T(8,128)}, u32[]{:S(2)}) copy-start(f32[6,8,128]{2,1,0:T(8,128)} %param.7) | copy-start | bytes 73732
  6.1 3.5 %copy-start.2 = (s32[6,8,128]{2,1,0:T(8,128)S(1)}, s32[6,8,128]{2,1,0:T(8,128)}, u32[]{:S(2)}) copy-start(s32[6,8,128]{2,1,0:T(8,128)} %param.8) | copy-start | bytes 73732
  6.1 3.5 %copy-start.3 = (s32[6,8,128]{2,1,0:T(8,128)S(1)}, s32[6,8,128]{2,1,0:T(8,128)}, u32[]{:S(2)}) copy-start(s32[6,8,128]{2,1,0:T(8,128)} %param.9) | copy-start | bytes 73732
  6.1 3.6 %copy-start.4 = (s32[6,8,128]{2,1,0:T(8,128)S(1)}, s32[6,8,128]{2,1,0:T(8,128)}, u32[]{:S(2)}) copy-start(s32[6,8,128]{2,1,0:T(8,128)} %param.10) | copy-start | bytes 73732
  6.1 3.5 %collective-permute-start.1 = (f32[240,128]{1,0:T(8,128)}, f32[240,128]{1,0:T(8,128)S(1)}, u32[]{:S(2)}, u32[]{:S(2)}) collective-permute-start(f32[240,128]{1,0:T(8,128)} %get-tuple-element.21), channel_id=1, source_target_pairs={{4,8},{8,4},{12,16},{16,12},{20,24},{24,20},{5,9},{9,5},{13,17},{1... | collective-permute-start | bytes 368648 | tf_op jit(solution)/shard_map/ppermute | solution.py:634
  9.8 13.3 %collective-permute-start.2 = (f32[264,128]{1,0:T(8,128)S(1)}, f32[264,128]{1,0:T(8,128)S(1)}, u32[]{:S(2)}, u32[]{:S(2)}) collective-permute-start(f32[264,128]{1,0:T(8,128)S(1)} %get-tuple-element.26), channel_id=1, source_target_pairs={{0,1},{1,0},{2,3},{3,2},{4,5},{5,4},{6,7},{7,6},{8,9},{9,8},{10,11... | collective-permute-start | bytes 405512 | tf_op jit(solution)/shard_map/ppermute | solution.py:634
  9.9 13.2 %collective-permute-start.3 = (f32[264,128]{1,0:T(8,128)S(1)}, f32[264,128]{1,0:T(8,128)S(1)}, u32[]{:S(2)}, u32[]{:S(2)}) collective-permute-start(f32[264,128]{1,0:T(8,128)S(1)} %get-tuple-element.27), channel_id=1, source_target_pairs={{1,2},{2,1},{5,6},{6,5},{9,10},{10,9},{13,14},{14,13},{17,18},{18,... | collective-permute-start | bytes 405512 | tf_op jit(solution)/shard_map/ppermute | solution.py:634
  10.5 18.4 %all-to-all-start = ((f32[32,1,128]{2,1,0:T(1,128)}), f32[32,1,128]{2,1,0:T(1,128)S(1)}, u32[]{:S(2)}, u32[]{:S(2)}) async-start(f32[32,1,128]{2,1,0:T(1,128)} %bitcast.8), calls=%async_computation | async-start | bytes 32768 | tf_op jit(solution)/shard_map/all_to_all | solution.py:639
  21.8 0.7 %copy-start.5 = (f32[96]{0:T(128)S(1)}, f32[96]{0:T(128)}, u32[]{:S(2)}) copy-start(f32[96]{0:T(128)} %param.11) | copy-start | bytes 1156

commit v6 on v5

--- a/solution.py
+++ b/solution.py
@@ -79,7 +79,7 @@
 
 
 def first_kernel(
-    rows, cols, chunks, copies,
+    rows, cols, chunks, copies, label_span,
     pops_in, mass_in, flags_in, bubble_in, conversion_in,
     across_even_out, across_odd_out, tally_out,
     aux, pops, mass, flags, bubble, conversion, sems,
@@ -111,7 +111,8 @@
 
     contributions = []
     lane_count = mass.shape[-1]
-    label_rows = lax.broadcasted_iota(jnp.int32, (128, lane_count), 0)
+    tall_labels = 128 if chunks > 1 else label_span
+    label_rows = lax.broadcasted_iota(jnp.int32, (tall_labels, lane_count), 0)
 
     def count_row(total, r, chunk):
         for c in range(cols):
@@ -160,21 +161,25 @@
 
 
     def count(chunk):
-        total = jnp.zeros((128, lane_count), jnp.float32)
+        total = jnp.zeros((tall_labels, lane_count), jnp.float32)
         for r in range(rows):
             total = count_row(total, r, chunk)
+        high = total.astype(jnp.bfloat16)
+        left = total - high.astype(jnp.float32)
+        middle = left.astype(jnp.bfloat16)
+        low = (left - middle.astype(jnp.float32)).astype(jnp.bfloat16)
         return lax.dot_general(
-            jnp.ones((8, lane_count), jnp.float32),
-            total,
+            jnp.ones((16, 3 * lane_count), jnp.bfloat16),
+            jnp.concatenate([high, middle, low], axis=1),
             (((1,), (1,)), ((), ())),
-            precision=lax.Precision.HIGHEST,
             preferred_element_type=jnp.float32,
         )
 
     for chunk in range(chunks):
         summed = count(chunk)
         if chunks == 1:
-            tally[...] = jnp.broadcast_to(summed[0:1], tally.shape)
+            tally[...] = jnp.zeros(tally.shape, jnp.float32)
+            tally[:, pl.ds(0, tall_labels)] = jnp.broadcast_to(summed[0:1], (copies, tall_labels))
         else:
             for k in range(copies):
                 tally[pl.ds(k * chunks + chunk, 1), :] = summed[0:1]
@@ -524,36 +529,6 @@
         ]
         states.append((gas, velocity, rest_part(velocity), jnp.where(dry, 0.0, RELAX * density)))
 
-    relaxed_copies = []
-
-    def leave(q):
-        copy = pltpu.make_async_copy(
-            relaxed_stage.at[pl.ds((q * tall + 1) * cols, block), :],
-            relaxed_out.at[pl.ds(q * block, block), :],
-            wet_sem.at[q],
-        )
-        copy.start()
-        relaxed_copies.append(copy)
-
-    def put(q, c, value):
-        relaxed_stage[pl.ds(q * tall * cols + c, tall, stride=cols), :] = value
-
-    for c, (_, _, still, scaled) in enumerate(states):
-        (fixed, _, _, _), _, column = place(c)
-        put(0, c, fixed[0, column, :] + (scaled * WEIGHTS[0]) * still)
-    leave(0)
-    for first in range(1, LANES, 2):
-        for c, (gas, velocity, still, scaled) in enumerate(states):
-            (fixed, scaling, _, _), _, column = place(c)
-            project = projection(velocity, first)
-            even = still + 4.5 * project * project
-            odd = 3.0 * project
-            share = scaled * WEIGHTS[first]
-            for q, part in ((first, even + odd), (first + 1, even - odd)):
-                put(q, c, fixed[q, column, :] + gas * scaling[q - 1, column, :] + share * part)
-        leave(first)
-        leave(first + 1)
-
     portions = [settled(-1)[-1]] + portions + [settled(cols)[-1]]
     ends = [roll(p, 1) + roll(p, -1) for p in portions]
     full = [p + e for p, e in zip(portions, ends)]
@@ -571,6 +546,36 @@
         mass_stage.at[pl.ds(cols, block), :], new_mass_out, mass_sem
     )
     mass_copy.start()
+    relaxed_copies = []
+
+    def leave(q):
+        copy = pltpu.make_async_copy(
+            relaxed_stage.at[pl.ds((q * tall + 1) * cols, block), :],
+            relaxed_out.at[pl.ds(q * block, block), :],
+            wet_sem.at[q],
+        )
+        copy.start()
+        relaxed_copies.append(copy)
+
+    def put(q, c, value):
+        relaxed_stage[pl.ds(q * tall * cols + c, tall, stride=cols), :] = value
+
+    for c, (_, _, still, scaled) in enumerate(states):
+        (fixed, _, _, _), _, column = place(c)
+        put(0, c, fixed[0, column, :] + (scaled * WEIGHTS[0]) * still)
+    leave(0)
+    for first in range(1, LANES, 2):
+        for c, (gas, velocity, still, scaled) in enumerate(states):
+            (fixed, scaling, _, _), _, column = place(c)
+            project = projection(velocity, first)
+            even = still + 4.5 * project * project
+            odd = 3.0 * project
+            share = scaled * WEIGHTS[first]
+            for q, part in ((first, even + odd), (first + 1, even - odd)):
+                put(q, c, fixed[q, column, :] + gas * scaling[q - 1, column, :] + share * part)
+        leave(first)
+        leave(first + 1)
+
     for copy in relaxed_copies:
         copy.wait()
     mass_copy.wait()
@@ -601,7 +606,7 @@
         (copies * chunks, 128),
     ]
     across_even, across_odd, tally = pl.pallas_call(
-        functools.partial(first_kernel, rows, cols, chunks, copies),
+        functools.partial(first_kernel, rows, cols, chunks, copies, min(128, -(-labels // 8) * 8)),
         out_shape=[jax.ShapeDtypeStruct(shape, f32) for shape in packed],
         in_specs=[hbm] * 5,
         out_specs=[hbm] * len(packed),

time: 30.4 us -> 30.2 us (level)
  no operation moved by 1% of the time
where the time goes in v6:
time: 30.2 us; the launch traced here: 30 us
  starting transfers between devices  15.8 us (52%)
  waiting for transfers between devices  8.11 us (27%)
  Pallas kernels  4.62 us (15%)
  between operations  0.76 us (3%)
  local copies, waits for them, and re-layouts  0.67 us (2%)
    all_to_all x1, starting transfers between devices, shards(): tallies = lax.all_to_all(tally, ('gx', 'gy'), 0, 0, tiled=True)  11.3 us
    all_to_all x1, waiting for transfers between devices, shards(): tallies = lax.all_to_all(tally, ('gx', 'gy'), 0, 0, tiled=True)  5.41 us
    ppermute x4, starting transfers between devices, swapped(): return lax.ppermute(x, axis, paired(size, odd))  4.56 us
    ppermute x4, waiting for transfers between devices, swapped(): return lax.ppermute(x, axis, paired(size, odd))  2.7 us
    pallas_call x1, Pallas kernels, shards(): pl.pallas_call(functools.partial(first_kernel, rows, cols, chunks, copies...  2.24 us
    pallas_call x1, Pallas kernels, shards(): pl.pallas_call(functools.partial(fourth_kernel, rows, cols, chunks, copie...  1.25 us
    pallas_call x2, Pallas kernels, prepare(): pl.pallas_call(functools.partial(third_kernel, rows, cols, edges), out_sh...  1 us
    unnamed x12, local copies, waits for them, and re-layouts  0.67 us
  transfers between devices with their start and end apart: 5, of which 2 were waited for; matrix products, arithmetic and copies ran while one was open for 0% of the time, Pallas kernels for 3%

profile of v6, /device:TPU:0, one launch (start us, length us, event | category | flops | bytes accessed | tf_op | source)
XLA Modules:
  0.0 30.0 jit_solution(6598760400559398774)
XLA Ops:
  0.6 2.2 %pack.1 = (f32[240,128]{1,0:T(8,128)}, f32[240,128]{1,0:T(8,128)}, f32[32,128]{1,0:T(8,128)}) custom-call(f32[19,48,128]{2,1,0:T(8,128)} %bitcast.14, f32[48,128]{1,0:T(8,128)} %bitcast.18, s32[48,128]{1,0:T(8,128)} %bitcast.22, s32[48,128]{1,0:T(8,128)} %bitcast.26, s32[48,128]{1,0:T(8,128)} %bitcast.30), custom_call_target="tpu_custom_call" | custom-call | flops 2000000 | bytes 2000000 | tf_op jit(solution)/shard_map/pack/pallas_call | solution.py:608
  2.9 3.0 %collective-permute-start = (f32[240,128]{1,0:T(8,128)}, f32[240,128]{1,0:T(8,128)S(1)}, u32[]{:S(2)}, u32[]{:S(2)}) collective-permute-start(f32[240,128]{1,0:T(8,128)} %get-tuple-element.20), channel_id=1, source_target_pairs={{0,4},{4,0},{8,12},{12,8},{16,20},{20,16},{24,28},{28,24},{1,5},{5... | collective-permute-start | bytes 368648 | tf_op jit(solution)/shard_map/ppermute | solution.py:639
  5.9 0.0 copy-start
  5.9 0.0 copy-start.1
  5.9 0.0 copy-start.2
  5.9 0.0 copy-start.3
  5.9 0.0 copy-start.4
  5.9 0.8 %collective-permute-start.1 = (f32[240,128]{1,0:T(8,128)}, f32[240,128]{1,0:T(8,128)S(1)}, u32[]{:S(2)}, u32[]{:S(2)}) collective-permute-start(f32[240,128]{1,0:T(8,128)} %get-tuple-element.21), channel_id=1, source_target_pairs={{4,8},{8,4},{12,16},{16,12},{20,24},{24,20},{5,9},{9,5},{13,17},{1... | collective-permute-start | bytes 368648 | tf_op jit(solution)/shard_map/ppermute | solution.py:639
  6.7 2.7 %collective-permute-done.refs_5_.across_even = f32[240,128]{1,0:T(8,128)S(1)} collective-permute-done((f32[240,128]{1,0:T(8,128)}, f32[240,128]{1,0:T(8,128)S(1)}, u32[]{:S(2)}, u32[]{:S(2)}) %collective-permute-start) | collective-permute-done | bytes 122912 | tf_op jit(solution)/shard_map/ppermute | solution.py:639
  9.4 0.0 collective-permute-done.1.refs_6_.across_odd
  9.4 0.0 copy-done
  9.4 0.0 copy-done.1
  9.4 0.0 copy-done.2
  9.4 0.0 copy-done.3
  9.5 0.0 copy-done.4
  9.5 0.1 relay.1
  9.6 0.1 collective-permute-start.2
  9.7 0.7 %collective-permute-start.3 = (f32[264,128]{1,0:T(8,128)S(1)}, f32[264,128]{1,0:T(8,128)S(1)}, u32[]{:S(2)}, u32[]{:S(2)}) collective-permute-start(f32[264,128]{1,0:T(8,128)S(1)} %get-tuple-element.27), channel_id=1, source_target_pairs={{1,2},{2,1},{5,6},{6,5},{9,10},{10,9},{13,14},{14,13},{17,18},{18,... | collective-permute-start | bytes 405512 | tf_op jit(solution)/shard_map/ppermute | solution.py:639
  10.4 11.3 %all-to-all-start = ((f32[32,1,128]{2,1,0:T(1,128)}), f32[32,1,128]{2,1,0:T(1,128)S(1)}, u32[]{:S(2)}, u32[]{:S(2)}) async-start(f32[32,1,128]{2,1,0:T(1,128)} %bitcast.8), calls=%async_computation | async-start | bytes 32768 | tf_op jit(solution)/shard_map/all_to_all | solution.py:644
  21.6 0.0 copy-start.5
  21.6 0.6 %copy-done.5 = f32[96]{0:T(128)S(1)} copy-done((f32[96]{0:T(128)S(1)}, f32[96]{0:T(128)}, u32[]{:S(2)}) %copy-start.5) | copy-done | bytes 408
  22.3 0.6 %inner.1 = (f32[1,8,128]{2,1,0:T(8,128)S(1)}, f32[19,48,128]{2,1,0:T(8,128)S(1)}, f32[18,48,128]{2,1,0:T(8,128)S(1)}, f32[8,48,128]{2,1,0:T(8,128)S(1)}, f32[5,48,128]{2,1,0:T(8,128)S(1)}) custom-call(f32[912,128]{1,0:T(8,128)S(1)} %bitcast.16, f32[48,128]{1,0:T(8,128)S(1)} %bitcast.20, s32[48,128]{1,0:T(8,128)S(1)} %bitcast.24, s32[48,128]{1,0:T(8,128)S(1)} %bitcast.28, ...), custom_call_target="tpu_custom_call" | custom-call | flops 5000000 | bytes 3000000 | tf_op jit(solution)/shard_map/inner/pallas_call | solution.py:670
  22.9 0.0 collective-permute-done.2.refs_7_
  22.9 0.0 collective-permute-done.3.refs_8_
  22.9 0.4 %edges.1 = (f32[19,16,128]{2,1,0:T(8,128)S(1)}, f32[18,16,128]{2,1,0:T(8,128)S(1)}, f32[8,32,128]{2,1,0:T(8,128)S(1)}, f32[5,32,128]{2,1,0:T(8,128)S(1)}) custom-call(f32[912,128]{1,0:T(8,128)S(1)} %bitcast.17, f32[48,128]{1,0:T(8,128)S(1)} %bitcast.21, s32[48,128]{1,0:T(8,128)S(1)} %bitcast.25, s32[48,128]{1,0:T(8,128)S(1)} %bitcast.29, ...), custom_call_target="tpu_custom_call" | custom-call | flops 5000000 | bytes 3000000 | tf_op jit(solution)/shard_map/edges/pallas_call | solution.py:670
  23.3 5.4 %all-to-all-done = f32[32,1,128]{2,1,0:T(1,128)S(1)} async-done(((f32[32,1,128]{2,1,0:T(1,128)}), f32[32,1,128]{2,1,0:T(1,128)S(1)}, u32[]{:S(2)}, u32[]{:S(2)}) %all-to-all-start) | async-done | bytes 16416 | tf_op jit(solution)/shard_map/all_to_all | solution.py:644
  28.7 1.3 %settle.1 = (f32[912,128]{1,0:T(8,128)}, f32[48,128]{1,0:T(8,128)}, f32[1,96]{1,0:T(1,128)}) custom-call(f32[19,48,128]{2,1,0:T(8,128)S(1)} %get-tuple-element.22.inner_fixed, f32[18,48,128]{2,1,0:T(8,128)S(1)} %get-tuple-element.23.inner_scaling, f32[8,48,128]{2,1,0:T(8,128)S(1)} %get-tuple-element.24.inner_linear, ...), custom_call_target="tpu_custom_call" | custom-call | flops 2000000 | bytes 3000000 | tf_op jit(solution)/shard_map/settle/pallas_call | solution.py:686
  (1 shorter events, 0.0 us)
Async XLA Ops:
  2.9 6.6 %collective-permute-start = (f32[240,128]{1,0:T(8,128)}, f32[240,128]{1,0:T(8,128)S(1)}, u32[]{:S(2)}, u32[]{:S(2)}) collective-permute-start(f32[240,128]{1,0:T(8,128)} %get-tuple-element.20), channel_id=1, source_target_pairs={{0,4},{4,0},{8,12},{12,8},{16,20},{20,16},{24,28},{28,24},{1,5},{5... | collective-permute-start | bytes 368648 | tf_op jit(solution)/shard_map/ppermute | solution.py:639
  5.9 3.5 %copy-start = (f32[19,6,8,128]{3,2,1,0:T(8,128)S(1)}, f32[19,6,8,128]{3,2,1,0:T(8,128)}, u32[]{:S(2)}) copy-start(f32[19,6,8,128]{3,2,1,0:T(8,128)} %param.6) | copy-start | bytes 1400836
  5.9 3.5 %copy-start.1 = (f32[6,8,128]{2,1,0:T(8,128)S(1)}, f32[6,8,128]{2,1,0:T(8,128)}, u32[]{:S(2)}) copy-start(f32[6,8,128]{2,1,0:T(8,128)} %param.7) | copy-start | bytes 73732
  5.9 3.5 %copy-start.2 = (s32[6,8,128]{2,1,0:T(8,128)S(1)}, s32[6,8,128]{2,1,0:T(8,128)}, u32[]{:S(2)}) copy-start(s32[6,8,128]{2,1,0:T(8,128)} %param.8) | copy-start | bytes 73732
  5.9 3.5 %copy-start.3 = (s32[6,8,128]{2,1,0:T(8,128)S(1)}, s32[6,8,128]{2,1,0:T(8,128)}, u32[]{:S(2)}) copy-start(s32[6,8,128]{2,1,0:T(8,128)} %param.9) | copy-start | bytes 73732
  5.9 3.6 %copy-start.4 = (s32[6,8,128]{2,1,0:T(8,128)S(1)}, s32[6,8,128]{2,1,0:T(8,128)}, u32[]{:S(2)}) copy-start(s32[6,8,128]{2,1,0:T(8,128)} %param.10) | copy-start | bytes 73732
  5.9 3.5 %collective-permute-start.1 = (f32[240,128]{1,0:T(8,128)}, f32[240,128]{1,0:T(8,128)S(1)}, u32[]{:S(2)}, u32[]{:S(2)}) collective-permute-start(f32[240,128]{1,0:T(8,128)} %get-tuple-element.21), channel_id=1, source_target_pairs={{4,8},{8,4},{12,16},{16,12},{20,24},{24,20},{5,9},{9,5},{13,17},{1... | collective-permute-start | bytes 368648 | tf_op jit(solution)/shard_map/ppermute | solution.py:639
  9.6 13.3 %collective-permute-start.2 = (f32[264,128]{1,0:T(8,128)S(1)}, f32[264,128]{1,0:T(8,128)S(1)}, u32[]{:S(2)}, u32[]{:S(2)}) collective-permute-start(f32[264,128]{1,0:T(8,128)S(1)} %get-tuple-element.26), channel_id=1, source_target_pairs={{0,1},{1,0},{2,3},{3,2},{4,5},{5,4},{6,7},{7,6},{8,9},{9,8},{10,11... | collective-permute-start | bytes 405512 | tf_op jit(solution)/shard_map/ppermute | solution.py:639
  9.7 13.2 %collective-permute-start.3 = (f32[264,128]{1,0:T(8,128)S(1)}, f32[264,128]{1,0:T(8,128)S(1)}, u32[]{:S(2)}, u32[]{:S(2)}) collective-permute-start(f32[264,128]{1,0:T(8,128)S(1)} %get-tuple-element.27), channel_id=1, source_target_pairs={{1,2},{2,1},{5,6},{6,5},{9,10},{10,9},{13,14},{14,13},{17,18},{18,... | collective-permute-start | bytes 405512 | tf_op jit(solution)/shard_map/ppermute | solution.py:639
  10.4 18.4 %all-to-all-start = ((f32[32,1,128]{2,1,0:T(1,128)}), f32[32,1,128]{2,1,0:T(1,128)S(1)}, u32[]{:S(2)}, u32[]{:S(2)}) async-start(f32[32,1,128]{2,1,0:T(1,128)} %bitcast.8), calls=%async_computation | async-start | bytes 32768 | tf_op jit(solution)/shard_map/all_to_all | solution.py:644
  21.6 0.7 %copy-start.5 = (f32[96]{0:T(128)S(1)}, f32[96]{0:T(128)}, u32[]{:S(2)}) copy-start(f32[96]{0:T(128)} %param.11) | copy-start | bytes 1156
